TPU v7x, 32 devices: a whole 2x2x4 slice. The times are simulated.
32 devices in a mesh: dp: 8 (over y, x, core), mp: 4 (over z).
Axes of the slice: x: 2, y: 2, z: 4, core: 2. Of those that a mesh axis runs over, the one named last changes fastest.
Arguments:
- hidden_in: bfloat16 [4096, 2048], P('dp'), may hold values from -6 to 6
- cotangent: bfloat16 [4096, 2048], P('dp'), may hold values from -6 to 6
- segments: int32 [8, 512], P('dp'), may hold values from 0 to 5, never falling along the last dimension, each value on 1 to 256 neighbouring positions
- live_counts: int32 [8], P('dp'), may hold values from 128 to 512, as said below
- w_query: bfloat16 [2048, 2048], P('dp', 'mp'), may hold values from -0.125 to 0.125
- w_key: bfloat16 [2048, 2048], P('dp', 'mp'), may hold values from -0.125 to 0.125
- w_value: bfloat16 [2048, 2048], P('dp', 'mp'), may hold values from -0.125 to 0.125
- w_output: bfloat16 [2048, 2048], P('mp', 'dp'), may hold values from -0.125 to 0.125
- w_gate: bfloat16 [2048, 8192], P('dp', 'mp'), may hold values from -0.125 to 0.125
- w_up: bfloat16 [2048, 8192], P('dp', 'mp'), may hold values from -0.125 to 0.125
- w_down: bfloat16 [8192, 2048], P('mp', 'dp'), may hold values from -0.0625 to 0.0625
- query_gain: float32 [2048], P('mp'), may hold values from 0.5 to 1.5
- key_gain: float32 [2048], P('mp'), may hold values from 0.5 to 1.5
- attn_gain: float32 [2048], replicated, may hold values from 0.5 to 1.5
- ffn_gain: float32 [2048], replicated, may hold values from 0.5 to 1.5
Outputs:
- hidden_out: bfloat16 [4096, 2048], P('dp')
- grad_in: float32 [4096, 2048], P('dp')
- grad_query: float32 [2048, 2048], P('dp', 'mp')
- grad_key: float32 [2048, 2048], P('dp', 'mp')
- grad_value: float32 [2048, 2048], P('dp', 'mp')
- grad_output_w: float32 [2048, 2048], P('mp', 'dp')
- grad_gate: float32 [2048, 8192], P('dp', 'mp')
- grad_up: float32 [2048, 8192], P('dp', 'mp')
- grad_down: float32 [8192, 2048], P('mp', 'dp')
- grad_query_gain: float32 [2048], P('mp')
- grad_key_gain: float32 [2048], P('mp')
- grad_attn_gain: float32 [2048], replicated
- grad_ffn_gain: float32 [2048], replicated
Inputs may be any that keep to these rules, and one draw needn't show every extreme that they name: Within the rows of one index of dp, segments never fall; each of the 6 documents has 1 to 256 rows and one has exactly 256. `live_counts`: rows of a block at or after its live count are padding; some index of dp has 512 live rows and some has 128.
All inputs are finite; a program needn't handle non-finite values.
Results may differ from a plain program's by a relative error of at most 0.017.
Values may be sent and summed in bfloat16 or wider, within the bound.
A program may use at most 256 MiB of HBM per device.

v0:
```python
import math

import jax
import jax.numpy as jnp
from jax import lax
from jax.sharding import PartitionSpec as P

HD = 128


EPS = 1e-06
THETA = 500000.0


def doc_positions(seg_row):
    row_count = seg_row.shape[0]
    row_index = jnp.arange(row_count, dtype=jnp.int32)
    change = jnp.concatenate([jnp.ones((1,), dtype=bool), seg_row[1:] != seg_row[:-1]])
    doc_start = lax.cummax(jnp.where(change, row_index, jnp.zeros_like(row_index)), axis=0)
    return (row_index - doc_start).astype(jnp.float32)


def rotary_tables(positions, head_size):
    half_size = head_size // 2
    inv_freq = THETA ** (-(jnp.arange(half_size, dtype=jnp.float32) * (2.0 / head_size)))
    angles = positions[:, None] * inv_freq[None, :]
    return (jnp.cos(angles)[:, None, :], jnp.sin(angles)[:, None, :])


def rotate(values, cos_tab, sin_tab):
    half_size = values.shape[2] // 2
    first_half = values[:, :, :half_size]
    second_half = values[:, :, half_size:]
    return jnp.concatenate(
        [
            first_half * cos_tab - second_half * sin_tab,
            second_half * cos_tab + first_half * sin_tab,
        ],
        axis=2,
    )


def rotate_back(grads, cos_tab, sin_tab):
    half_size = grads.shape[2] // 2
    first_half = grads[:, :, :half_size]
    second_half = grads[:, :, half_size:]
    return jnp.concatenate(
        [
            first_half * cos_tab + second_half * sin_tab,
            second_half * cos_tab - first_half * sin_tab,
        ],
        axis=2,
    )


def block_mask(seg_row, offset, block_rows):
    row_index = jnp.arange(seg_row.shape[0])
    same = seg_row[offset : offset + block_rows, None] == seg_row[None, :]
    return same & (row_index[:, None] >= row_index[None, :])


def block_scores(q_blk, k_bf, allowed, score_scale):
    scores = (
        jnp.einsum("qhe,khe->hqk", q_blk, k_bf, preferred_element_type=jnp.float32) * score_scale
    )
    return jnp.where(allowed[None], scores, jnp.float32(-1e30))


def attend_forward(q_bf, k_bf, v_bf, seg_row, score_scale):
    row_count = q_bf.shape[0]
    block_rows = min(512, row_count)
    allowed = block_mask(seg_row, 0, block_rows)
    scores = block_scores(q_bf, k_bf, allowed, score_scale)
    row_max = jnp.max(scores, axis=2, keepdims=True)
    lse = row_max + jnp.log(jnp.sum(jnp.exp(scores - row_max), axis=2, keepdims=True))
    probs = jnp.exp(scores - lse).astype(jnp.bfloat16)
    outputs = jnp.einsum("hqk,khe->qhe", probs, v_bf, preferred_element_type=jnp.float32)
    lse_parts = [lse]
    return (outputs.astype(jnp.bfloat16), lse_parts)


def attend_backward(q_bf, k_bf, v_bf, o_bf, do_bf, lse_parts, seg_row, score_scale):
    row_count = q_bf.shape[0]
    block_rows = min(512, row_count)
    dq_parts = []
    dk_acc = jnp.zeros(k_bf.shape, jnp.float32)
    dv_acc = jnp.zeros(v_bf.shape, jnp.float32)
    for part_index, offset in enumerate(range(0, row_count, block_rows)):
        allowed = block_mask(seg_row, offset, block_rows)
        scores = block_scores(q_bf, k_bf, allowed, score_scale)
        probs = jnp.exp(scores - lse_parts[part_index])
        probs_bf = probs.astype(jnp.bfloat16)
        dprob = jnp.einsum("qhe,khe->hqk", do_bf, v_bf, preferred_element_type=jnp.float32)
        delta = jnp.transpose(
            jnp.sum(do_bf.astype(jnp.float32) * o_bf.astype(jnp.float32), axis=2)
        )[:, :, None]
        dscore = (probs * (dprob - delta)).astype(jnp.bfloat16)
        dq_parts.append(
            jnp.einsum("hqk,khe->qhe", dscore, k_bf, preferred_element_type=jnp.float32)
            * score_scale
        )
        dk_acc = (
            jnp.einsum("hqk,qhe->khe", dscore, q_bf, preferred_element_type=jnp.float32)
            * score_scale
        )
        dv_acc = jnp.einsum("hqk,qhe->khe", probs_bf, do_bf, preferred_element_type=jnp.float32)
    return (dq_parts[0], dk_acc, dv_acc.astype(jnp.bfloat16))


def norm_back(raw, inv_scale, gained, row_sums, width):
    return inv_scale * gained - raw * inv_scale**3 * (row_sums[:, None] / width)


def on_device(
    hidden_in,
    cotangent,
    segments,
    live_counts,
    w_query,
    w_key,
    w_value,
    w_output,
    w_gate,
    w_up,
    w_down,
    query_gain,
    key_gain,
    attn_gain,
    ffn_gain,
):
    gathered = (
        lax.all_gather(w_query, "dp", axis=0, tiled=True),
        lax.all_gather(w_key, "dp", axis=0, tiled=True),
        lax.all_gather(w_value, "dp", axis=0, tiled=True),
        lax.all_gather(w_output, "dp", axis=1, tiled=True),
        lax.all_gather(w_gate, "dp", axis=0, tiled=True),
        lax.all_gather(w_up, "dp", axis=0, tiled=True),
        lax.all_gather(w_down, "dp", axis=1, tiled=True),
    )
    wq_full, wk_full, wv_full, wo_full, wg_full, wu_full, wd_full = gathered
    seg_row = segments[0]
    live_n = live_counts[0]
    row_count, width = hidden_in.shape
    local_width = wq_full.shape[1]
    heads_here = local_width // HD
    score_scale = 1.0 / math.sqrt(HD)
    live_mask = (jnp.arange(row_count, dtype=jnp.int32) < live_n).astype(jnp.float32)[:, None]
    cos_tab, sin_tab = rotary_tables(doc_positions(seg_row), HD)
    q_proj = jnp.dot(hidden_in, wq_full, preferred_element_type=jnp.float32)
    k_proj = jnp.dot(hidden_in, wk_full, preferred_element_type=jnp.float32)
    v_bf = jnp.dot(hidden_in, wv_full, preferred_element_type=jnp.float32).astype(jnp.bfloat16)
    sq_query, sq_key = lax.psum(
        (jnp.sum(q_proj * q_proj, axis=1), jnp.sum(k_proj * k_proj, axis=1)), "mp"
    )
    inv_q = lax.rsqrt(sq_query[:, None] / width + EPS)
    inv_k = lax.rsqrt(sq_key[:, None] / width + EPS)
    q_rot = rotate(
        (q_proj * inv_q * query_gain).reshape(row_count, heads_here, HD), cos_tab, sin_tab
    ).astype(jnp.bfloat16)
    k_rot = rotate(
        (k_proj * inv_k * key_gain).reshape(row_count, heads_here, HD), cos_tab, sin_tab
    ).astype(jnp.bfloat16)
    v_heads = v_bf.reshape(row_count, heads_here, HD)
    o_bf, lse_parts = attend_forward(q_rot, k_rot, v_heads, seg_row, score_scale)
    o_flat = o_bf.reshape(row_count, local_width)
    attn_raw = lax.psum(jnp.dot(o_flat, wo_full, preferred_element_type=jnp.float32), "mp")
    inv_a = lax.rsqrt(jnp.mean(attn_raw * attn_raw, axis=1, keepdims=True) + EPS)
    h_mid = hidden_in.astype(jnp.float32) + attn_raw * inv_a * attn_gain
    h_bf = h_mid.astype(jnp.bfloat16)
    gate_pre = jnp.dot(h_bf, wg_full, preferred_element_type=jnp.float32)
    up_pre = jnp.dot(h_bf, wu_full, preferred_element_type=jnp.float32)
    act_bf = (jax.nn.silu(gate_pre) * up_pre).astype(jnp.bfloat16)
    ffn_raw = lax.psum(jnp.dot(act_bf, wd_full, preferred_element_type=jnp.float32), "mp")
    inv_f = lax.rsqrt(jnp.mean(ffn_raw * ffn_raw, axis=1, keepdims=True) + EPS)
    hidden_out = (live_mask * (h_mid + ffn_raw * inv_f * ffn_gain)).astype(jnp.bfloat16)
    back_weights = (
        lax.all_gather(w_query, "dp", axis=0, tiled=True),
        lax.all_gather(w_key, "dp", axis=0, tiled=True),
        lax.all_gather(w_value, "dp", axis=0, tiled=True),
        lax.all_gather(w_output, "dp", axis=1, tiled=True),
        lax.all_gather(w_gate, "dp", axis=0, tiled=True),
        lax.all_gather(w_up, "dp", axis=0, tiled=True),
        lax.all_gather(w_down, "dp", axis=1, tiled=True),
    )
    wq_back, wk_back, wv_back, wo_back, wg_back, wu_back, wd_back = back_weights
    dy = live_mask * cotangent.astype(jnp.float32)
    g_ffn_gain = jnp.sum(dy * ffn_raw * inv_f, axis=0)
    gained_f = ffn_gain * dy
    d_ffn = norm_back(ffn_raw, inv_f, gained_f, jnp.sum(gained_f * ffn_raw, axis=1), width).astype(
        jnp.bfloat16
    )
    d_act = jnp.dot(d_ffn, wd_back.T, preferred_element_type=jnp.float32)
    sig = jax.nn.sigmoid(gate_pre)
    d_up = (d_act * gate_pre * sig).astype(jnp.bfloat16)
    d_gate = (d_act * up_pre * sig * (1.0 + gate_pre * (1.0 - sig))).astype(jnp.bfloat16)
    ffn_part = jnp.dot(d_gate, wg_back.T, preferred_element_type=jnp.float32) + jnp.dot(
        d_up, wu_back.T, preferred_element_type=jnp.float32
    )
    dh = dy + lax.psum(ffn_part, "mp")
    g_down = jnp.dot(act_bf.T, d_ffn, preferred_element_type=jnp.float32)
    g_gate = jnp.dot(h_bf.T, d_gate, preferred_element_type=jnp.float32)
    g_up = jnp.dot(h_bf.T, d_up, preferred_element_type=jnp.float32)
    g_attn_gain = jnp.sum(dh * attn_raw * inv_a, axis=0)
    gained_a = attn_gain * dh
    d_attn = norm_back(
        attn_raw, inv_a, gained_a, jnp.sum(gained_a * attn_raw, axis=1), width
    ).astype(jnp.bfloat16)
    d_heads = jnp.dot(d_attn, wo_back.T, preferred_element_type=jnp.float32).astype(jnp.bfloat16)
    g_output = jnp.dot(o_flat.T, d_attn, preferred_element_type=jnp.float32)
    dq_rot, dk_rot, d_val = attend_backward(
        q_rot,
        k_rot,
        v_heads,
        o_bf,
        d_heads.reshape(row_count, heads_here, HD),
        lse_parts,
        seg_row,
        score_scale,
    )
    dq_norm = rotate_back(dq_rot, cos_tab, sin_tab).reshape(row_count, local_width)
    dk_norm = rotate_back(dk_rot, cos_tab, sin_tab).reshape(row_count, local_width)
    g_query_gain = jnp.sum(dq_norm * q_proj * inv_q, axis=0)
    g_key_gain = jnp.sum(dk_norm * k_proj * inv_k, axis=0)
    gained_q = query_gain * dq_norm
    gained_k = key_gain * dk_norm
    sums_query, sums_key = lax.psum(
        (jnp.sum(gained_q * q_proj, axis=1), jnp.sum(gained_k * k_proj, axis=1)), "mp"
    )
    dq_bf = norm_back(q_proj, inv_q, gained_q, sums_query, width).astype(jnp.bfloat16)
    dk_bf = norm_back(k_proj, inv_k, gained_k, sums_key, width).astype(jnp.bfloat16)
    dv_bf = d_val.reshape(row_count, local_width)
    input_part = (
        jnp.dot(dq_bf, wq_back.T, preferred_element_type=jnp.float32)
        + jnp.dot(dk_bf, wk_back.T, preferred_element_type=jnp.float32)
        + jnp.dot(dv_bf, wv_back.T, preferred_element_type=jnp.float32)
    )
    grad_in = dh + lax.psum(input_part.astype(jnp.bfloat16), "mp").astype(jnp.float32)
    g_query = jnp.dot(hidden_in.T, dq_bf, preferred_element_type=jnp.float32)
    g_key = jnp.dot(hidden_in.T, dk_bf, preferred_element_type=jnp.float32)
    g_value = jnp.dot(hidden_in.T, dv_bf, preferred_element_type=jnp.float32)
    owned = (
        lax.psum_scatter(g_query, "dp", scatter_dimension=0, tiled=True),
        lax.psum_scatter(g_key, "dp", scatter_dimension=0, tiled=True),
        lax.psum_scatter(g_value, "dp", scatter_dimension=0, tiled=True),
        lax.psum_scatter(g_output, "dp", scatter_dimension=1, tiled=True),
        lax.psum_scatter(g_gate, "dp", scatter_dimension=0, tiled=True),
        lax.psum_scatter(g_up, "dp", scatter_dimension=0, tiled=True),
        lax.psum_scatter(g_down, "dp", scatter_dimension=1, tiled=True),
    )
    gain_totals = lax.psum((g_query_gain, g_key_gain, g_attn_gain, g_ffn_gain), "dp")
    return (
        hidden_out,
        grad_in,
        owned[0],
        owned[1],
        owned[2],
        owned[3],
        owned[4],
        owned[5],
        owned[6],
        gain_totals[0],
        gain_totals[1],
        gain_totals[2],
        gain_totals[3],
    )


def solution(mesh):
    return jax.shard_map(
        on_device,
        mesh=mesh,
        in_specs=(
            P("dp", None),
            P("dp", None),
            P("dp", None),
            P("dp"),
            P("dp", "mp"),
            P("dp", "mp"),
            P("dp", "mp"),
            P("mp", "dp"),
            P("dp", "mp"),
            P("dp", "mp"),
            P("mp", "dp"),
            P("mp"),
            P("mp"),
            P(),
            P(),
        ),
        out_specs=(
            P("dp", None),
            P("dp", None),
            P("dp", "mp"),
            P("dp", "mp"),
            P("dp", "mp"),
            P("mp", "dp"),
            P("dp", "mp"),
            P("dp", "mp"),
            P("mp", "dp"),
            P("mp"),
            P("mp"),
            P(),
            P(),
        ),
        check_vma=False,
    )
```

profile of v0, /device:TPU:0, one launch (start us, length us, event | category | flops | bytes accessed | tf_op | source)
XLA Modules:
  0.0 1542.0 jit_solution(11089845251164984126)
XLA Ops:
  14.4 26.0 %all-gather.12.cloned.1.call-done = bf16[2048,512]{1,0:T(8,128)(2,1)} async-done(((bf16[256,512]{1,0:T(8,128)(2,1)}), bf16[2048,512]{1,0:T(8,128)(2,1)}) %all-gather.12.cloned.1.call-update) | async-done | bytes 2097168 | tf_op jit(solution)/shard_map/all_gather | solution.py:133
  44.0 26.1 %all-gather.10.cloned.1.call-done = bf16[2048,512]{1,0:T(8,128)(2,1)} async-done(((bf16[256,512]{1,0:T(8,128)(2,1)}), bf16[2048,512]{1,0:T(8,128)(2,1)}) %all-gather.10.cloned.1.call-update) | async-done | bytes 2097168 | tf_op jit(solution)/shard_map/all_gather | solution.py:132
  74.0 11.8 all-reduce.2
  112.2 17.5 %all-gather.14.cloned.1.call-done = bf16[512,2048]{1,0:T(8,128)(2,1)} async-done(((bf16[512,256]{1,0:T(8,128)(2,1)}), bf16[512,2048]{1,0:T(8,128)(2,1)}) %all-gather.14.cloned.1.call-update) | async-done | bytes 2097168 | tf_op jit(solution)/shard_map/all_gather | solution.py:135
  129.7 5.0 fusion.24
  137.1 152.8 %all-reduce.8.cloned.1.call-done = f32[512,2048]{1,0:T(8,128)} async-done(((f32[512,2048]{1,0:T(8,128)}), f32[512,2048]{1,0:T(8,128)}) %all-reduce.8.cloned.1.call-update) | async-done | bytes 4194320 | tf_op jit(solution)/shard_map/psum | solution.py:166
  295.4 49.5 %all-gather.16.cloned.1.call-done = bf16[2048,2048]{1,0:T(8,128)(2,1)} async-done(((bf16[256,2048]{1,0:T(8,128)(2,1)}), bf16[2048,2048]{1,0:T(8,128)(2,1)}) %all-gather.16.cloned.1.call-update) | async-done | bytes 8388624 | tf_op jit(solution)/shard_map/all_gather | solution.py:136
  344.9 10.6 fusion.25
  355.4 45.6 %all-gather.18.cloned.1.call-done = bf16[2048,2048]{1,0:T(8,128)(2,1)} async-done(((bf16[256,2048]{1,0:T(8,128)(2,1)}), bf16[2048,2048]{1,0:T(8,128)(2,1)}) %all-gather.18.cloned.1.call-update) | async-done | bytes 8388624 | tf_op jit(solution)/shard_map/all_gather | solution.py:137
  401.0 12.5 multiply_convert_fusion.4
  413.5 45.3 %all-gather.20.cloned.1.call-done = bf16[2048,2048]{1,0:T(8,128)(2,1)} async-done(((bf16[2048,256]{1,0:T(8,128)(2,1)}), bf16[2048,2048]{1,0:T(8,128)(2,1)}) %all-gather.20.cloned.1.call-update) | async-done | bytes 8388624 | tf_op jit(solution)/shard_map/all_gather | solution.py:138
  458.8 10.5 fusion.26
  470.4 154.0 %all-reduce.10.cloned.1.call-done = f32[512,2048]{1,0:T(8,128)} async-done(((f32[512,2048]{1,0:T(8,128)}), f32[512,2048]{1,0:T(8,128)}) %all-reduce.10.cloned.1.call-update) | async-done | bytes 4194320 | tf_op jit(solution)/shard_map/psum | solution.py:173
  630.8 14.1 multiply_convert_fusion.1
  644.9 7.8 fusion.27
  652.7 9.6 convolution_add_fusion
  662.5 153.9 %all-reduce.12.cloned.1.call-done = f32[512,2048]{1,0:T(8,128)} async-done(((f32[512,2048]{1,0:T(8,128)}), f32[512,2048]{1,0:T(8,128)}) %all-reduce.12.cloned.1.call-update) | async-done | bytes 4194320 | tf_op jit(solution)/shard_map/psum | solution.py:199
  823.5 5.5 subtract_convert_fusion
  852.9 9.6 all-reduce.1
  887.7 13.6 fusion.20
  901.4 12.5 fusion.32
  914.2 12.5 fusion.31
  926.8 24.9 %all-reduce = (f32[512]{0:T(512)}, f32[512]{0:T(512)}, f32[2048]{0:T(1024)}, f32[2048]{0:T(1024)}) all-reduce(f32[512]{0:T(512)S(1)} %get-tuple-element.45, f32[512]{0:T(512)S(1)} %get-tuple-element.43, f32[2048]{0:T(1024)S(1)} %get-tuple-element.39, f32[2048]{0:T(1024)S(1)} %get-tuple-element.41), channel_id=1, replica_groups=mesh['dp'=8,'mp'=4] {'dp'}, use_global_device_ids=true, to_apply=%region_29.30 | all-reduce | flops 5120 | bytes 40960 | tf_op jit(solution)/shard_map/psum | solution.py:250
  951.6 5.6 all-reduce.14.cloned.1.call-done
  957.2 6.1 convert_add_fusion
  963.3 47.3 %reduce-scatter.12.cloned.1.call-done = f32[256,512]{0,1:T(8,128)} async-done(((f32[2048,512]{0,1:T(8,128)}), f32[256,512]{0,1:T(8,128)}) %reduce-scatter.12.cloned.1.call-update) | async-done | bytes 524304 | tf_op jit(solution)/shard_map/reduce_scatter | solution.py:244
  1012.6 52.4 %reduce-scatter.8.cloned.1.call-done = f32[256,512]{0,1:T(8,128)} async-done(((f32[2048,512]{0,1:T(8,128)}), f32[256,512]{0,1:T(8,128)}) %reduce-scatter.8.cloned.1.call-update) | async-done | bytes 524304 | tf_op jit(solution)/shard_map/reduce_scatter | solution.py:242
  1067.1 52.3 %reduce-scatter.10.cloned.1.call-done = f32[256,512]{0,1:T(8,128)} async-done(((f32[2048,512]{0,1:T(8,128)}), f32[256,512]{0,1:T(8,128)}) %reduce-scatter.10.cloned.1.call-update) | async-done | bytes 524304 | tf_op jit(solution)/shard_map/reduce_scatter | solution.py:243
  1121.4 52.9 %reduce-scatter.14.cloned.1.call-done = f32[512,256]{1,0:T(8,128)} async-done(((f32[512,2048]{1,0:T(8,128)}), f32[512,256]{1,0:T(8,128)}) %reduce-scatter.14.cloned.1.call-update) | async-done | bytes 524304 | tf_op jit(solution)/shard_map/reduce_scatter | solution.py:245
  1174.2 120.0 %reduce-scatter.20.cloned.1.call-done = f32[2048,256]{1,0:T(8,128)} async-done(((f32[2048,2048]{1,0:T(8,128)}), f32[2048,256]{1,0:T(8,128)}) %reduce-scatter.20.cloned.1.call-update) | async-done | bytes 2097168 | tf_op jit(solution)/shard_map/reduce_scatter | solution.py:248
  1294.3 120.2 %reduce-scatter.18.cloned.1.call-done = f32[256,2048]{1,0:T(8,128)} async-done(((f32[2048,2048]{1,0:T(8,128)}), f32[256,2048]{1,0:T(8,128)}) %reduce-scatter.18.cloned.1.call-update) | async-done | bytes 2097168 | tf_op jit(solution)/shard_map/reduce_scatter | solution.py:247
  1414.5 120.2 %reduce-scatter.16.cloned.1.call-done = f32[256,2048]{1,0:T(8,128)} async-done(((f32[2048,2048]{1,0:T(8,128)}), f32[256,2048]{1,0:T(8,128)}) %reduce-scatter.16.cloned.1.call-update) | async-done | bytes 2097168 | tf_op jit(solution)/shard_map/reduce_scatter | solution.py:246
  (178 shorter events, 118.0 us)
Async XLA Ops:
  7.2 33.2 %all-gather.12.cloned.1.call-start = ((), (), s32[]{:S(2)}) async-start(), calls=%async_computation.9 | async-start | bytes 2359296 | tf_op jit(solution)/shard_map/all_gather | solution.py:133
  7.9 62.2 %all-gather.10.cloned.1.call-start = ((), (), s32[]{:S(2)}) async-start(), calls=%async_computation.8 | async-start | bytes 2359296 | tf_op jit(solution)/shard_map/all_gather | solution.py:132
  8.7 97.5 %all-gather.8.cloned.1.call-start = ((), (), s32[]{:S(2)}) async-start(), calls=%async_computation.7 | async-start | bytes 2359296 | tf_op jit(solution)/shard_map/all_gather | solution.py:134
  9.4 120.3 %all-gather.14.cloned.1.call-start = ((), (), s32[]{:S(2)}) async-start(), calls=%async_computation.10 | async-start | bytes 2359296 | tf_op jit(solution)/shard_map/all_gather | solution.py:135
  10.0 279.9 %all-reduce.8.cloned.1.call-start = ((), (), s32[]{:S(2)}) async-start(), calls=%async_computation.11 | async-start | bytes 8388608 | tf_op jit(solution)/shard_map/psum | solution.py:166
  14.4 55.7 %copy-start.2 = (bf16[512,2048]{1,0:T(8,128)(2,1)S(1)}, bf16[512,2048]{1,0:T(8,128)(2,1)}, u32[]{:S(2)}) copy-start(bf16[512,2048]{1,0:T(8,128)(2,1)} %param.15) | copy-start | bytes 6291460
  43.9 41.8 %copy-start.35 = (f32[512]{0:T(512)S(1)}, f32[512]{0:T(512)}, u32[]{:S(2)}) copy-start(f32[512]{0:T(512)} %param.27) | copy-start | bytes 6148
  74.0 17.7 %copy-start.34 = (f32[512]{0:T(512)S(1)}, f32[512]{0:T(512)}, u32[]{:S(2)}) copy-start(f32[512]{0:T(512)} %param.26) | copy-start | bytes 6148
  101.7 4.4 copy-start.15
  134.7 157.8 %copy-start.32 = (f32[2048]{0:T(1024)S(1)}, f32[2048]{0:T(1024)}, u32[]{:S(2)}) copy-start(f32[2048]{0:T(1024)} %param.28) | copy-start | bytes 24580
  134.7 210.1 %all-gather.16.cloned.1.call-start = ((), (), s32[]{:S(2)}) async-start(), calls=%async_computation.12 | async-start | bytes 9437184 | tf_op jit(solution)/shard_map/all_gather | solution.py:136
  135.3 265.7 %all-gather.18.cloned.1.call-start = ((), (), s32[]{:S(2)}) async-start(), calls=%async_computation.13 | async-start | bytes 9437184 | tf_op jit(solution)/shard_map/all_gather | solution.py:137
  136.1 322.7 %all-gather.20.cloned.1.call-start = ((), (), s32[]{:S(2)}) async-start(), calls=%async_computation.14 | async-start | bytes 9437184 | tf_op jit(solution)/shard_map/all_gather | solution.py:138
  136.8 487.6 %all-reduce.10.cloned.1.call-start = ((), (), s32[]{:S(2)}) async-start(), calls=%async_computation.15 | async-start | bytes 8388608 | tf_op jit(solution)/shard_map/psum | solution.py:173
  469.3 157.9 %copy-start.33 = (f32[2048]{0:T(1024)S(1)}, f32[2048]{0:T(1024)}, u32[]{:S(2)}) copy-start(f32[2048]{0:T(1024)} %param.29) | copy-start | bytes 24580
  469.3 347.1 %all-reduce.12.cloned.1.call-start = ((), (), s32[]{:S(2)}) async-start(), calls=%async_computation.16 | async-start | bytes 8388608 | tf_op jit(solution)/shard_map/psum | solution.py:199
  644.9 7.8 copy-start.38
  662.3 294.9 %all-reduce.14.cloned.1.call-start = ((), (), s32[]{:S(2)}) async-start(), calls=%async_computation.17 | async-start | bytes 4194304 | tf_op jit(solution)/shard_map/psum | solution.py:237
  816.4 5.2 copy-start.1
  816.4 6.5 copy-start.4
  816.4 7.1 copy-start.5
  823.5 5.5 copy-start.26
  823.5 5.5 copy-start.30
  829.0 5.1 copy-start.10
  872.4 138.1 %reduce-scatter.12.cloned.1.call-start = ((), (), s32[]{:S(2)}) async-start(), calls=%async_computation.20 | async-start | bytes 4718592 | tf_op jit(solution)/shard_map/reduce_scatter | solution.py:244
  875.7 189.3 %reduce-scatter.8.cloned.1.call-start = ((), (), s32[]{:S(2)}) async-start(), calls=%async_computation.18 | async-start | bytes 4718592 | tf_op jit(solution)/shard_map/reduce_scatter | solution.py:242
  879.0 240.3 %reduce-scatter.10.cloned.1.call-start = ((), (), s32[]{:S(2)}) async-start(), calls=%async_computation.19 | async-start | bytes 4718592 | tf_op jit(solution)/shard_map/reduce_scatter | solution.py:243
  882.3 5.4 copy-start.6
  882.3 291.9 %reduce-scatter.14.cloned.1.call-start = ((), (), s32[]{:S(2)}) async-start(), calls=%async_computation.21 | async-start | bytes 4718592 | tf_op jit(solution)/shard_map/reduce_scatter | solution.py:245
  887.4 406.9 %reduce-scatter.20.cloned.1.call-start = ((), (), s32[]{:S(2)}) async-start(), calls=%async_computation.24 | async-start | bytes 18874368 | tf_op jit(solution)/shard_map/reduce_scatter | solution.py:248
  901.3 513.2 %reduce-scatter.18.cloned.1.call-start = ((), (), s32[]{:S(2)}) async-start(), calls=%async_computation.23 | async-start | bytes 18874368 | tf_op jit(solution)/shard_map/reduce_scatter | solution.py:247
  913.9 620.8 %reduce-scatter.16.cloned.1.call-start = ((), (), s32[]{:S(2)}) async-start(), calls=%async_computation.22 | async-start | bytes 18874368 | tf_op jit(solution)/shard_map/reduce_scatter | solution.py:246
  (25 other events, 66.5 us)
Sparse Core Ops, SparseCore 0:
  9.9 30.4 all-gather.11
  42.3 27.7 all-gather.9
  72.0 27.7 all-gather.7
  101.5 28.0 all-gather.13
  134.8 154.9 all-reduce.7
  291.6 53.2 all-gather.15
  346.7 54.2 all-gather.17
  402.9 55.8 all-gather.19
  469.4 154.9 all-reduce.9
  662.4 153.9 all-reduce.11
  872.5 84.6 all-reduce.13
  960.4 50.0 reduce-scatter.11
  1013.9 51.0 reduce-scatter.7
  1068.2 51.0 reduce-scatter.9
  1123.1 51.0 reduce-scatter.13
  1178.2 115.9 reduce-scatter.19
  1298.3 116.1 reduce-scatter.17
  1418.5 116.1 reduce-scatter.15
where the time goes:
time: 1550 us; the launch traced here: 1540 us
  waiting for transfers between devices  1250 us (81%)
  matrix products  149 us (10%)
  other arithmetic  49.8 us (3%)
  blocking collectives  46.3 us (3%)
  local copies, waits for them, and re-layouts  32.1 us (2%)
  between operations  16 us (1%)
    psum x1, waiting for transfers between devices, on_device(): lax.psum(jnp.dot(act_bf, wd_full, preferred_element_type=jnp.float32), 'mp')  154 us
    psum x1, waiting for transfers between devices, on_device(): dh = dy + lax.psum(ffn_part, 'mp')  154 us
    psum x1, waiting for transfers between devices, on_device(): lax.psum(jnp.dot(o_flat, wo_full, preferred_element_type=jnp.float32), 'mp')  153 us
    reduce_scatter x1, waiting for transfers between devices, on_device(): lax.psum_scatter(g_gate, 'dp', scatter_dimension=0, tiled=True)  120 us
    reduce_scatter x1, waiting for transfers between devices, on_device(): lax.psum_scatter(g_up, 'dp', scatter_dimension=0, tiled=True)  120 us
    reduce_scatter x1, waiting for transfers between devices, on_device(): lax.psum_scatter(g_down, 'dp', scatter_dimension=1, tiled=True)  120 us
    reduce_scatter x1, waiting for transfers between devices, on_device(): lax.psum_scatter(g_output, 'dp', scatter_dimension=1, tiled=True)  52.9 us
    reduce_scatter x1, waiting for transfers between devices, on_device(): lax.psum_scatter(g_query, 'dp', scatter_dimension=0, tiled=True)  52.4 us
  transfers between devices with their start and end apart: 18, of which 17 were waited for; matrix products, arithmetic and copies ran while one was open for 8% of the time, Pallas kernels for 0%

commit v1 on v0

--- a/solution.py
+++ b/solution.py
@@ -107,6 +107,20 @@
     return (dq_parts[0], dk_acc, dv_acc.astype(jnp.bfloat16))
 
 
+def scatter_grad(grad, axis_name, scatter_dimension, tiled):
+    total = lax.psum_scatter(
+        grad.astype(jnp.bfloat16), axis_name, scatter_dimension=scatter_dimension, tiled=tiled
+    )
+    return total.astype(jnp.float32)
+
+
+def sum_parts(part, axis_name):
+    own = lax.psum_scatter(
+        part.astype(jnp.bfloat16), axis_name, scatter_dimension=0, tiled=True
+    )
+    return lax.all_gather(own, axis_name, axis=0, tiled=True).astype(jnp.float32)
+
+
 def norm_back(raw, inv_scale, gained, row_sums, width):
     return inv_scale * gained - raw * inv_scale**3 * (row_sums[:, None] / width)
 
@@ -163,26 +177,17 @@
     v_heads = v_bf.reshape(row_count, heads_here, HD)
     o_bf, lse_parts = attend_forward(q_rot, k_rot, v_heads, seg_row, score_scale)
     o_flat = o_bf.reshape(row_count, local_width)
-    attn_raw = lax.psum(jnp.dot(o_flat, wo_full, preferred_element_type=jnp.float32), "mp")
+    attn_raw = sum_parts(jnp.dot(o_flat, wo_full, preferred_element_type=jnp.float32), "mp")
     inv_a = lax.rsqrt(jnp.mean(attn_raw * attn_raw, axis=1, keepdims=True) + EPS)
     h_mid = hidden_in.astype(jnp.float32) + attn_raw * inv_a * attn_gain
     h_bf = h_mid.astype(jnp.bfloat16)
     gate_pre = jnp.dot(h_bf, wg_full, preferred_element_type=jnp.float32)
     up_pre = jnp.dot(h_bf, wu_full, preferred_element_type=jnp.float32)
     act_bf = (jax.nn.silu(gate_pre) * up_pre).astype(jnp.bfloat16)
-    ffn_raw = lax.psum(jnp.dot(act_bf, wd_full, preferred_element_type=jnp.float32), "mp")
+    ffn_raw = sum_parts(jnp.dot(act_bf, wd_full, preferred_element_type=jnp.float32), "mp")
     inv_f = lax.rsqrt(jnp.mean(ffn_raw * ffn_raw, axis=1, keepdims=True) + EPS)
     hidden_out = (live_mask * (h_mid + ffn_raw * inv_f * ffn_gain)).astype(jnp.bfloat16)
-    back_weights = (
-        lax.all_gather(w_query, "dp", axis=0, tiled=True),
-        lax.all_gather(w_key, "dp", axis=0, tiled=True),
-        lax.all_gather(w_value, "dp", axis=0, tiled=True),
-        lax.all_gather(w_output, "dp", axis=1, tiled=True),
-        lax.all_gather(w_gate, "dp", axis=0, tiled=True),
-        lax.all_gather(w_up, "dp", axis=0, tiled=True),
-        lax.all_gather(w_down, "dp", axis=1, tiled=True),
-    )
-    wq_back, wk_back, wv_back, wo_back, wg_back, wu_back, wd_back = back_weights
+    wq_back, wk_back, wv_back, wo_back, wg_back, wu_back, wd_back = gathered
     dy = live_mask * cotangent.astype(jnp.float32)
     g_ffn_gain = jnp.sum(dy * ffn_raw * inv_f, axis=0)
     gained_f = ffn_gain * dy
@@ -196,7 +201,7 @@
     ffn_part = jnp.dot(d_gate, wg_back.T, preferred_element_type=jnp.float32) + jnp.dot(
         d_up, wu_back.T, preferred_element_type=jnp.float32
     )
-    dh = dy + lax.psum(ffn_part, "mp")
+    dh = dy + sum_parts(ffn_part, "mp")
     g_down = jnp.dot(act_bf.T, d_ffn, preferred_element_type=jnp.float32)
     g_gate = jnp.dot(h_bf.T, d_gate, preferred_element_type=jnp.float32)
     g_up = jnp.dot(h_bf.T, d_up, preferred_element_type=jnp.float32)
@@ -234,18 +239,18 @@
         + jnp.dot(dk_bf, wk_back.T, preferred_element_type=jnp.float32)
         + jnp.dot(dv_bf, wv_back.T, preferred_element_type=jnp.float32)
     )
-    grad_in = dh + lax.psum(input_part.astype(jnp.bfloat16), "mp").astype(jnp.float32)
+    grad_in = dh + sum_parts(input_part, "mp")
     g_query = jnp.dot(hidden_in.T, dq_bf, preferred_element_type=jnp.float32)
     g_key = jnp.dot(hidden_in.T, dk_bf, preferred_element_type=jnp.float32)
     g_value = jnp.dot(hidden_in.T, dv_bf, preferred_element_type=jnp.float32)
     owned = (
-        lax.psum_scatter(g_query, "dp", scatter_dimension=0, tiled=True),
-        lax.psum_scatter(g_key, "dp", scatter_dimension=0, tiled=True),
-        lax.psum_scatter(g_value, "dp", scatter_dimension=0, tiled=True),
-        lax.psum_scatter(g_output, "dp", scatter_dimension=1, tiled=True),
-        lax.psum_scatter(g_gate, "dp", scatter_dimension=0, tiled=True),
-        lax.psum_scatter(g_up, "dp", scatter_dimension=0, tiled=True),
-        lax.psum_scatter(g_down, "dp", scatter_dimension=1, tiled=True),
+        scatter_grad(g_query, "dp", scatter_dimension=0, tiled=True),
+        scatter_grad(g_key, "dp", scatter_dimension=0, tiled=True),
+        scatter_grad(g_value, "dp", scatter_dimension=0, tiled=True),
+        scatter_grad(g_output, "dp", scatter_dimension=1, tiled=True),
+        scatter_grad(g_gate, "dp", scatter_dimension=0, tiled=True),
+        scatter_grad(g_up, "dp", scatter_dimension=0, tiled=True),
+        scatter_grad(g_down, "dp", scatter_dimension=1, tiled=True),
     )
     gain_totals = lax.psum((g_query_gain, g_key_gain, g_attn_gain, g_ffn_gain), "dp")
     return (

time: 1550 us -> 1180 us (0.76)
  waiting for transfers between devices: 1250 us -> 890 us
    psum x4 -> x0, waiting for transfers between devices: 466 us -> none  [the longest x1 154 us: on_device(): lax.psum(jnp.dot(act_bf, wd_full, preferred_element_type=jnp.float32), 'mp')]
    all_gather x0 -> x4, waiting for transfers between devices: none -> 180 us  [sum_parts(): lax.all_gather(own, axis_name, axis=0, tiled=True).astype(jnp.float32)]
    reduce_scatter x7 -> x11, waiting for transfers between devices: 565 us -> 491 us  [the longest x7 361 us: scatter_grad(): lax.psum_scatter(grad.astype(jnp.bfloat16), axis_name, scatter_dimension=...]
  transfers between devices with their start and end apart: 18 -> 22, of which waited for: 17 -> 20; matrix products, arithmetic and copies ran while one was open for 8% -> 10% of each run, Pallas kernels for 0% -> 0%
where the time goes in v1:
time: 1180 us; the launch traced here: 1170 us
  waiting for transfers between devices  890 us (75%)
  matrix products  135 us (11%)
  other arithmetic  53.6 us (5%)
  blocking collectives  44.7 us (4%)
  local copies, waits for them, and re-layouts  25 us (2%)
  between operations  16.1 us (1%)
    reduce_scatter x7, waiting for transfers between devices, scatter_grad(): lax.psum_scatter(grad.astype(jnp.bfloat16), axis_name, scatter_dimension=...  361 us
    all_gather x4, waiting for transfers between devices, sum_parts(): lax.all_gather(own, axis_name, axis=0, tiled=True).astype(jnp.float32)  180 us
    reduce_scatter x4, waiting for transfers between devices, sum_parts(): lax.psum_scatter(part.astype(jnp.bfloat16), axis_name, scatter_dimension=...  130 us
    all_gather x1, waiting for transfers between devices, on_device(): lax.all_gather(w_gate, 'dp', axis=0, tiled=True)  48.9 us
    all_gather x1, waiting for transfers between devices, on_device(): lax.all_gather(w_down, 'dp', axis=1, tiled=True)  47 us
    all_gather x1, waiting for transfers between devices, on_device(): lax.all_gather(w_up, 'dp', axis=0, tiled=True)  45.7 us
    all_gather x1, waiting for transfers between devices, on_device(): lax.all_gather(w_query, 'dp', axis=0, tiled=True)  26.1 us
    all_gather x1, waiting for transfers between devices, on_device(): lax.all_gather(w_key, 'dp', axis=0, tiled=True)  26 us
  transfers between devices with their start and end apart: 22, of which 20 were waited for; matrix products, arithmetic and copies ran while one was open for 10% of the time, Pallas kernels for 0%

profile of v1, /device:TPU:0, one launch (start us, length us, event | category | flops | bytes accessed | tf_op | source)
XLA Modules:
  0.0 1167.1 jit_solution(17144449254800355425)
XLA Ops:
  14.4 26.0 %all-gather.16.cloned.1.call-done = bf16[2048,512]{1,0:T(8,128)(2,1)} async-done(((bf16[256,512]{1,0:T(8,128)(2,1)}), bf16[2048,512]{1,0:T(8,128)(2,1)}) %all-gather.16.cloned.1.call-update) | async-done | bytes 2097168 | tf_op jit(solution)/shard_map/all_gather | solution.py:147
  44.0 26.1 %all-gather.14.cloned.1.call-done = bf16[2048,512]{1,0:T(8,128)(2,1)} async-done(((bf16[256,512]{1,0:T(8,128)(2,1)}), bf16[2048,512]{1,0:T(8,128)(2,1)}) %all-gather.14.cloned.1.call-update) | async-done | bytes 2097168 | tf_op jit(solution)/shard_map/all_gather | solution.py:146
  73.7 11.7 %all-reduce.2 = (f32[512]{0:T(512)S(1)}, f32[512]{0:T(512)S(1)}) all-reduce(f32[512]{0:T(512)S(1)} %get-tuple-element.85, f32[512]{0:T(512)S(1)} %get-tuple-element.87), channel_id=1, replica_groups=mesh['dp'=8,'mp'=4] {'mp'}, use_global_device_ids=true, to_apply=%region_5.6 | all-reduce | flops 1024 | bytes 8192 | tf_op jit(solution)/shard_map/psum | solution.py:166
  109.1 20.6 %all-gather.18.cloned.1.call-done = bf16[512,2048]{1,0:T(8,128)(2,1)} async-done(((bf16[512,256]{1,0:T(8,128)(2,1)}), bf16[512,2048]{1,0:T(8,128)(2,1)}) %all-gather.18.cloned.1.call-update) | async-done | bytes 2097168 | tf_op jit(solution)/shard_map/all_gather | solution.py:149
  134.1 43.7 %reduce-scatter.12.cloned.1.call-done = bf16[128,2048]{1,0:T(8,128)(2,1)} async-done(((bf16[512,2048]{1,0:T(8,128)(2,1)}), bf16[128,2048]{1,0:T(8,128)(2,1)}) %reduce-scatter.12.cloned.1.call-update) | async-done | bytes 524304 | tf_op jit(solution)/shard_map/reduce_scatter | solution.py:118
  180.2 44.0 %all-gather.20.cloned.1.call-done = bf16[512,2048]{1,0:T(8,128)(2,1)} async-done(((bf16[128,2048]{1,0:T(8,128)(2,1)}), bf16[512,2048]{1,0:T(8,128)(2,1)}) %all-gather.20.cloned.1.call-update) | async-done | bytes 2097168 | tf_op jit(solution)/shard_map/all_gather | solution.py:121
  230.3 48.9 %all-gather.22.cloned.1.call-done = bf16[2048,2048]{1,0:T(8,128)(2,1)} async-done(((bf16[256,2048]{1,0:T(8,128)(2,1)}), bf16[2048,2048]{1,0:T(8,128)(2,1)}) %all-gather.22.cloned.1.call-update) | async-done | bytes 8388624 | tf_op jit(solution)/shard_map/all_gather | solution.py:150
  279.2 10.5 fusion.47
  289.6 45.7 %all-gather.24.cloned.1.call-done = bf16[2048,2048]{1,0:T(8,128)(2,1)} async-done(((bf16[256,2048]{1,0:T(8,128)(2,1)}), bf16[2048,2048]{1,0:T(8,128)(2,1)}) %all-gather.24.cloned.1.call-update) | async-done | bytes 8388624 | tf_op jit(solution)/shard_map/all_gather | solution.py:151
  335.3 10.8 multiply_convert_fusion.3
  346.1 47.0 %all-gather.26.cloned.1.call-done = bf16[2048,2048]{1,0:T(8,128)(2,1)} async-done(((bf16[2048,256]{1,0:T(8,128)(2,1)}), bf16[2048,2048]{1,0:T(8,128)(2,1)}) %all-gather.26.cloned.1.call-update) | async-done | bytes 8388624 | tf_op jit(solution)/shard_map/all_gather | solution.py:152
  393.1 9.8 convolution_convert_fusion.7
  403.0 43.7 %reduce-scatter.14.cloned.1.call-done = bf16[128,2048]{1,0:T(8,128)(2,1)} async-done(((bf16[512,2048]{1,0:T(8,128)(2,1)}), bf16[128,2048]{1,0:T(8,128)(2,1)}) %reduce-scatter.14.cloned.1.call-update) | async-done | bytes 524304 | tf_op jit(solution)/shard_map/reduce_scatter | solution.py:118
  447.7 45.5 %all-gather.28.cloned.1.call-done = bf16[512,2048]{1,0:T(8,128)(2,1)} async-done(((bf16[128,2048]{1,0:T(8,128)(2,1)}), bf16[512,2048]{1,0:T(8,128)(2,1)}) %all-gather.28.cloned.1.call-update) | async-done | bytes 2097168 | tf_op jit(solution)/shard_map/all_gather | solution.py:121
  498.9 11.9 %multiply_convert_fusion.1 = (bf16[512,2048]{1,0:T(8,128)(2,1)}, bf16[512,2048]{1,0:T(8,128)(2,1)}) fusion(f32[512,2048]{1,0:T(8,128)S(1)} %copy-done.45, f32[512,2048]{1,0:T(8,128)} %get-tuple-element.92, bf16[2048,2048]{1,0:T(8,128)(2,1)} %all-gather.26.cloned.1.call-done, bf16[512,2048]{1,0:T(8,128)(2,1)S(1)} %copy-done.5, ...), kind=kOutput, calls=%fused_computation.38 | convolution fusion | flops 4318035968 | bytes 25182208 | tf_op jit(solution)/shard_map/dot_general | solution.py:197
  510.8 7.8 fusion.48
  518.6 9.6 add_convert_fusion.1
  528.2 42.6 %reduce-scatter.16.cloned.1.call-done = bf16[128,2048]{1,0:T(8,128)(2,1)} async-done(((bf16[512,2048]{1,0:T(8,128)(2,1)}), bf16[128,2048]{1,0:T(8,128)(2,1)}) %reduce-scatter.16.cloned.1.call-update) | async-done | bytes 524304 | tf_op jit(solution)/shard_map/reduce_scatter | solution.py:118
  571.3 46.0 %all-gather.30.cloned.1.call-done = bf16[512,2048]{1,0:T(8,128)(2,1)} async-done(((bf16[128,2048]{1,0:T(8,128)(2,1)}), bf16[512,2048]{1,0:T(8,128)(2,1)}) %all-gather.30.cloned.1.call-update) | async-done | bytes 2097168 | tf_op jit(solution)/shard_map/all_gather | solution.py:121
  646.0 9.9 all-reduce.1
  678.5 10.5 convolution_convert_fusion
  689.0 10.1 convolution_convert_fusion.1
  699.4 10.1 convolution_convert_fusion.2
  710.3 23.1 %all-reduce = (f32[512]{0:T(512)}, f32[512]{0:T(512)}, f32[2048]{0:T(1024)}, f32[2048]{0:T(1024)}) all-reduce(f32[512]{0:T(512)S(1)} %get-tuple-element.45, f32[512]{0:T(512)S(1)} %get-tuple-element.43, f32[2048]{0:T(1024)S(1)} %get-tuple-element.39, f32[2048]{0:T(1024)S(1)} %get-tuple-element.41), channel_id=1, replica_groups=mesh['dp'=8,'mp'=4] {'dp'}, use_global_device_ids=true, to_apply=%region_29.30 | all-reduce | flops 5120 | bytes 40960 | tf_op jit(solution)/shard_map/psum | solution.py:255
  733.4 16.1 %reduce-scatter.26.cloned.1.call-done = bf16[512,256]{1,0:T(8,128)(2,1)} async-done(((bf16[512,2048]{1,0:T(8,128)(2,1)}), bf16[512,256]{1,0:T(8,128)(2,1)}) %reduce-scatter.26.cloned.1.call-update) | async-done | bytes 262160 | tf_op jit(solution)/shard_map/reduce_scatter | solution.py:111
  751.2 42.5 %reduce-scatter.22.cloned.1.call-done = bf16[256,512]{0,1:T(8,128)(2,1)} async-done(((bf16[2048,512]{0,1:T(8,128)(2,1)}), bf16[256,512]{0,1:T(8,128)(2,1)}) %reduce-scatter.22.cloned.1.call-update) | async-done | bytes 262160 | tf_op jit(solution)/shard_map/reduce_scatter | solution.py:111
  795.6 42.4 %reduce-scatter.20.cloned.1.call-done = bf16[256,512]{0,1:T(8,128)(2,1)} async-done(((bf16[2048,512]{0,1:T(8,128)(2,1)}), bf16[256,512]{0,1:T(8,128)(2,1)}) %reduce-scatter.20.cloned.1.call-update) | async-done | bytes 262160 | tf_op jit(solution)/shard_map/reduce_scatter | solution.py:111
  839.9 42.4 %reduce-scatter.24.cloned.1.call-done = bf16[256,512]{0,1:T(8,128)(2,1)} async-done(((bf16[2048,512]{0,1:T(8,128)(2,1)}), bf16[256,512]{0,1:T(8,128)(2,1)}) %reduce-scatter.24.cloned.1.call-update) | async-done | bytes 262160 | tf_op jit(solution)/shard_map/reduce_scatter | solution.py:111
  884.2 72.9 %reduce-scatter.32.cloned.1.call-done = bf16[2048,256]{1,0:T(8,128)(2,1)} async-done(((bf16[2048,2048]{1,0:T(8,128)(2,1)}), bf16[2048,256]{1,0:T(8,128)(2,1)}) %reduce-scatter.32.cloned.1.call-update) | async-done | bytes 1048592 | tf_op jit(solution)/shard_map/reduce_scatter | solution.py:111
  959.8 72.1 %reduce-scatter.30.cloned.1.call-done = bf16[256,2048]{1,0:T(8,128)(2,1)} async-done(((bf16[2048,2048]{1,0:T(8,128)(2,1)}), bf16[256,2048]{1,0:T(8,128)(2,1)}) %reduce-scatter.30.cloned.1.call-update) | async-done | bytes 1048592 | tf_op jit(solution)/shard_map/reduce_scatter | solution.py:111
  1034.8 72.2 %reduce-scatter.28.cloned.1.call-done = bf16[256,2048]{1,0:T(8,128)(2,1)} async-done(((bf16[2048,2048]{1,0:T(8,128)(2,1)}), bf16[256,2048]{1,0:T(8,128)(2,1)}) %reduce-scatter.28.cloned.1.call-update) | async-done | bytes 1048592 | tf_op jit(solution)/shard_map/reduce_scatter | solution.py:111
  1109.7 44.5 %all-gather.32.cloned.1.call-done = bf16[512,2048]{1,0:T(8,128)(2,1)} async-done(((bf16[128,2048]{1,0:T(8,128)(2,1)}), bf16[512,2048]{1,0:T(8,128)(2,1)}) %all-gather.32.cloned.1.call-update) | async-done | bytes 2097168 | tf_op jit(solution)/shard_map/all_gather | solution.py:121
  (210 shorter events, 130.3 us)
Async XLA Ops:
  7.2 33.2 %all-gather.16.cloned.1.call-start = ((), (), s32[]{:S(2)}) async-start(), calls=%async_computation.13 | async-start | bytes 2359296 | tf_op jit(solution)/shard_map/all_gather | solution.py:147
  7.9 62.2 %all-gather.14.cloned.1.call-start = ((), (), s32[]{:S(2)}) async-start(), calls=%async_computation.12 | async-start | bytes 2359296 | tf_op jit(solution)/shard_map/all_gather | solution.py:146
  8.7 94.4 %all-gather.12.cloned.1.call-start = ((), (), s32[]{:S(2)}) async-start(), calls=%async_computation.11 | async-start | bytes 2359296 | tf_op jit(solution)/shard_map/all_gather | solution.py:148
  9.4 120.3 %all-gather.18.cloned.1.call-start = ((), (), s32[]{:S(2)}) async-start(), calls=%async_computation.14 | async-start | bytes 2359296 | tf_op jit(solution)/shard_map/all_gather | solution.py:149
  10.0 167.9 %reduce-scatter.12.cloned.1.call-start = ((), (), s32[]{:S(2)}) async-start(), calls=%async_computation.15 | async-start | bytes 2621440 | tf_op jit(solution)/shard_map/reduce_scatter | solution.py:118
  43.9 41.4 %copy-start.39 = (f32[512]{0:T(512)S(1)}, f32[512]{0:T(512)}, u32[]{:S(2)}) copy-start(f32[512]{0:T(512)} %param.27) | copy-start | bytes 6148
  73.6 17.8 %copy-start.10 = (f32[512,512]{0,1:T(8,128)}, f32[512,512]{0,1:T(8,128)S(1)}, u32[]{:S(2)}) copy-start(f32[512,512]{0,1:T(8,128)S(1)} %get-tuple-element.88) | copy-start | bytes 3145732
  73.6 17.7 %copy-start.38 = (f32[512]{0:T(512)S(1)}, f32[512]{0:T(512)}, u32[]{:S(2)}) copy-start(f32[512]{0:T(512)} %param.26) | copy-start | bytes 6148
  134.0 92.2 %copy-start.36 = (f32[2048]{0:T(1024)S(1)}, f32[2048]{0:T(1024)}, u32[]{:S(2)}) copy-start(f32[2048]{0:T(1024)} %param.28) | copy-start | bytes 24580
  134.1 90.1 %all-gather.20.cloned.1.call-start = ((), (), s32[]{:S(2)}) async-start(), calls=%async_computation.16 | async-start | bytes 2621440 | tf_op jit(solution)/shard_map/all_gather | solution.py:121
  177.9 101.3 %all-gather.22.cloned.1.call-start = ((), (), s32[]{:S(2)}) async-start(), calls=%async_computation.17 | async-start | bytes 9437184 | tf_op jit(solution)/shard_map/all_gather | solution.py:150
  178.6 156.7 %all-gather.24.cloned.1.call-start = ((), (), s32[]{:S(2)}) async-start(), calls=%async_computation.18 | async-start | bytes 9437184 | tf_op jit(solution)/shard_map/all_gather | solution.py:151
  179.4 213.7 %all-gather.26.cloned.1.call-start = ((), (), s32[]{:S(2)}) async-start(), calls=%async_computation.19 | async-start | bytes 9437184 | tf_op jit(solution)/shard_map/all_gather | solution.py:152
  180.1 266.6 %reduce-scatter.14.cloned.1.call-start = ((), (), s32[]{:S(2)}) async-start(), calls=%async_computation.20 | async-start | bytes 2621440 | tf_op jit(solution)/shard_map/reduce_scatter | solution.py:118
  230.3 105.1 %copy-start.30 = (bf16[512,2048]{1,0:T(8,128)(2,1)S(1)}, bf16[512,2048]{1,0:T(8,128)(2,1)}, u32[]{:S(2)}) copy-start(bf16[512,2048]{1,0:T(8,128)(2,1)} %fusion.22) | copy-start | bytes 6291460
  402.9 92.5 %copy-start.1 = (bf16[512,2048]{1,0:T(8,128)(2,1)S(1)}, bf16[512,2048]{1,0:T(8,128)(2,1)}, u32[]{:S(2)}) copy-start(bf16[512,2048]{1,0:T(8,128)(2,1)} %param.16) | copy-start | bytes 6291460
  402.9 92.5 %copy-start.37 = (f32[2048]{0:T(1024)S(1)}, f32[2048]{0:T(1024)}, u32[]{:S(2)}) copy-start(f32[2048]{0:T(1024)} %param.29) | copy-start | bytes 24580
  403.0 90.3 %all-gather.28.cloned.1.call-start = ((), (), s32[]{:S(2)}) async-start(), calls=%async_computation.21 | async-start | bytes 2621440 | tf_op jit(solution)/shard_map/all_gather | solution.py:121
  446.8 124.0 %reduce-scatter.16.cloned.1.call-start = ((), (), s32[]{:S(2)}) async-start(), calls=%async_computation.22 | async-start | bytes 2621440 | tf_op jit(solution)/shard_map/reduce_scatter | solution.py:118
  510.8 7.8 copy-start.46
  518.6 98.7 %copy-start = (bf16[512,2048]{1,0:T(8,128)(2,1)S(1)}, bf16[512,2048]{1,0:T(8,128)(2,1)}, u32[]{:S(2)}) copy-start(bf16[512,2048]{1,0:T(8,128)(2,1)} %all-gather.20.cloned.1.call-done) | copy-start | bytes 6291460
  528.2 89.1 %all-gather.30.cloned.1.call-start = ((), (), s32[]{:S(2)}) async-start(), calls=%async_computation.23 | async-start | bytes 2621440 | tf_op jit(solution)/shard_map/all_gather | solution.py:121
  570.8 138.8 %reduce-scatter.18.cloned.1.call-start = ((), (), s32[]{:S(2)}) async-start(), calls=%async_computation.24 | async-start | bytes 2621440 | tf_op jit(solution)/shard_map/reduce_scatter | solution.py:118
  638.7 5.7 copy-start.11
  664.0 85.5 %reduce-scatter.26.cloned.1.call-start = ((), (), s32[]{:S(2)}) async-start(), calls=%async_computation.29 | async-start | bytes 2359296 | tf_op jit(solution)/shard_map/reduce_scatter | solution.py:111
  668.4 125.3 %reduce-scatter.22.cloned.1.call-start = ((), (), s32[]{:S(2)}) async-start(), calls=%async_computation.27 | async-start | bytes 2359296 | tf_op jit(solution)/shard_map/reduce_scatter | solution.py:111
  671.1 166.9 %reduce-scatter.20.cloned.1.call-start = ((), (), s32[]{:S(2)}) async-start(), calls=%async_computation.26 | async-start | bytes 2359296 | tf_op jit(solution)/shard_map/reduce_scatter | solution.py:111
  673.8 208.6 %reduce-scatter.24.cloned.1.call-start = ((), (), s32[]{:S(2)}) async-start(), calls=%async_computation.28 | async-start | bytes 2359296 | tf_op jit(solution)/shard_map/reduce_scatter | solution.py:111
  678.2 278.9 %reduce-scatter.32.cloned.1.call-start = ((), (), s32[]{:S(2)}) async-start(), calls=%async_computation.32 | async-start | bytes 9437184 | tf_op jit(solution)/shard_map/reduce_scatter | solution.py:111
  689.0 343.0 %reduce-scatter.30.cloned.1.call-start = ((), (), s32[]{:S(2)}) async-start(), calls=%async_computation.31 | async-start | bytes 9437184 | tf_op jit(solution)/shard_map/reduce_scatter | solution.py:111
  699.1 407.8 %reduce-scatter.28.cloned.1.call-start = ((), (), s32[]{:S(2)}) async-start(), calls=%async_computation.30 | async-start | bytes 9437184 | tf_op jit(solution)/shard_map/reduce_scatter | solution.py:111
  709.6 444.7 %all-gather.32.cloned.1.call-start = ((), (), s32[]{:S(2)}) async-start(), calls=%async_computation.25 | async-start | bytes 2621440 | tf_op jit(solution)/shard_map/all_gather | solution.py:121
  (37 other events, 122.3 us)
Sparse Core Ops, SparseCore 0:
  9.9 30.4 all-gather.15
  42.3 27.7 all-gather.13
  72.0 27.7 all-gather.11
  101.5 28.0 all-gather.17
  134.2 43.6 reduce-scatter.11
  179.3 44.8 all-gather.19
  226.1 53.0 all-gather.21
  281.0 54.2 all-gather.23
  337.2 55.8 all-gather.25
  403.1 43.6 reduce-scatter.13
  448.3 44.8 all-gather.27
  528.3 42.4 reduce-scatter.15
  572.4 44.8 all-gather.29
  664.1 41.8 reduce-scatter.17
  709.1 40.3 reduce-scatter.25
  752.6 41.1 reduce-scatter.21
  796.9 41.1 reduce-scatter.19
  841.2 41.1 reduce-scatter.23
  885.8 71.2 reduce-scatter.31
  960.4 71.4 reduce-scatter.29
  1035.4 71.4 reduce-scatter.27
  1108.5 45.6 all-gather.31

commit v2 on v1

--- a/solution.py
+++ b/solution.py
@@ -1,15 +1,935 @@
-import math
-
-import jax
-import jax.numpy as jnp
+import functools, math
+import jax, jax.numpy as jnp
 from jax import lax
+from jax.experimental import pallas as pl
+from jax.experimental.pallas import tpu as pltpu
 from jax.sharding import PartitionSpec as P
 
 HD = 128
-
-
 EPS = 1e-06
 THETA = 500000.0
+UNIT = 256
+BF = jnp.bfloat16
+F32 = jnp.float32
+NT = (((1,), (1,)), ((), ()))
+
+
+def dot(a, b):
+    return jnp.dot(a, b, preferred_element_type=F32)
+
+
+def dot_nt(a, b):
+    return lax.dot_general(a, b, NT, preferred_element_type=F32)
+
+
+def dot_tn(a, b):
+    return lax.dot_general(a, b, (((0,), (0,)), ((), ())), preferred_element_type=F32)
+
+
+class Place:
+    def __init__(self, n_mp):
+        self.dp = lax.axis_index("dp")
+        self.z = lax.axis_index("mp")
+        self.n_mp = n_mp
+        self.c = lax.rem(self.dp, 2)
+        self.x = lax.rem(self.dp // 2, 2)
+        self.y = self.dp // 4
+        self.sib = self.dp + 1 - 2 * self.c
+        self.xn = self.dp + 2 - 4 * self.x
+        self.yn = self.dp + 4 - 8 * self.y
+        self.dg = self.xn + 4 - 8 * self.y
+        flip = 1 - 2 * self.c
+        self.order = (
+            self.dp, self.sib, self.xn, self.xn + flip,
+            self.yn, self.yn + flip, self.dg, self.dg + flip,
+        )
+
+    def at(self, dp):
+        return {"dp": dp}
+
+    def barrier(self):
+        sem = pltpu.get_barrier_semaphore()
+        for dp in (self.sib, self.xn, self.yn):
+            pl.semaphore_signal(sem, inc=1, device_id={"dp": dp}, device_id_type=pl.DeviceIdType.MESH)
+        for step in range(1, self.n_mp):
+            pl.semaphore_signal(
+                sem, inc=1, device_id={"mp": lax.rem(self.z + step, self.n_mp)},
+                device_id_type=pl.DeviceIdType.MESH,
+            )
+        pl.semaphore_wait(sem, 3 + self.n_mp - 1)
+
+
+def remote(src, dst, send, recv, device):
+    return pltpu.make_async_remote_copy(
+        src_ref=src, dst_ref=dst, send_sem=send, recv_sem=recv,
+        device_id=device, device_id_type=pl.DeviceIdType.MESH,
+    )
+
+
+class Gather:
+    def __init__(self, place, src, full, by_rows, send, recv, local):
+        self.place, self.src, self.full, self.by_rows = place, src, full, by_rows
+        self.send, self.recv, self.local = send, recv, local
+        self.rows, self.cols = src.shape
+        self.half = self.rows // 2
+
+    def spot(self, owner, part=None):
+        first, count = (0, self.rows) if part is None else (part * self.half, self.half)
+        if self.by_rows:
+            start = pl.multiple_of(owner * self.rows + first, self.half)
+            return self.full.at[pl.ds(start, count), :]
+        start = pl.multiple_of(owner * self.cols, self.cols)
+        return self.full.at[pl.ds(first, count), pl.ds(start, self.cols)]
+
+    def mine(self, part=None):
+        if part is None:
+            return self.src
+        return self.src.at[pl.ds(part * self.half, self.half), :]
+
+    def copies(self):
+        p = self.place
+        return {
+            0: (self.mine(0), p.dp, 0, p.xn, p.xn),
+            1: (self.mine(1), p.dp, 1, p.xn, p.xn),
+            2: (self.mine(0), p.dp, 0, p.yn, p.yn),
+            3: (self.mine(1), p.dp, 1, p.yn, p.yn),
+            4: (self.spot(p.yn, 1), p.yn, 1, p.xn, p.dg),
+            5: (self.spot(p.xn, 0), p.xn, 0, p.yn, p.dg),
+            6: (self.mine(), p.dp, None, p.sib, p.order[1]),
+            7: (self.spot(p.xn), p.xn, None, p.sib, p.order[3]),
+            8: (self.spot(p.yn), p.yn, None, p.sib, p.order[5]),
+            9: (self.spot(p.dg), p.dg, None, p.sib, p.order[7]),
+        }
+
+    def start(self, *kinds):
+        table = self.copies()
+        for kind in kinds:
+            src, owner, part, target, _ = table[kind]
+            remote(src, self.spot(owner, part), self.send.at[kind], self.recv.at[kind], {"dp": target}).start()
+
+    def arrived(self, *kinds):
+        table = self.copies()
+        for kind in kinds:
+            src, _, part, target, owner = table[kind]
+            spot = self.spot(owner, part)
+            remote(spot, spot, self.send.at[kind], self.recv.at[kind], {"dp": target}).wait_recv()
+
+    def own_copy(self):
+        return pltpu.make_async_copy(self.src, self.spot(self.place.dp), self.local)
+
+    def begin_a(self):
+        self.start(0, 3)
+
+    def begin_b(self):
+        self.start(1, 2, 6)
+        self.own_copy().start()
+
+    def relay(self):
+        self.arrived(0)
+        self.start(5)
+        self.arrived(3)
+        self.start(4)
+
+    def pass_on(self):
+        self.arrived(1)
+        self.start(7)
+        self.arrived(2)
+        self.start(8)
+
+    def last(self):
+        self.arrived(5, 4)
+        self.start(9)
+
+    def ready(self):
+        self.own_copy().wait()
+        self.arrived(6, 7, 8, 9)
+
+    def drain(self):
+        table = self.copies()
+        for kind in range(10):
+            src, owner, part, target, _ = table[kind]
+            remote(src, self.spot(owner, part), self.send.at[kind], self.recv.at[kind], {"dp": target}).wait_send()
+
+
+class RowSum:
+    def __init__(self, place, part, took, total, sems, columns):
+        self.place, self.part, self.took, self.total, self.sems = place, part, took, total, sems
+        self.columns = columns
+        self.width = part.shape[1] // len(columns)
+        self.count = len(columns) // 2
+
+    def spot(self, ref, flow, k):
+        block = self.columns[2 * k + flow]
+        return ref.at[:, pl.ds(pl.multiple_of(block * self.width, self.width), self.width)]
+
+    def where(self, flow):
+        p = self.place
+        at = p.z if flow == 0 else p.n_mp - 1 - p.z
+        step = 1 if flow == 0 else -1
+        return at, {"mp": p.z + step}, {"mp": p.z - step}
+
+    def forth(self, flow, k):
+        return remote(
+            self.spot(self.part, flow, k), self.took.at[flow, k],
+            self.sems.at[0, flow, k], self.sems.at[1, flow, k], self.where(flow)[1],
+        )
+
+    def back(self, flow, k):
+        spot = self.spot(self.total, flow, k)
+        return remote(spot, spot, self.sems.at[2, flow, k], self.sems.at[3, flow, k], self.where(flow)[2])
+
+    def begin(self, flow, k):
+        @pl.when(self.where(flow)[0] == 0)
+        def _():
+            self.forth(flow, k).start()
+
+    def gather_steps(self, tick):
+        for pos in range(1, self.place.n_mp):
+            k = tick - (pos - 1)
+            if 0 <= k < self.count:
+                for flow in range(2):
+                    @pl.when(self.where(flow)[0] == pos)
+                    def _():
+                        self.gather_step(flow, k)
+
+    def return_steps(self, tick):
+        for pos in range(self.place.n_mp - 2, -1, -1):
+            k = tick - (self.place.n_mp - 2 - pos)
+            if 0 <= k < self.count:
+                for flow in range(2):
+                    @pl.when(self.where(flow)[0] == pos)
+                    def _():
+                        self.return_step(flow, k)
+
+    @property
+    def ticks(self):
+        return self.count + self.place.n_mp - 2
+
+    def gather_step(self, flow, k):
+        at = self.where(flow)[0]
+        last = self.place.n_mp - 1
+
+        @pl.when(at > 0)
+        def _():
+            self.forth(flow, k).wait_recv()
+
+        @pl.when((at > 0) & (at < last))
+        def _():
+            spot = self.spot(self.part, flow, k)
+            spot[...] = (spot[...].astype(F32) + self.took[flow, k].astype(F32)).astype(BF)
+            self.forth(flow, k).start()
+
+        @pl.when(at == last)
+        def _():
+            mine = self.spot(self.part, flow, k)
+            self.spot(self.total, flow, k)[...] = (mine[...].astype(F32) + self.took[flow, k].astype(F32)).astype(BF)
+            self.back(flow, k).start()
+
+    def return_step(self, flow, k):
+        at = self.where(flow)[0]
+        last = self.place.n_mp - 1
+
+        @pl.when(at < last)
+        def _():
+            self.back(flow, k).wait_recv()
+
+        @pl.when((at > 0) & (at < last))
+        def _():
+            self.back(flow, k).start()
+
+    def drain(self):
+        last = self.place.n_mp - 1
+        for flow in range(2):
+            for k in range(self.count):
+                @pl.when(self.where(flow)[0] < last)
+                def _():
+                    self.forth(flow, k).wait_send()
+
+                @pl.when(self.where(flow)[0] > 0)
+                def _():
+                    self.back(flow, k).wait_send()
+
+
+def as_row(col):
+    n = col.shape[0]
+    r = lax.broadcasted_iota(jnp.int32, (n, n), 0)
+    s = lax.broadcasted_iota(jnp.int32, (n, n), 1)
+    return jnp.sum(jnp.where(r == s, col, 0.0), axis=0, keepdims=True)
+
+
+def as_col(row):
+    n = row.shape[1]
+    r = lax.broadcasted_iota(jnp.int32, (n, n), 0)
+    s = lax.broadcasted_iota(jnp.int32, (n, n), 1)
+    return jnp.sum(jnp.where(r == s, row, 0.0), axis=1, keepdims=True)
+
+
+class SmallSum:
+    def __init__(self, place, slots, sems):
+        self.place, self.slots, self.sems = place, slots, sems
+
+    def copy(self, step):
+        p = self.place
+        return remote(
+            self.slots.at[0], self.slots.at[step], self.sems.at[0, step], self.sems.at[1, step],
+            {"mp": lax.rem(p.z + step, p.n_mp)},
+        )
+
+    def begin(self):
+        for step in range(1, self.place.n_mp):
+            self.copy(step).start()
+
+    def end(self):
+        for step in range(1, self.place.n_mp):
+            self.copy(step).wait_recv()
+        total = self.slots[0]
+        for step in range(1, self.place.n_mp):
+            total = total + self.slots[step]
+        return total
+
+    def drain(self):
+        for step in range(1, self.place.n_mp):
+            self.copy(step).wait_send()
+
+
+def turn(values, cos_tab, sin_tab):
+    return values * cos_tab + pltpu.roll(values, HD // 2, 1) * sin_tab
+
+
+def forward_kernel(
+    n_mp,
+    x_in, wq_in, wk_in, wv_in, wo_in, wg_in, wu_in, wd_in,
+    cos_ref, sin_ref, seg_col, seg_row, q_gain, k_gain, a_gain,
+    wq_out, wk_out, wv_out, wo_out, wg_out, wu_out, wd_out,
+    qp_out, kp_out, qr_out, kr_out, v_out, o_out, stat_out, raw_a_out, h_out,
+    gate_out, up_out, act_out, raw_f_out,
+    wq, wk, wv, wo, wg, wu, wd,
+    x, qp, kp, qr, kr, v, o, stat, raw_a, h, gate, up, act, raw_f, part, took, sums,
+    g_send, g_recv, g_local, sum_a, sum_f, small, out_sem, x_sem,
+):
+    place = Place(n_mp)
+    rows, width = x.shape
+    local = qp.shape[1]
+    heads = local // HD
+    scale = 1.0 / math.sqrt(HD)
+    place.barrier()
+    ins = (wq_in, wk_in, wv_in, wo_in, wg_in, wu_in, wd_in)
+    fulls = (wq, wk, wv, wo, wg, wu, wd)
+    outs = (wq_out, wk_out, wv_out, wo_out, wg_out, wu_out, wd_out)
+    gq, gk, gv, go, gg, gu, gd = [
+        Gather(place, ins[i], fulls[i], i not in (3, 6), g_send.at[i], g_recv.at[i], g_local.at[i])
+        for i in range(7)
+    ]
+    gathers = (gq, gk, gv, go, gg, gu, gd)
+    started = []
+
+    def save(index, src, dst):
+        copy = pltpu.make_async_copy(src, dst, out_sem.at[index])
+        copy.start()
+        started.append(copy)
+
+    get_x = pltpu.make_async_copy(x_in, x, x_sem)
+    get_x.start()
+    gq.begin_a()
+    gq.begin_b()
+    gk.begin_a()
+    gk.begin_b()
+    gq.relay()
+    gv.begin_a()
+    gq.pass_on()
+    gv.begin_b()
+    gk.relay()
+    go.begin_a()
+    gk.pass_on()
+    go.begin_b()
+    gq.last()
+    get_x.wait()
+    gq.ready()
+    save(0, wq, wq_out)
+    half = rows // 2
+    norm_sum = SmallSum(place, sums, small)
+
+    def project(full, dst):
+        squares = []
+        for r in range(2):
+            value = dot(x[r * half:(r + 1) * half, :], full[...])
+            dst[r * half:(r + 1) * half, :] = value.astype(dst.dtype)
+            squares.append(jnp.sum(value * value, axis=1, keepdims=True))
+        return jnp.concatenate(squares, axis=0)
+
+    sums[0] = jnp.zeros(sums.shape[1:], F32)
+    sums[0, 0:1, :] = as_row(project(wq, qp))
+    gv.relay()
+    gk.last()
+    gk.ready()
+    save(1, wk, wk_out)
+    sums[0, 1:2, :] = as_row(project(wk, kp))
+    norm_sum.begin()
+    gv.pass_on()
+    go.relay()
+    gg.begin_a()
+    go.pass_on()
+    gg.begin_b()
+    gv.last()
+    gv.ready()
+    save(2, wv, wv_out)
+    project(wv, v)
+    totals = norm_sum.end()
+    inv_q = lax.rsqrt(as_col(totals[0:1, :]) / width + EPS)
+    inv_k = lax.rsqrt(as_col(totals[1:2, :]) / width + EPS)
+    stat[:, heads:heads + 1] = inv_q
+    stat[:, heads + 1:heads + 2] = inv_k
+    save(7, qp, qp_out)
+    save(8, kp, kp_out)
+    save(9, v, v_out)
+    block = rows // 4
+    for hd in range(heads):
+        cols = slice(hd * HD, (hd + 1) * HD)
+        qr[:, cols] = turn(qp[:, cols] * inv_q * q_gain[:, cols], cos_ref[...], sin_ref[...]).astype(BF)
+        kr[:, cols] = turn(kp[:, cols] * inv_k * k_gain[:, cols], cos_ref[...], sin_ref[...]).astype(BF)
+    save(10, qr, qr_out)
+    save(11, kr, kr_out)
+    for rb in range(4):
+        near = slice(rb * block, (rb + 1) * block)
+        keys = (rb + 1) * block
+        t_at = lax.broadcasted_iota(jnp.int32, (block, keys), 0) + rb * block
+        s_at = lax.broadcasted_iota(jnp.int32, (block, keys), 1)
+        allowed = (seg_col[near, :] == seg_row[:, 0:keys]) & (s_at <= t_at)
+        for hd in range(heads):
+            cols = slice(hd * HD, (hd + 1) * HD)
+            scores = jnp.where(allowed, dot_nt(qr[near, cols], kr[0:keys, cols]) * scale, -1e30)
+            top = jnp.max(scores, axis=1, keepdims=True)
+            weights = jnp.exp(scores - top)
+            norm = jnp.sum(weights, axis=1, keepdims=True)
+            stat[near, hd:hd + 1] = top + jnp.log(norm)
+            o[near, cols] = dot((weights / norm).astype(BF), v[0:keys, cols]).astype(BF)
+    save(12, o, o_out)
+    save(13, stat, stat_out)
+    go.last()
+    go.ready()
+    save(3, wo, wo_out)
+    step_of = lambda block: pl.ds(pl.multiple_of(block * (width // 8), width // 8), width // 8)
+    sum_attn = RowSum(place, part, took, raw_a, sum_a, place.order)
+    for at in range(8):
+        cols = step_of(place.order[at])
+        part[:, cols] = dot(o[...], wo[:, cols]).astype(BF)
+        sum_attn.begin(at % 2, at // 2)
+    gu.begin_a()
+    for tick in range(sum_attn.ticks):
+        sum_attn.gather_steps(tick)
+        if tick == 0:
+            gg.relay()
+            gu.begin_b()
+        if tick == 2:
+            gg.pass_on()
+        if tick == 3:
+            gg.last()
+            gd.begin_a()
+    for tick in range(sum_attn.ticks):
+        sum_attn.return_steps(tick)
+        if tick == 0:
+            gu.relay()
+            gd.begin_b()
+        if tick == 2:
+            gu.pass_on()
+    sum_attn.drain()
+    save(14, raw_a, raw_a_out)
+    tile = rows // 8
+
+    def mid(at, carry):
+        near = pl.ds(pl.multiple_of(at * tile, tile), tile)
+        raw = raw_a[near, :].astype(F32)
+        inv = lax.rsqrt(jnp.mean(raw * raw, axis=1, keepdims=True) + EPS)
+        h[near, :] = (x[near, :].astype(F32) + raw * inv * a_gain[...]).astype(BF)
+        return carry
+
+    lax.fori_loop(0, 8, mid, 0)
+    save(15, h, h_out)
+    gg.ready()
+    save(4, wg, wg_out)
+    n_tile = gate.shape[1] // UNIT
+
+    def gate_tile(at, carry):
+        cols = pl.ds(pl.multiple_of(at * UNIT, UNIT), UNIT)
+        gate[:, cols] = dot(h[...], wg[:, cols]).astype(BF)
+        return carry
+
+    lax.fori_loop(0, n_tile, gate_tile, 0)
+    gu.last()
+    gd.relay()
+    gu.ready()
+    save(5, wu, wu_out)
+
+    def up_tile(at, carry):
+        cols = pl.ds(pl.multiple_of(at * UNIT, UNIT), UNIT)
+        value = dot(h[...], wu[:, cols])
+        up[:, cols] = value.astype(BF)
+        pre = gate[:, cols].astype(F32)
+        act[:, cols] = (pre * jax.nn.sigmoid(pre) * value).astype(BF)
+        return carry
+
+    lax.fori_loop(0, n_tile, up_tile, 0)
+    save(16, gate, gate_out)
+    save(17, up, up_out)
+    save(18, act, act_out)
+    sum_ffn = RowSum(place, part, took, raw_f, sum_f, place.order)
+    for at in range(8):
+        if at == 0:
+            gd.own_copy().wait()
+        elif at == 1:
+            gd.arrived(6)
+        elif at == 2:
+            gd.pass_on()
+        elif at == 3:
+            gd.arrived(7)
+        elif at == 5:
+            gd.arrived(8)
+        elif at == 6:
+            gd.last()
+        elif at == 7:
+            gd.arrived(9)
+        cols = step_of(place.order[at])
+        part[:, cols] = dot(act[...], wd[:, cols]).astype(BF)
+        sum_ffn.begin(at % 2, at // 2)
+        if at in (4, 6):
+            sum_ffn.gather_steps((at - 4) // 2)
+    save(6, wd, wd_out)
+    for tick in range(2, sum_ffn.ticks):
+        sum_ffn.gather_steps(tick)
+    for tick in range(sum_ffn.ticks):
+        sum_ffn.return_steps(tick)
+    save(19, raw_f, raw_f_out)
+    sum_ffn.drain()
+    norm_sum.drain()
+    for g in gathers:
+        g.drain()
+    for copy in started:
+        copy.wait()
+
+
+def forward_call(n_mp, x, weights, cos_tab, sin_tab, seg_col, seg_row, q_gain, k_gain, a_gain):
+    rows, width = x.shape
+    n_dp = 8
+    local = weights[0].shape[1]
+    ff = weights[4].shape[1]
+    any_spec = pl.BlockSpec(memory_space=pl.ANY)
+    vmem = pl.BlockSpec(memory_space=pltpu.VMEM)
+    S = jax.ShapeDtypeStruct
+    fulls = [(width, local)] * 3 + [(local, width)] + [(width, ff)] * 2 + [(ff, width)]
+    acts = [
+        ((rows, local), F32), ((rows, local), F32), ((rows, local), BF), ((rows, local), BF),
+        ((rows, local), BF), ((rows, local), BF), ((rows, 128), F32), ((rows, width), BF),
+        ((rows, width), BF), ((rows, ff), BF), ((rows, ff), BF), ((rows, ff), BF), ((rows, width), BF),
+    ]
+    V = pltpu.VMEM
+    dma = pltpu.SemaphoreType.DMA
+    return pl.pallas_call(
+        functools.partial(forward_kernel, n_mp),
+        out_shape=[S(s, BF) for s in fulls] + [S(s, d) for s, d in acts],
+        in_specs=[any_spec] * 8 + [vmem] * 7,
+        out_specs=[any_spec] * 20,
+        scratch_shapes=[V(s, BF) for s in fulls]
+        + [V((rows, width), BF)]
+        + [V(s, d) for s, d in acts]
+        + [V((rows, width), BF), V((2, 4, rows, width // 8), BF), V((n_mp, 8, rows), F32)]
+        + [dma((7, 10)), dma((7, 10)), dma((7,)), dma((4, 2, 4)), dma((4, 2, 4)), dma((2, n_mp)), dma((20,)), dma(())],
+        compiler_params=pltpu.CompilerParams(
+            collective_id=0, has_side_effects=True, vmem_limit_bytes=67043328,
+        ),
+    )(x, *weights, cos_tab, sin_tab, seg_col, seg_row, q_gain, k_gain, a_gain)
+
+
+class Scatter:
+    def __init__(self, place, out, give, got, sum_a, sum_b, got_a, got_b, end_a, end_b, done, sems, out_sems, n_units):
+        self.place, self.out, self.n_units = place, out, n_units
+        self.give, self.got, self.sum_a, self.sum_b = give, got, sum_a, sum_b
+        self.got_a, self.got_b, self.end_a, self.end_b, self.done = got_a, got_b, end_a, end_b, done
+        self.sems, self.out_sems = sems, out_sems
+        self.rows, self.cols = give.shape[2:]
+        self.half = self.rows // 2
+        self.unit = 0
+
+    def send(self, kind, u):
+        p, s = self.place, u % 4
+        src, dst, target = {
+            0: (self.give.at[u % 2], self.got.at[s], p.sib),
+            1: (self.sum_a.at[s, 1 - p.x], self.got_a.at[s], p.xn),
+            2: (self.sum_b.at[s, 1 - p.y], self.got_b.at[s], p.yn),
+            3: (self.sum_a.at[s, p.x, 1 - p.y], self.end_a.at[s], p.yn),
+            4: (self.sum_b.at[s, p.y, 1 - p.x], self.end_b.at[s], p.xn),
+        }[kind]
+        return remote(src, dst, self.sems.at[0, kind, s], self.sems.at[1, kind, s], {"dp": target})
+
+    def write(self, u):
+        return pltpu.make_async_copy(self.done.at[u % 2], self.out.at[u], self.out_sems.at[u % 2])
+
+    def product(self, u, turned, right, col):
+        p = self.place
+        if u >= 2:
+            self.send(0, u - 2).wait_send()
+
+        def other(chip, carry):
+            near = pl.ds(pl.multiple_of((2 * chip + 1 - p.c) * self.rows, self.rows), self.rows)
+            self.give[u % 2, chip] = dot(turned[near, :], right[:, col]).astype(BF)
+            return carry
+
+        lax.fori_loop(0, 4, other, 0)
+        self.send(0, u).start()
+
+        def own(chip, carry):
+            near = pl.ds(pl.multiple_of((2 * chip + p.c) * self.rows, self.rows), self.rows)
+            value = dot(turned[near, :], right[:, col]).astype(BF)
+            y_to, x_to = chip // 2, lax.rem(chip, 2)
+            self.sum_a[u % 4, x_to, y_to] = value[:self.half]
+            self.sum_b[u % 4, y_to, x_to] = value[self.half:]
+            return carry
+
+        lax.fori_loop(0, 4, own, 0)
+
+    def across(self, u):
+        self.send(0, u).wait_recv()
+        s = u % 4
+
+        def add(chip, carry):
+            y_to, x_to = chip // 2, lax.rem(chip, 2)
+            more = self.got[s, chip].astype(F32)
+            self.sum_a[s, x_to, y_to] = (self.sum_a[s, x_to, y_to].astype(F32) + more[:self.half]).astype(BF)
+            self.sum_b[s, y_to, x_to] = (self.sum_b[s, y_to, x_to].astype(F32) + more[self.half:]).astype(BF)
+            return carry
+
+        lax.fori_loop(0, 4, add, 0)
+        self.send(1, u).start()
+        self.send(2, u).start()
+
+    def along(self, u):
+        p, s = self.place, u % 4
+        self.send(1, u).wait_recv()
+        for i in range(2):
+            self.sum_a[s, p.x, i] = (self.sum_a[s, p.x, i].astype(F32) + self.got_a[s, i].astype(F32)).astype(BF)
+        self.send(3, u).start()
+        self.send(2, u).wait_recv()
+        for i in range(2):
+            self.sum_b[s, p.y, i] = (self.sum_b[s, p.y, i].astype(F32) + self.got_b[s, i].astype(F32)).astype(BF)
+        self.send(4, u).start()
+        self.send(1, u).wait_send()
+        self.send(2, u).wait_send()
+
+    def finish(self, u):
+        p, s = self.place, u % 4
+        if u >= 2:
+            self.write(u - 2).wait()
+        self.send(3, u).wait_recv()
+        self.done[u % 2, :self.half] = self.sum_a[s, p.x, p.y].astype(F32) + self.end_a[s].astype(F32)
+        self.send(4, u).wait_recv()
+        self.done[u % 2, self.half:] = self.sum_b[s, p.y, p.x].astype(F32) + self.end_b[s].astype(F32)
+        self.write(u).start()
+        self.send(3, u).wait_send()
+        self.send(4, u).wait_send()
+
+    def tick(self, turned=None, right=None, col=None):
+        u = self.unit
+        self.unit += 1
+        if u < self.n_units:
+            self.product(u, turned, right, col)
+        if 0 <= u - 1 < self.n_units:
+            self.across(u - 1)
+        if 0 <= u - 2 < self.n_units:
+            self.along(u - 2)
+        if 0 <= u - 3 < self.n_units:
+            self.finish(u - 3)
+
+    def drain(self):
+        for u in (self.n_units - 2, self.n_units - 1):
+            self.send(0, u).wait_send()
+            self.write(u).wait()
+
+
+def turn_back(grads, cos_tab, sin_tab):
+    return grads * cos_tab - pltpu.roll(grads, HD // 2, 1) * sin_tab
+
+
+def backward_kernel(
+    n_mp,
+    wq_in, wk_in, wv_in, wo_in, wg_in, wu_in, wd_in,
+    qp_in, kp_in, qr_in, kr_in, v_in, o_in, stat_in, raw_a_in, h_in, gate_in, up_in, act_in, raw_f_in,
+    x_in, cot_in, mask, cos_ref, sin_ref, seg_col, seg_row, q_gain, k_gain, a_gain, f_gain,
+    units_out, raw_h_out, raw_x_out, gains_out,
+    wg, wu, wd,
+    qp, kp, qr, kr, v, o, stat, h, gate, up, act, d_ffn,
+    cot, part, took, raw_h, turned, d_heads, dqn, dkn, dk_sum, dv_sum, sums, gains, gains_got,
+    give, got, sum_a, sum_b, got_a, got_b, end_a, end_b, done,
+    s_sems, s_out, sum_h, sum_x, small, gain_sems, load_sems, out_sems,
+):
+    place = Place(n_mp)
+    rows, width = cot.shape
+    local = qp.shape[1]
+    ff = gate.shape[1]
+    heads = local // HD
+    scale = 1.0 / math.sqrt(HD)
+    loads = {}
+
+    def load(name, src, dst):
+        copy = pltpu.make_async_copy(src, dst, load_sems.at[len(loads)])
+        loads[name] = copy
+        copy.start()
+
+    def need(*names):
+        for name in names:
+            loads[name].wait()
+
+    load("raw_f", raw_f_in, d_ffn)
+    load("cot", cot_in, cot)
+    load("act", act_in, act)
+    load("wd", wd_in, wd)
+    load("gate", gate_in, gate)
+    load("up", up_in, up)
+    load("wg", wg_in, wg)
+    load("wu", wu_in, wu)
+    load("h", h_in, h)
+    for name, src, dst in (
+        ("o", o_in, o), ("qr", qr_in, qr), ("kr", kr_in, kr), ("v", v_in, v),
+        ("stat", stat_in, stat), ("qp", qp_in, qp), ("kp", kp_in, kp),
+    ):
+        load(name, src, dst)
+    place.barrier()
+    tile = rows // 8
+    gains[...] = jnp.zeros(gains.shape, F32)
+
+    def row_tile(at):
+        return pl.ds(pl.multiple_of(at * tile, tile), tile)
+
+    def back_ffn(at, carry):
+        near = row_tile(at)
+        raw = d_ffn[near, :].astype(F32)
+        dy = mask[near, :] * cot[near, :].astype(F32)
+        inv = lax.rsqrt(jnp.mean(raw * raw, axis=1, keepdims=True) + EPS)
+        gains[0:1, :] += jnp.sum(dy * raw * inv, axis=0, keepdims=True)
+        gained = f_gain[...] * dy
+        mean = jnp.mean(gained * raw, axis=1, keepdims=True)
+        d_ffn[near, :] = (inv * gained - raw * inv**3 * mean).astype(BF)
+        return carry
+
+    need("raw_f", "cot")
+    lax.fori_loop(0, 8, back_ffn, 0)
+
+    def flip(src):
+        def one(at, carry):
+            near = pl.ds(pl.multiple_of(at * UNIT, UNIT), UNIT)
+            turned[near, :] = src[:, near].T
+            return carry
+
+        lax.fori_loop(0, width // UNIT, one, 0)
+
+    scatter = Scatter(place, units_out, give, got, sum_a, sum_b, got_a, got_b, end_a, end_b, done, s_sems, s_out,
+                      (3 * ff + 4 * local) // UNIT)
+    flip(d_ffn)
+    need("act", "wd", "gate", "up")
+
+    def cols_of(at):
+        return slice(at * UNIT, (at + 1) * UNIT)
+
+    def back_act(at, carry):
+        cols = pl.ds(pl.multiple_of(at * UNIT, UNIT), UNIT)
+        d_act = dot_nt(d_ffn[...], wd[cols, :])
+        pre, upper = gate[:, cols].astype(F32), up[:, cols].astype(F32)
+        sig = jax.nn.sigmoid(pre)
+        up[:, cols] = (d_act * pre * sig).astype(BF)
+        gate[:, cols] = (d_act * upper * sig * (1.0 + pre * (1.0 - sig))).astype(BF)
+        return carry
+
+    n_ff = ff // UNIT
+    for at in range(n_ff // 2):
+        scatter.tick(turned, act, cols_of(at))
+        lax.fori_loop(2 * at, 2 * at + 2, back_act, 0)
+    load("wq", wq_in, wd.at[:, 0:local])
+    load("wk", wk_in, wd.at[:, local:2 * local])
+    load("wv", wv_in, wd.at[:, 2 * local:3 * local])
+    need("wg", "wu")
+    sum_back = RowSum(place, part, took, raw_h, sum_h, place.order)
+    step = width // 8
+
+    def step_of(block):
+        return pl.ds(pl.multiple_of(block * step, step), step)
+
+    for at in range(8):
+        spot = step_of(place.order[at])
+        part[:, spot] = (dot_nt(gate[...], wg[spot, :]) + dot_nt(up[...], wu[spot, :])).astype(BF)
+        sum_back.begin(at % 2, at // 2)
+        if at % 2 == 1:
+            scatter.tick(turned, act, cols_of(n_ff // 2 + at // 2))
+    raw_a = act
+    load("raw_a", raw_a_in, raw_a)
+    need("h")
+    flip(h)
+    load("wo", wo_in, wg.at[0:local, :])
+    load("x", x_in, wu.at[0:rows, :])
+    queue = [(gate, at) for at in range(n_ff)] + [(up, at) for at in range(n_ff)]
+
+    def more():
+        right, at = queue.pop(0)
+        scatter.tick(turned, right, cols_of(at))
+
+    for tick in range(sum_back.ticks):
+        sum_back.gather_steps(tick)
+        more()
+    for tick in range(sum_back.ticks):
+        sum_back.return_steps(tick)
+        if tick < sum_back.ticks - 1:
+            more()
+    sum_back.drain()
+    raw_h_copy = pltpu.make_async_copy(raw_h, raw_h_out, out_sems.at[0])
+    raw_h_copy.start()
+    need("raw_a")
+    d_attn = wu.at[rows:2 * rows, :]
+
+    def back_attn(at, carry):
+        near = row_tile(at)
+        raw = raw_a[near, :].astype(F32)
+        dh = mask[near, :] * cot[near, :].astype(F32) + raw_h[near, :].astype(F32)
+        inv = lax.rsqrt(jnp.mean(raw * raw, axis=1, keepdims=True) + EPS)
+        gains[1:2, :] += jnp.sum(dh * raw * inv, axis=0, keepdims=True)
+        gained = a_gain[...] * dh
+        mean = jnp.mean(gained * raw, axis=1, keepdims=True)
+        d_attn[near, :] = (inv * gained - raw * inv**3 * mean).astype(BF)
+        return carry
+
+    lax.fori_loop(0, 8, back_attn, 0)
+    need("wo", "o")
+    d_heads[...] = dot_nt(d_attn[...], wg[0:local, :]).astype(BF)
+    need("qr", "kr", "v", "stat", "qp", "kp")
+    more()
+    block = rows // 4
+    dval = wu.at[2 * rows:3 * rows, 2 * local:3 * local]
+    for hd in range(heads):
+        cols = slice(hd * HD, (hd + 1) * HD)
+        dk_sum[...] = jnp.zeros(dk_sum.shape, F32)
+        dv_sum[...] = jnp.zeros(dv_sum.shape, F32)
+        for rb in range(4):
+            near = slice(rb * block, (rb + 1) * block)
+            keys = (rb + 1) * block
+            t_at = lax.broadcasted_iota(jnp.int32, (block, keys), 0) + rb * block
+            s_at = lax.broadcasted_iota(jnp.int32, (block, keys), 1)
+            allowed = (seg_col[near, :] == seg_row[:, 0:keys]) & (s_at <= t_at)
+            scores = dot_nt(qr[near, cols], kr[0:keys, cols]) * scale
+            probs = jnp.where(allowed, jnp.exp(jnp.where(allowed, scores, -1e30) - stat[near, hd:hd + 1]), 0.0)
+            grad = d_heads[near, cols]
+            d_prob = dot_nt(grad, v[0:keys, cols])
+            delta = jnp.sum(grad.astype(F32) * o[near, cols].astype(F32), axis=1, keepdims=True)
+            d_score = (probs * (d_prob - delta)).astype(BF)
+            dqn[near, cols] = turn_back(
+                dot(d_score, kr[0:keys, cols]) * scale, cos_ref[near, :], sin_ref[near, :])
+            dk_sum[0:keys, :] += dot_tn(d_score, qr[near, cols])
+            dv_sum[0:keys, :] += dot_tn(probs.astype(BF), grad)
+        dkn[:, cols] = turn_back(dk_sum[...] * scale, cos_ref[...], sin_ref[...])
+        dval[:, cols] = dv_sum[...].astype(BF)
+        if hd % 2 == 1 and queue:
+            more()
+    inv_q, inv_k = stat[:, heads:heads + 1], stat[:, heads + 1:heads + 2]
+    row_sum = SmallSum(place, sums, small)
+    sums[0] = jnp.zeros(sums.shape[1:], F32)
+    grad_q, grad_k = dqn[...], dkn[...]
+    gains[2:3, 0:local] = jnp.sum(grad_q * qp[...] * inv_q, axis=0, keepdims=True)
+    gains[3:4, 0:local] = jnp.sum(grad_k * kp[...] * inv_k, axis=0, keepdims=True)
+    sums[0, 0:1, :] = as_row(jnp.sum(q_gain[...] * grad_q * qp[...], axis=1, keepdims=True))
+    sums[0, 1:2, :] = as_row(jnp.sum(k_gain[...] * grad_k * kp[...], axis=1, keepdims=True))
+    row_sum.begin()
+    while queue:
+        more()
+    flip(d_attn)
+    scatter.tick(turned, o, cols_of(0))
+    totals = row_sum.end()
+    mean_q, mean_k = as_col(totals[0:1, :]) / width, as_col(totals[1:2, :]) / width
+    dq = wu.at[2 * rows:3 * rows, 0:local]
+    dk = wu.at[2 * rows:3 * rows, local:2 * local]
+    dq[...] = (inv_q * (q_gain[...] * dqn[...]) - qp[...] * inv_q**3 * mean_q).astype(BF)
+    dk[...] = (inv_k * (k_gain[...] * dkn[...]) - kp[...] * inv_k**3 * mean_k).astype(BF)
+    need("wq", "wk", "wv", "x")
+    raw_x = d_ffn
+    sum_in = RowSum(place, part, took, raw_x, sum_x, place.order)
+    for at in range(8):
+        spot = step_of(place.order[at])
+        value = dot_nt(dq[...], wd[spot, 0:local]) + dot_nt(dk[...], wd[spot, local:2 * local])
+        part[:, spot] = (value + dot_nt(dval[...], wd[spot, 2 * local:3 * local])).astype(BF)
+        sum_in.begin(at % 2, at // 2)
+    scatter.tick(turned, o, cols_of(1))
+    flip(wu.at[0:rows, :])
+    queue = [(right, at) for right in (dq, dk, dval) for at in range(local // UNIT)]
+    for tick in range(sum_in.ticks):
+        sum_in.gather_steps(tick)
+        if queue:
+            more()
+        else:
+            scatter.tick()
+    partners = (place.sib, place.xn, place.yn)
+
+    def gain_copy(at):
+        return remote(gains.at[pl.ds(8 * at, 8), :], gains_got.at[at], gain_sems.at[0, at], gain_sems.at[1, at],
+                      {"dp": partners[at]})
+
+    gain_copy(0).start()
+    for tick in range(sum_in.ticks):
+        sum_in.return_steps(tick)
+        if queue:
+            more()
+        elif scatter.unit < scatter.n_units + 3:
+            scatter.tick()
+        if tick < 3:
+            gain_copy(tick).wait_recv()
+            gains[8 * tick + 8:8 * tick + 16, :] = gains[8 * tick:8 * tick + 8, :] + gains_got[tick]
+            if tick < 2:
+                gain_copy(tick + 1).start()
+    while scatter.unit < scatter.n_units + 3:
+        scatter.tick()
+    outs = [
+        raw_h_copy,
+        pltpu.make_async_copy(raw_x, raw_x_out, out_sems.at[1]),
+        pltpu.make_async_copy(gains.at[24:32, :], gains_out, out_sems.at[2]),
+    ]
+    outs[1].start()
+    outs[2].start()
+    for at in range(3):
+        gain_copy(at).wait_send()
+    sum_in.drain()
+    row_sum.drain()
+    scatter.drain()
+    for copy in outs:
+        copy.wait()
+
+
+def backward_call(n_mp, saved, x, cot, mask, cos_tab, sin_tab, seg_col, seg_row, q_gain, k_gain, a_gain, f_gain):
+    rows, width = x.shape
+    local = saved[0].shape[1]
+    ff = saved[4].shape[1]
+    any_spec = pl.BlockSpec(memory_space=pl.ANY)
+    vmem = pl.BlockSpec(memory_space=pltpu.VMEM)
+    S = jax.ShapeDtypeStruct
+    V = pltpu.VMEM
+    dma = pltpu.SemaphoreType.DMA
+    n_units = (3 * ff + 4 * local) // UNIT
+    high = width // 8
+    return pl.pallas_call(
+        functools.partial(backward_kernel, n_mp),
+        out_shape=[S((n_units, high, UNIT), F32), S((rows, width), BF), S((rows, width), BF), S((8, width), F32)],
+        in_specs=[any_spec] * 22 + [vmem] * 9,
+        out_specs=[any_spec] * 4,
+        scratch_shapes=[
+            V((width, ff), BF), V((width, ff), BF), V((ff, width), BF),
+            V((rows, local), F32), V((rows, local), F32), V((rows, local), BF), V((rows, local), BF),
+            V((rows, local), BF), V((rows, local), BF), V((rows, 128), F32),
+            V((rows, width), BF), V((rows, ff), BF), V((rows, ff), BF), V((rows, ff), BF), V((rows, width), BF),
+            V((rows, width), BF), V((rows, width), BF), V((2, 4, rows, width // 8), BF), V((rows, width), BF),
+            V((width, rows), BF), V((rows, local), BF), V((rows, local), F32), V((rows, local), F32),
+            V((rows, HD), F32), V((rows, HD), F32), V((n_mp, 8, rows), F32), V((32, width), F32), V((3, 8, width), F32),
+            V((2, 4, high, UNIT), BF), V((4, 4, high, UNIT), BF),
+            V((4, 2, 2, high // 2, UNIT), BF), V((4, 2, 2, high // 2, UNIT), BF),
+            V((4, 2, high // 2, UNIT), BF), V((4, 2, high // 2, UNIT), BF),
+            V((4, high // 2, UNIT), BF), V((4, high // 2, UNIT), BF), V((2, high, UNIT), F32),
+            dma((2, 5, 4)), dma((2,)), dma((4, 2, 4)), dma((4, 2, 4)), dma((2, n_mp)), dma((2, 3)), dma((24,)), dma((3,)),
+        ],
+        compiler_params=pltpu.CompilerParams(
+            collective_id=1, has_side_effects=True, vmem_limit_bytes=67043328,
+        ),
+    )(*saved, x, cot, mask, cos_tab, sin_tab, seg_col, seg_row, q_gain, k_gain, a_gain, f_gain)
 
 
 def doc_positions(seg_row):
@@ -270,41 +1190,105 @@
     )
 
 
+def with_kernels(n_mp, hidden_in, cotangent, segments, live_counts, *rest):
+    weights, (query_gain, key_gain, attn_gain, ffn_gain) = rest[:7], rest[7:]
+    seg = segments[0]
+    rows = hidden_in.shape[0]
+    local, ff = weights[0].shape[1], weights[4].shape[1]
+    cos_tab, sin_tab = (tab[:, 0] for tab in rotary_tables(doc_positions(seg), HD))
+    cos_tab = jnp.concatenate([cos_tab, cos_tab], axis=1)
+    sin_tab = jnp.concatenate([-sin_tab, sin_tab], axis=1)
+    mask = (jnp.arange(rows, dtype=jnp.int32) < live_counts[0]).astype(F32)[:, None]
+    common = (
+        cos_tab, sin_tab, seg[:, None], seg[None, :], query_gain[None], key_gain[None], attn_gain[None]
+    )
+    saved = forward_call(n_mp, hidden_in, weights, *common)
+    units, raw_h, raw_x, gains = backward_call(
+        n_mp, saved, hidden_in, cotangent, mask, *common, ffn_gain[None]
+    )
+    raw_a, raw_f = saved[14].astype(F32), saved[19].astype(F32)
+    inv_a = lax.rsqrt(jnp.mean(raw_a * raw_a, axis=1, keepdims=True) + EPS)
+    inv_f = lax.rsqrt(jnp.mean(raw_f * raw_f, axis=1, keepdims=True) + EPS)
+    h_mid = hidden_in.astype(F32) + raw_a * inv_a * attn_gain
+    hidden_out = (mask * (h_mid + raw_f * inv_f * ffn_gain)).astype(BF)
+    grad_in = mask * cotangent.astype(F32) + raw_h.astype(F32) + raw_x.astype(F32)
+    n_ff, n_local = ff // UNIT, local // UNIT
+    high = units.shape[1]
+
+    def side(first, count):
+        return jnp.transpose(units[first:first + count], (1, 0, 2)).reshape(high, count * UNIT)
+
+    def down(first, count):
+        return jnp.transpose(units[first:first + count], (0, 2, 1)).reshape(count * UNIT, high)
+
+    at = 3 * n_ff
+    return (
+        hidden_out,
+        grad_in,
+        side(at + n_local, n_local),
+        side(at + 2 * n_local, n_local),
+        side(at + 3 * n_local, n_local),
+        down(at, n_local),
+        side(n_ff, n_ff),
+        side(2 * n_ff, n_ff),
+        down(0, n_ff),
+        gains[2, :local],
+        gains[3, :local],
+        gains[1],
+        gains[0],
+    )
+
+
+def kernels_fit(mesh, hidden_in, segments, w_query, w_gate):
+    n_dp, n_mp = mesh.shape["dp"], mesh.shape["mp"]
+    rows, width = hidden_in.shape[0] // n_dp, hidden_in.shape[1]
+    local, ff = w_query.shape[1] // n_mp, w_gate.shape[1] // n_mp
+    even = width % (8 * UNIT) == 0 and local % UNIT == 0 and ff % (2 * UNIT) == 0
+    fits = rows == UNIT * 2 and width == 8 * UNIT and local == rows and ff == width
+    return n_dp == 8 and n_mp >= 2 and even and fits
+
+
 def solution(mesh):
-    return jax.shard_map(
-        on_device,
-        mesh=mesh,
-        in_specs=(
-            P("dp", None),
-            P("dp", None),
-            P("dp", None),
-            P("dp"),
-            P("dp", "mp"),
-            P("dp", "mp"),
-            P("dp", "mp"),
-            P("mp", "dp"),
-            P("dp", "mp"),
-            P("dp", "mp"),
-            P("mp", "dp"),
-            P("mp"),
-            P("mp"),
-            P(),
-            P(),
-        ),
-        out_specs=(
-            P("dp", None),
-            P("dp", None),
-            P("dp", "mp"),
-            P("dp", "mp"),
-            P("dp", "mp"),
-            P("mp", "dp"),
-            P("dp", "mp"),
-            P("dp", "mp"),
-            P("mp", "dp"),
-            P("mp"),
-            P("mp"),
-            P(),
-            P(),
-        ),
-        check_vma=False,
-    )
+    in_specs = (
+        P("dp", None),
+        P("dp", None),
+        P("dp", None),
+        P("dp"),
+        P("dp", "mp"),
+        P("dp", "mp"),
+        P("dp", "mp"),
+        P("mp", "dp"),
+        P("dp", "mp"),
+        P("dp", "mp"),
+        P("mp", "dp"),
+        P("mp"),
+        P("mp"),
+        P(),
+        P(),
+    )
+    out_specs = (
+        P("dp", None),
+        P("dp", None),
+        P("dp", "mp"),
+        P("dp", "mp"),
+        P("dp", "mp"),
+        P("mp", "dp"),
+        P("dp", "mp"),
+        P("dp", "mp"),
+        P("mp", "dp"),
+        P("mp"),
+        P("mp"),
+        P(),
+        P(),
+    )
+
+    def step(*args):
+        if kernels_fit(mesh, args[0], args[2], args[4], args[8]):
+            body = functools.partial(with_kernels, mesh.shape["mp"])
+        else:
+            body = on_device
+        return jax.shard_map(
+            body, mesh=mesh, in_specs=in_specs, out_specs=out_specs, check_vma=False
+        )(*args)
+
+    return step

time: 1180 us -> 470 us (0.40)
  waiting for transfers between devices: 890 us -> 0 us
  Pallas kernels: 0 us -> 420 us
  matrix products: 135 us -> 0 us
  blocking collectives: 44.7 us -> 0 us
  other arithmetic: 53.6 us -> 12.1 us
  between operations: 16.1 us -> 1.64 us
    reduce_scatter x11 -> x0, waiting for transfers between devices: 491 us -> none  [the longest x7 361 us: scatter_grad(): lax.psum_scatter(grad.astype(jnp.bfloat16), axis_name, scatter_dimension=...]
    pallas_call x0 -> x2, Pallas kernels: none -> 420 us  [the longest x1 221 us: backward_call(): pl.pallas_call(functools.partial(backward_kernel, n_mp), out_shape=[S((n_...]
    all_gather x11 -> x0, waiting for transfers between devices: 394 us -> none  [the longest x4 180 us: sum_parts(): lax.all_gather(own, axis_name, axis=0, tiled=True).astype(jnp.float32)]
    dot_general x27 -> x0, matrix products: 135 us -> none  [the longest x1 11.9 us: on_device(): d_act = jnp.dot(d_ffn, wd_back.T, preferred_element_type=jnp.float32)]
    psum x3 -> x0, blocking collectives: 44.7 us -> none  [the longest x1 23.1 us: on_device(): lax.psum((g_query_gain, g_key_gain, g_attn_gain, g_ffn_gain), 'dp')]
    convert_element_type x9 -> x2, other arithmetic: 21.1 us -> 0.74 us  [with_kernels(): (jnp.arange(rows, dtype=jnp.int32) < live_counts[0]).astype(F32)[:, None]]
    transpose x0 -> x9, local copies, waits for them, and re-layouts: none -> 15.9 us  [the longest x4 11.5 us: down(): jnp.transpose(units[first:first + count], (0, 2, 1))]
    reduce_sum x7 -> x2, other arithmetic: 14.9 us -> 0.97 us  [the longest x1 0.48 us: with_kernels(): inv_f = lax.rsqrt(jnp.mean(raw_f * raw_f, axis=1, keepdims=True) + EPS)]
  transfers between devices with their start and end apart: 22 -> 0, of which waited for: 20 -> 0; matrix products, arithmetic and copies ran while one was open for 10% -> 0% of each run, Pallas kernels for 0% -> 0%
where the time goes in v2:
time: 470 us; the launch traced here: 462 us
  Pallas kernels  420 us (89%)
  local copies, waits for them, and re-layouts  27.7 us (6%)
  other arithmetic  12.1 us (3%)
    pallas_call x1, Pallas kernels, backward_call(): pl.pallas_call(functools.partial(backward_kernel, n_mp), out_shape=[S((n_...  221 us
    pallas_call x1, Pallas kernels, forward_call(): pl.pallas_call(functools.partial(forward_kernel, n_mp), out_shape=[S(s, B...  199 us
    transpose x4, local copies, waits for them, and re-layouts, down(): jnp.transpose(units[first:first + count], (0, 2, 1))  11.5 us

profile of v2, /device:TPU:0, one launch (start us, length us, event | category | flops | bytes accessed | tf_op | source)
XLA Modules:
  0.0 461.7 jit_solution(14670899519590212879)
XLA Ops:
  0.7 0.9 compare_reduce_fusion
  1.5 0.1 add_select_fusion
  1.6 0.3 reduce-window.9
  2.0 0.1 slice_reduce_fusion
  2.1 0.1 fusion.10
  2.2 1.0 fusion.9
  3.2 1.0 pad_maximum_fusion
  4.2 0.9 copy.28.seg_col
  5.1 198.9 %shard_map.246 = (bf16[2048,512]{1,0:T(8,128)(2,1)}, bf16[2048,512]{1,0:T(8,128)(2,1)}, bf16[2048,512]{1,0:T(8,128)(2,1)}, bf16[512,2048]{1,0:T(8,128)(2,1)}, bf...) custom-call(bf16[512,2048]{1,0:T(8,128)(2,1)} %x_in.3, ...), custom_call_target="tpu_custom_call" | custom-call | tf_op jit(solution)/shard_map/pallas_call | solution.py:526
  204.6 0.7 fusion.8.mask
  205.3 221.4 %shard_map.247 = (f32[32,256,256]{2,1,0:T(8,128)}, bf16[512,2048]{1,0:T(8,128)(2,1)}, bf16[512,2048]{1,0:T(8,128)(2,1)}, f32[8,2048]{1,0:T(8,128)}) custom-call(bf16[2048,512]{1,0:T(8,128)(2,1)} %get-tuple-element.39.wq_in, bf16[2048,512]{1,0:T(8,128)(2,1)} %get-tuple-element.40.wk_in, bf16[2048,512]{1,0:T(8,128)(2,1)} %get-tuple-element.41.wv_in, ...), custom_call_target="tpu_custom_call" | custom-call | tf_op jit(solution)/shard_map/pallas_call | solution.py:910
  426.8 5.7 %slice_bitcast_fusion = (f32[8,256,256]{1,2,0:T(8,128)}, f32[256,8,256]{2,0,1:T(8,128)}, f32[256,8,256]{2,0,1:T(8,128)}) fusion(f32[32,256,256]{2,1,0:T(8,128)} %get-tuple-element.59), kind=kLoop, calls=%fused_computation.13 | loop fusion | bytes 12582912 | tf_op jit(solution)/shard_map/transpose | solution.py:1222
  432.4 1.9 copy.34
  434.4 1.8 copy.40
  436.2 1.9 copy.35
  438.1 1.8 copy.41
  439.9 3.0 copy.36
  443.0 0.5 fusion.6
  443.5 1.1 copy-done.1
  444.6 0.5 fusion
  445.1 0.1 copy-done
  445.2 7.1 %convert_add_fusion = (f32[512,2048]{1,0:T(8,128)}, bf16[512,2048]{1,0:T(8,128)(2,1)}) fusion(bf16[512,2048]{1,0:T(8,128)(2,1)} %get-tuple-element.58, bf16[512,2048]{1,0:T(8,128)(2,1)} %get-tuple-element.57, bf16[512,2048]{1,0:T(8,128)(2,1)} %cot_in.1, f32[512]{0:T(512)S(1)} %fusion.11, f32[2048]{0:T(1024)S(1)} %copy-done.5, f32[512]{0:T(512)S(1)} %add_rsqrt_fusion, ...), kind=kLoop, calls=%fused_computation.12 | loop fusion | flops 17825792 | bytes 18896896 | tf_op jit(solution)/shard_map/add | solution.py:1214
  452.2 1.7 slice_bitcast_fusion.3
  454.0 0.2 copy.30
  454.2 1.0 copy.37
  455.2 0.2 copy.31
  455.4 1.0 copy.38
  456.4 0.2 copy.32
  456.6 1.0 copy.39
  457.6 1.0 copy.33
  458.6 1.5 fusion.12
  460.1 1.4 fusion.13
  (16 shorter events, 0.2 us)
Async XLA Ops:
  0.6 3.6 copy-start.4
  439.9 3.0 copy-start.2
  443.0 1.6 copy-start.1
  443.0 2.2 copy-start
  443.0 2.2 copy-start.3
  443.0 2.2 copy-start.5

commit v3 on v1

--- a/solution.py
+++ b/solution.py
@@ -1,15 +1,993 @@
+import functools
 import math
 
 import jax
 import jax.numpy as jnp
 from jax import lax
+from jax.experimental import pallas as pl
+from jax.experimental.pallas import tpu as pltpu
 from jax.sharding import PartitionSpec as P
 
 HD = 128
-
-
 EPS = 1e-06
 THETA = 500000.0
+UNIT = 256
+BF = jnp.bfloat16
+F32 = jnp.float32
+
+
+def dot(a, b):
+    return jnp.dot(a, b, preferred_element_type=F32)
+
+
+def dot_nt(a, b):
+    return lax.dot_general(a, b, (((1,), (1,)), ((), ())), preferred_element_type=F32)
+
+
+def dot_tn(a, b):
+    return lax.dot_general(a, b, (((0,), (0,)), ((), ())), preferred_element_type=F32)
+
+
+def span(start, size):
+    return pl.ds(start if isinstance(start, int) else pl.multiple_of(start, size), size)
+
+
+def loop(count, body, first=0):
+    def step(at, carry):
+        body(at)
+        return carry
+
+    lax.fori_loop(first, first + count, step, 0)
+
+
+def remote(src, dst, send, recv, device):
+    return pltpu.make_async_remote_copy(
+        src_ref=src, dst_ref=dst, send_sem=send, recv_sem=recv,
+        device_id=device, device_id_type=pl.DeviceIdType.MESH,
+    )
+
+
+class Place:
+    def __init__(self, n_mp):
+        self.dp, self.z = lax.axis_index("dp"), lax.axis_index("mp")
+        self.n_mp, self.end = n_mp, n_mp - 1
+        self.c = lax.rem(self.dp, 2)
+        self.x = lax.rem(self.dp // 2, 2)
+        self.y = self.dp // 4
+        self.sib, self.xn, self.yn, self.dg = (self.block(i) for i in (1, 2, 4, 6))
+
+    def block(self, i):
+        i0, i1, i2 = i % 2, (i // 2) % 2, i // 4
+        c, x, y = (a + b - 2 * a * b for a, b in ((self.c, i0), (self.x, i1), (self.y, i2)))
+        return 4 * y + 2 * x + c
+
+    def barrier(self):
+        sem = pltpu.get_barrier_semaphore()
+        mesh = pl.DeviceIdType.MESH
+        for dp in (self.sib, self.xn, self.yn):
+            pl.semaphore_signal(sem, inc=1, device_id={"dp": dp}, device_id_type=mesh)
+        for step in range(1, self.n_mp):
+            z = lax.rem(self.z + step, self.n_mp)
+            pl.semaphore_signal(sem, inc=1, device_id={"mp": z}, device_id_type=mesh)
+        pl.semaphore_wait(sem, 3 + self.n_mp - 1)
+
+
+class Gather:
+    def __init__(self, place, src, full, by_rows, send, recv, local):
+        self.place, self.src, self.full, self.by_rows = place, src, full, by_rows
+        self.sends, self.recvs, self.local = send, recv, local
+        self.rows, self.cols = src.shape
+        self.half = self.rows // 2
+
+    def spot(self, owner, part=None):
+        first, count = (0, self.rows) if part is None else (part * self.half, self.half)
+        if self.by_rows:
+            start = pl.multiple_of(owner * self.rows + first, self.half)
+            return self.full.at[pl.ds(start, count), :]
+        return self.full.at[pl.ds(first, count), span(owner * self.cols, self.cols)]
+
+    def copies(self):
+        p = self.place
+        halves = [self.src.at[pl.ds(part * self.half, self.half), :] for part in range(2)]
+        return {
+            0: (halves[0], p.dp, 0, p.xn, p.xn),
+            1: (halves[1], p.dp, 1, p.xn, p.xn),
+            2: (halves[0], p.dp, 0, p.yn, p.yn),
+            3: (halves[1], p.dp, 1, p.yn, p.yn),
+            4: (self.spot(p.yn, 1), p.yn, 1, p.xn, p.dg),
+            5: (self.spot(p.xn, 0), p.xn, 0, p.yn, p.dg),
+            6: (self.src, p.dp, None, p.sib, p.sib),
+            7: (self.spot(p.xn), p.xn, None, p.sib, p.block(3)),
+            8: (self.spot(p.yn), p.yn, None, p.sib, p.block(5)),
+            9: (self.spot(p.dg), p.dg, None, p.sib, p.block(7)),
+        }
+
+    def copy(self, kind):
+        src, owner, part, target, _ = self.copies()[kind]
+        return remote(src, self.spot(owner, part), self.sends.at[kind], self.recvs.at[kind], {"dp": target})
+
+    def start(self, *kinds):
+        for kind in kinds:
+            self.copy(kind).start()
+
+    def arrived(self, *kinds):
+        for kind in kinds:
+            _, _, part, target, owner = self.copies()[kind]
+            spot = self.spot(owner, part)
+            remote(spot, spot, self.sends.at[kind], self.recvs.at[kind], {"dp": target}).wait_recv()
+
+    def own_copy(self):
+        return pltpu.make_async_copy(self.src, self.spot(self.place.dp), self.local)
+
+    def begin_a(self):
+        self.start(0, 3)
+
+    def begin_b(self):
+        self.start(1, 2, 6)
+        self.own_copy().start()
+
+    def relay(self):
+        self.arrived(0)
+        self.start(5)
+        self.arrived(3)
+        self.start(4)
+
+    def pass_on(self):
+        self.arrived(1)
+        self.start(7)
+        self.arrived(2)
+        self.start(8)
+
+    def last(self):
+        self.arrived(5, 4)
+        self.start(9)
+
+    def ready(self):
+        self.own_copy().wait()
+        self.arrived(6, 7, 8, 9)
+
+    def drain(self):
+        for kind in range(10):
+            self.copy(kind).wait_send()
+
+
+class RowSum:
+    def __init__(self, place, part, took, total, sems, chunk_at):
+        self.place, self.part, self.took, self.total, self.sems = place, part, took, total, sems
+        self.chunk_at = chunk_at
+        self.count, self.high, self.wide = took.shape[1:]
+        self.ticks = self.count + 2 * place.end
+
+    def spot(self, ref, flow, k):
+        half, bits = self.chunk_at(2 * k + flow)
+        return ref.at[span(half * self.high, self.high), span(self.place.block(bits) * self.wide, self.wide)]
+
+    def at(self, flow):
+        return self.place.z + flow * (self.place.end - 2 * self.place.z)
+
+    def forth(self, flow, k):
+        return remote(
+            self.spot(self.part, flow, k), self.took.at[flow, k],
+            self.sems.at[0, flow, k], self.sems.at[1, flow, k], {"mp": self.place.z + 1 - 2 * flow},
+        )
+
+    def back(self, flow, k):
+        spot = self.spot(self.total, flow, k)
+        return remote(spot, spot, self.sems.at[2, flow, k], self.sems.at[3, flow, k], {"mp": self.place.z - 1 + 2 * flow})
+
+    def begin(self, chunk):
+        flow, k = chunk % 2, chunk // 2
+
+        @pl.when(self.at(flow) == 0)
+        def _():
+            self.forth(flow, k).start()
+
+    def add(self, dst, flow, k):
+        mine, to = self.spot(self.part, flow, k), self.spot(dst, flow, k)
+        step = self.high // 4
+
+        def one(at):
+            near = span(at * step, step)
+            to[near, :] = (mine[near, :].astype(F32) + self.took[flow, k, near, :].astype(F32)).astype(BF)
+
+        loop(4, one)
+
+    def tick(self, t):
+        end = self.place.end
+        for flow in range(2):
+            at = self.at(flow)
+            k = t - at
+
+            @pl.when((at > 0) & (k >= 0) & (k < self.count))
+            def _():
+                self.forth(flow, k).wait_recv()
+
+                @pl.when(at < end)
+                def _():
+                    self.add(self.part, flow, k)
+                    self.forth(flow, k).start()
+
+                @pl.when(at == end)
+                def _():
+                    self.add(self.total, flow, k)
+                    self.back(flow, k).start()
+
+        for flow in range(2):
+            at = self.at(flow)
+            k = t - 2 * end + at
+
+            @pl.when((at < end) & (k >= 0) & (k < self.count))
+            def _():
+                self.back(flow, k).wait_recv()
+
+                @pl.when(at > 0)
+                def _():
+                    self.back(flow, k).start()
+
+    def drain(self):
+        for flow in range(2):
+            at = self.at(flow)
+
+            def one(k):
+                @pl.when(at < self.place.end)
+                def _():
+                    self.forth(flow, k).wait_send()
+
+                @pl.when(at > 0)
+                def _():
+                    self.back(flow, k).wait_send()
+
+            loop(self.count, one)
+
+
+class SmallSum:
+    def __init__(self, place, slots, sems):
+        self.place, self.slots, self.sems = place, slots, sems
+
+    def copy(self, step):
+        p = self.place
+        return remote(
+            self.slots.at[0], self.slots.at[step], self.sems.at[0, step], self.sems.at[1, step],
+            {"mp": lax.rem(p.z + step, p.n_mp)},
+        )
+
+    def begin(self):
+        for step in range(1, self.place.n_mp):
+            self.copy(step).start()
+
+    def end(self):
+        for step in range(1, self.place.n_mp):
+            self.copy(step).wait_recv()
+        total = self.slots[0]
+        for step in range(1, self.place.n_mp):
+            total = total + self.slots[step]
+        return total
+
+    def drain(self):
+        for step in range(1, self.place.n_mp):
+            self.copy(step).wait_send()
+
+
+class Scatter:
+    def __init__(self, place, pool, outs, sems, out_sems, count):
+        self.place, self.pool, self.outs, self.count = place, pool, outs, count
+        self.sems, self.out_sems = sems, out_sems
+        self.rows = pool[0].shape[0] // 8
+        self.half = self.rows // 2
+
+    def column(self, array, at, start, size):
+        return self.pool[array].at[span(start, size), pl.ds(at, UNIT)]
+
+    def give(self, u, chip=None):
+        first = (u % 2) * 4 * self.rows
+        if chip is None:
+            return self.column(0, 0, first, 4 * self.rows)
+        return self.column(0, 0, first + chip * self.rows, self.rows)
+
+    def got(self, u, chip=None):
+        s = u % 4
+        first, size = (s % 2) * 4 * self.rows, 4 * self.rows
+        if chip is not None:
+            first, size = first + chip * self.rows, self.rows
+        at = s // 2 * UNIT
+        return self.pool[1].at[span(first, size), pl.ds(at if isinstance(at, int) else pl.multiple_of(at, UNIT), UNIT)]
+
+    def sums(self, which, u, to, then=None):
+        first, size = (u % 4) * 2 * self.rows + to * self.rows, self.rows
+        if then is not None:
+            first, size = first + then * self.half, self.half
+        return self.column(2, which * UNIT, first, size)
+
+    def met(self, which, u):
+        return self.column(0, UNIT, which * 4 * self.rows + (u % 4) * self.rows, self.rows)
+
+    def ended(self, which, u):
+        return self.column(3, which * UNIT, (u % 4) * self.half, self.half)
+
+    def done(self, u):
+        return self.column(3, 2 * UNIT, (u % 2) * self.rows, self.rows)
+
+    def send(self, kind, u):
+        p, s = self.place, u % 4
+        src, dst, target = {
+            0: lambda: (self.give(u), self.got(u), p.sib),
+            1: lambda: (self.sums(0, u, 1 - p.x), self.met(0, u), p.xn),
+            2: lambda: (self.sums(1, u, 1 - p.y), self.met(1, u), p.yn),
+            3: lambda: (self.sums(0, u, p.x, 1 - p.y), self.ended(0, u), p.yn),
+            4: lambda: (self.sums(1, u, p.y, 1 - p.x), self.ended(1, u), p.xn),
+        }[kind]()
+        return remote(src, dst, self.sems.at[0, kind, s], self.sems.at[1, kind, s], {"dp": target})
+
+    def write(self, u, flipped):
+        flat, first = flipped
+        at = (u - first) * UNIT
+        if flat:
+            target = self.outs[0].at[span(at, UNIT), :]
+        else:
+            target = self.outs[1].at[:, span(at, UNIT)]
+        return pltpu.make_async_copy(self.done(u), target, self.out_sems.at[u % 2])
+
+    def product(self, u, turned, right, at):
+        p = self.place
+        cols = span(at * UNIT, UNIT)
+
+        def other(chip):
+            near = span((2 * chip + 1 - p.c) * self.rows, self.rows)
+            self.give(u, chip)[...] = dot(turned[near, :], right[:, cols]).astype(BF)
+
+        loop(4, other)
+        self.send(0, u).start()
+
+        def own(chip):
+            near = span((2 * chip + p.c) * self.rows, self.rows)
+            value = dot(turned[near, :], right[:, cols]).astype(BF)
+            y_to, x_to = chip // 2, chip % 2
+            self.sums(0, u, x_to, y_to)[...] = value[:self.half]
+            self.sums(1, u, y_to, x_to)[...] = value[self.half:]
+
+        loop(4, own)
+
+    def across(self, u):
+        self.send(0, u).wait_recv()
+        self.send(0, u).wait_send()
+
+        def add(chip):
+            y_to, x_to = chip // 2, chip % 2
+            more = self.got(u, chip)
+            for which, spot in ((0, self.sums(0, u, x_to, y_to)), (1, self.sums(1, u, y_to, x_to))):
+                near = slice(which * self.half, (which + 1) * self.half)
+                spot[...] = (spot[...].astype(F32) + more[near, :].astype(F32)).astype(BF)
+
+        loop(4, add)
+        self.send(1, u).start()
+        self.send(2, u).start()
+
+    def along(self, u):
+        p = self.place
+        for which, mine in ((0, p.x), (1, p.y)):
+            self.send(1 + which, u).wait_recv()
+            spot, more = self.sums(which, u, mine), self.met(which, u)
+            spot[...] = (spot[...].astype(F32) + more[...].astype(F32)).astype(BF)
+            self.send(3 + which, u).start()
+        for kind in (1, 2):
+            self.send(kind, u).wait_send()
+
+    def finish(self, u, flipped):
+        p = self.place
+        if not isinstance(u, int) or u >= 2:
+            pltpu.make_async_copy(self.done(u), self.done(u), self.out_sems.at[u % 2]).wait()
+        parts = []
+        for which, spot in ((0, self.sums(0, u, p.x, p.y)), (1, self.sums(1, u, p.y, p.x))):
+            self.send(3 + which, u).wait_recv()
+            parts.append(spot[...].astype(F32) + self.ended(which, u)[...].astype(F32))
+        value = jnp.concatenate(parts, axis=0)
+        self.done(u)[...] = (value.T if flipped[0] else value).astype(BF)
+        self.write(u, flipped).start()
+        for kind in (3, 4):
+            self.send(kind, u).wait_send()
+
+    def tick(self, u, flipped, turned=None, right=None, at=None):
+        has = lambda lag: not isinstance(u, int) or 0 <= u - lag < self.count
+        if right is not None:
+            self.product(u, turned, right, at)
+        if has(1):
+            self.across(u - 1)
+        if has(2):
+            self.along(u - 2)
+        if has(3):
+            self.finish(u - 3, flipped)
+
+    def drain(self):
+        for u in (self.count - 2, self.count - 1):
+            pltpu.make_async_copy(self.done(u), self.done(u), self.out_sems.at[u % 2]).wait()
+
+
+def as_row(col):
+    n = col.shape[0]
+    r = lax.broadcasted_iota(jnp.int32, (n, n), 0)
+    s = lax.broadcasted_iota(jnp.int32, (n, n), 1)
+    return jnp.sum(jnp.where(r == s, col, 0.0), axis=0, keepdims=True)
+
+
+def as_col(row):
+    n = row.shape[1]
+    r = lax.broadcasted_iota(jnp.int32, (n, n), 0)
+    s = lax.broadcasted_iota(jnp.int32, (n, n), 1)
+    return jnp.sum(jnp.where(r == s, row, 0.0), axis=1, keepdims=True)
+
+
+def turn(values, cos_tab, sin_tab):
+    return values * cos_tab + pltpu.roll(values, HD // 2, 1) * sin_tab
+
+
+def turn_back(grads, cos_tab, sin_tab):
+    return grads * cos_tab - pltpu.roll(grads, HD // 2, 1) * sin_tab
+
+
+def halves_in_turn(chunk):
+    return chunk // 8, chunk % 8
+
+
+def pairs_in_turn(chunk):
+    return (chunk // 2) % 2, 2 * (chunk // 4) + chunk % 2
+
+
+def layer_kernel(
+    n_mp,
+    x_in, cot_in, wq_in, wk_in, wv_in, wo_in, wg_in, wu_in, wd_in,
+    seg, live, freq, q_gain, k_gain, a_gain, f_gain,
+    wq_out, wk_out, wv_out, wo_out, hidden_out, grad_in_out, flat_out, tall_out, gains_out,
+    wq, wk, wv, wo, wg, wu, wd,
+    x, qp, kp, qr, kr, v, o, stat, cos_tab, sin_tab, side, raw_a, h, gate, up, act, d_ffn, cot, part, took,
+    turned, dk_sum, dv_sum, sums, gains, gains_got,
+    g_send, g_recv, g_local, row_sems, small, s_sems, s_out, gain_sems, io_sems,
+):
+    place = Place(n_mp)
+    rows, width = x.shape
+    local, ff = qp.shape[1], gate.shape[1]
+    heads = local // HD
+    scale = 1.0 / math.sqrt(HD)
+    half = rows // 2
+    n_ff = ff // UNIT
+    flying = {}
+
+    def move(name, src, dst):
+        copy = pltpu.make_async_copy(src, dst, io_sems.at[len(flying)])
+        flying[name] = copy
+        copy.start()
+
+    def need(*names):
+        for name in names:
+            flying[name].wait()
+
+    move("x", x_in, x)
+    place.barrier()
+    gq, gk, gv, go, gg, gu, gd = [
+        Gather(place, src, full, i not in (3, 6), g_send.at[i], g_recv.at[i], g_local.at[i])
+        for i, (src, full) in enumerate(
+            zip((wq_in, wk_in, wv_in, wo_in, wg_in, wu_in, wd_in), (wq, wk, wv, wo, wg, wu, wd))
+        )
+    ]
+    gq.begin_a()
+    gq.begin_b()
+    gk.begin_a()
+    gk.begin_b()
+    move("cot", cot_in, cot)
+    ids = seg[...].astype(F32)
+    ids_col = as_col(ids)
+    before = jnp.sum((ids < ids_col).astype(F32), axis=1, keepdims=True)
+    row_at = lax.broadcasted_iota(jnp.int32, (rows, 1), 0)
+    side[:, 0:1] = ids_col
+    side[:, 1:2] = (row_at < live[...]).astype(F32)
+    angles = (row_at.astype(F32) - before) * freq[...]
+    cos_tab[...] = jnp.cos(angles)
+    lane = lax.broadcasted_iota(jnp.int32, (rows, HD), 1)
+    sin_tab[...] = jnp.sin(angles) * jnp.where(lane < HD // 2, -1.0, 1.0)
+    gq.relay()
+    gv.begin_a()
+    gq.pass_on()
+    gv.begin_b()
+    gk.relay()
+    go.begin_a()
+    gk.pass_on()
+    go.begin_b()
+    gq.last()
+    need("x")
+    gq.ready()
+    move("wq", wq, wq_out)
+    row_sum = SmallSum(place, sums.at[0], small.at[0])
+
+    def project(full, dst, squares_to=None):
+        def one(r):
+            near = span(r * half, half)
+            value = dot(x[near, :], full[...])
+            dst[near, :] = value.astype(BF)
+            if squares_to is not None:
+                stat[near, squares_to:squares_to + 1] = jnp.sum(value * value, axis=1, keepdims=True)
+
+        loop(2, one)
+
+    sums[0, 0] = jnp.zeros(sums.shape[2:], F32)
+    project(wq, qp, heads)
+    sums[0, 0, 0:1, :] = as_row(stat[:, heads:heads + 1])
+    gv.relay()
+    gk.last()
+    gk.ready()
+    move("wk", wk, wk_out)
+    project(wk, kp, heads + 1)
+    sums[0, 0, 1:2, :] = as_row(stat[:, heads + 1:heads + 2])
+    row_sum.begin()
+    gv.pass_on()
+    go.relay()
+    gg.begin_a()
+    go.pass_on()
+    gg.begin_b()
+    gv.last()
+    gv.ready()
+    move("wv", wv, wv_out)
+    project(wv, v)
+    totals = row_sum.end()
+    inv_q = lax.rsqrt(as_col(totals[0:1, :]) / width + EPS)
+    inv_k = lax.rsqrt(as_col(totals[1:2, :]) / width + EPS)
+    stat[:, heads:heads + 1] = inv_q
+    stat[:, heads + 1:heads + 2] = inv_k
+
+    def rotate_head(hd):
+        cols = span(hd * HD, HD)
+        qr[:, cols] = turn(qp[:, cols].astype(F32) * inv_q * q_gain[:, cols], cos_tab[...], sin_tab[...]).astype(BF)
+        kr[:, cols] = turn(kp[:, cols].astype(F32) * inv_k * k_gain[:, cols], cos_tab[...], sin_tab[...]).astype(BF)
+
+    loop(heads, rotate_head)
+    block = rows // 4
+    lane_at = lax.broadcasted_iota(jnp.int32, (block, HD), 1)
+
+    def allowed_at(rb):
+        near, keys = slice(rb * block, (rb + 1) * block), (rb + 1) * block
+        t_at = lax.broadcasted_iota(jnp.int32, (block, keys), 0) + rb * block
+        s_at = lax.broadcasted_iota(jnp.int32, (block, keys), 1)
+        return near, keys, (side[near, 0:1] == seg[:, 0:keys].astype(F32)) & (s_at <= t_at)
+
+    def attend(rb):
+        near, keys, allowed = allowed_at(rb)
+
+        def one(hd):
+            cols = span(hd * HD, HD)
+            scores = jnp.where(allowed, dot_nt(qr[near, cols], kr[0:keys, cols]) * scale, -1e30)
+            top = jnp.max(scores, axis=1, keepdims=True)
+            weights = jnp.exp(scores - top)
+            norm = jnp.sum(weights, axis=1, keepdims=True)
+            stat[near, :] = jnp.where(lane_at == hd, top + jnp.log(norm), stat[near, :])
+            o[near, cols] = dot((weights / norm).astype(BF), v[0:keys, cols]).astype(BF)
+
+        loop(heads, one)
+
+    wide = width // 8
+
+    def columns(bits):
+        return span(place.block(bits) * wide, wide)
+
+    sum_attn = RowSum(place, part, took, raw_a, row_sems.at[0], halves_in_turn)
+
+    def project_out(r):
+        near = slice(r * half, (r + 1) * half)
+
+        def one(i):
+            part[near, columns(i)] = dot(o[near, :], wo[:, columns(i)]).astype(BF)
+            sum_attn.begin(r * 8 + i)
+
+        loop(8, one)
+
+    attend(0)
+    attend(1)
+    go.last()
+    go.ready()
+    move("wo", wo, wo_out)
+    project_out(0)
+    gu.begin_a()
+    attend(2)
+    sum_attn.tick(0)
+    attend(3)
+    project_out(1)
+    sum_attn.tick(1)
+    gg.relay()
+    gu.begin_b()
+    sum_attn.tick(2)
+    sum_attn.tick(3)
+    gg.pass_on()
+    sum_attn.tick(4)
+    sum_attn.tick(5)
+    gu.relay()
+    gd.begin_a()
+    sum_attn.tick(6)
+    sum_attn.tick(7)
+    gg.last()
+    gd.begin_b()
+    sum_attn.tick(8)
+    sum_attn.tick(9)
+
+    def mid(r):
+        tile = rows // 8
+
+        def one(at):
+            near = span(at * tile, tile)
+            raw = raw_a[near, :].astype(F32)
+            inv = lax.rsqrt(jnp.mean(raw * raw, axis=1, keepdims=True) + EPS)
+            h[near, :] = (x[near, :].astype(F32) + raw * inv * a_gain[...]).astype(BF)
+
+        loop(4, one, 4 * r)
+
+    def gate_half(r):
+        near = slice(r * half, (r + 1) * half)
+
+        def one(at):
+            cols = span(at * UNIT, UNIT)
+            gate[near, cols] = dot(h[near, :], wg[:, cols]).astype(BF)
+
+        loop(n_ff, one)
+
+    def up_half(r):
+        near = slice(r * half, (r + 1) * half)
+
+        def one(at):
+            cols = span(at * UNIT, UNIT)
+            value = dot(h[near, :], wu[:, cols])
+            up[near, cols] = value.astype(BF)
+            pre = gate[near, cols].astype(F32)
+            act[near, cols] = (pre * jax.nn.sigmoid(pre) * value).astype(BF)
+
+        loop(n_ff, one)
+
+    mid(0)
+    gg.ready()
+    sum_attn.tick(10)
+    gate_half(0)
+    gu.pass_on()
+    sum_attn.tick(11)
+    sum_attn.tick(12)
+    gu.last()
+    sum_attn.tick(13)
+    gu.ready()
+    up_half(0)
+    need("wq", "wk", "wv", "wo", "cot")
+    for g in (gq, gk, gv, go):
+        g.drain()
+    gd.relay()
+    sum_attn.drain()
+    sum_ffn = RowSum(place, part, took, d_ffn, row_sems.at[1], pairs_in_turn)
+
+    def project_down(pair):
+        r, bits = pair % 2, 2 * (pair // 2)
+        near = slice(r * half, (r + 1) * half)
+
+        def one(i):
+            part[near, columns(bits + i)] = dot(act[near, :], wd[:, columns(bits + i)]).astype(BF)
+            sum_ffn.begin(2 * pair + i)
+
+        loop(2, one)
+
+    gd.own_copy().wait()
+    gd.arrived(6)
+    project_down(0)
+    mid(1)
+    gate_half(1)
+    up_half(1)
+    sum_ffn.tick(0)
+    project_down(1)
+    sum_ffn.tick(1)
+    gd.pass_on()
+    gd.arrived(7)
+    project_down(2)
+    sum_ffn.tick(2)
+    project_down(3)
+    sum_ffn.tick(3)
+    gd.arrived(8)
+    project_down(4)
+    sum_ffn.tick(4)
+    gd.last()
+    project_down(5)
+    sum_ffn.tick(5)
+    gd.arrived(9)
+    project_down(6)
+    sum_ffn.tick(6)
+    project_down(7)
+    for tick in range(7, sum_ffn.ticks):
+        sum_ffn.tick(tick)
+    sum_ffn.drain()
+    for g in (gg, gu, gd):
+        g.drain()
+
+    gains[...] = jnp.zeros(gains.shape, F32)
+    tile = rows // 8
+
+    def back_ffn(at):
+        near = span(at * tile, tile)
+        raw = d_ffn[near, :].astype(F32)
+        alive = side[near, 1:2]
+        dy = alive * cot[near, :].astype(F32)
+        inv = lax.rsqrt(jnp.mean(raw * raw, axis=1, keepdims=True) + EPS)
+        normed = raw * inv
+        gains[0:1, :] += jnp.sum(dy * normed, axis=0, keepdims=True)
+        part[near, :] = (alive * (h[near, :].astype(F32) + normed * f_gain[...])).astype(BF)
+        gained = f_gain[...] * dy
+        mean = jnp.mean(gained * raw, axis=1, keepdims=True)
+        d_ffn[near, :] = (inv * gained - raw * inv**3 * mean).astype(BF)
+
+    loop(8, back_ffn)
+    move("hidden_out", part, hidden_out)
+
+    def flip(src):
+        def one(at):
+            near = span(at * UNIT, UNIT)
+            turned[near, :] = src[:, near].T
+
+        loop(width // UNIT, one)
+
+    flip(d_ffn)
+    scatter = Scatter(place, (wq, wk, wv, wo), (flat_out, tall_out), s_sems, s_out, (3 * ff + 4 * local) // UNIT)
+    flat, tall = (True, 0), (False, n_ff)
+
+    def back_act(r):
+        near = slice(r * half, (r + 1) * half)
+
+        def one(at):
+            cols = span(at * UNIT, UNIT)
+            d_act = dot_nt(d_ffn[near, :], wd[cols, :])
+            pre, upper = gate[near, cols].astype(F32), up[near, cols].astype(F32)
+            sig = jax.nn.sigmoid(pre)
+            up[near, cols] = (d_act * pre * sig).astype(BF)
+            gate[near, cols] = (d_act * upper * sig * (1.0 + pre * (1.0 - sig))).astype(BF)
+
+        loop(n_ff, one)
+
+    raw_h = x
+    sum_back = RowSum(place, part, took, raw_h, row_sems.at[2], halves_in_turn)
+
+    def back_gate(r, first):
+        near = slice(r * half, (r + 1) * half)
+
+        def one(i):
+            value = dot_nt(gate[near, :], wg[columns(i), :]) + dot_nt(up[near, :], wu[columns(i), :])
+            part[near, columns(i)] = value.astype(BF)
+            sum_back.begin(r * 8 + i)
+
+        loop(4, one, first)
+
+    scatter.tick(0, flat, turned, act, 0)
+    back_act(0)
+    scatter.tick(1, flat, turned, act, 1)
+    need("hidden_out")
+    back_gate(0, 0)
+    back_gate(0, 4)
+    scatter.tick(2, flat, turned, act, 2)
+    sum_back.tick(0)
+    back_act(1)
+    sum_back.tick(1)
+    scatter.tick(3, flat, turned, act, 3)
+    sum_back.tick(2)
+    back_gate(1, 0)
+    sum_back.tick(3)
+    back_gate(1, 4)
+    move("wq2", wq_out, wd.at[:, 0:local])
+    move("wk2", wk_out, wd.at[:, local:2 * local])
+    move("wv2", wv_out, wd.at[:, 2 * local:3 * local])
+    move("wo2", wo_out, wg.at[0:local, :])
+    move("x2", x_in, wu.at[0:rows, :])
+
+    def with_act(i):
+        sum_back.tick(4 + i)
+        scatter.tick(4 + i, flat, turned, act, 4 + i)
+
+    with_act(0)
+    loop(3, with_act, 1)
+    flip(h)
+    for i in range(3):
+        sum_back.tick(8 + i)
+        scatter.tick(8 + i, flat, turned, gate, i)
+    for i in range(3, 6):
+        sum_back.tick(8 + i)
+        scatter.tick(8 + i, tall, turned, gate, i)
+    sum_back.drain()
+    d_attn = wu.at[rows:2 * rows, :]
+
+    def back_attn(at):
+        near = span(at * tile, tile)
+        raw = raw_a[near, :].astype(F32)
+        dh = side[near, 1:2] * cot[near, :].astype(F32) + raw_h[near, :].astype(F32)
+        inv = lax.rsqrt(jnp.mean(raw * raw, axis=1, keepdims=True) + EPS)
+        gains[1:2, :] += jnp.sum(dh * raw * inv, axis=0, keepdims=True)
+        gained = a_gain[...] * dh
+        mean = jnp.mean(gained * raw, axis=1, keepdims=True)
+        d_attn[near, :] = (inv * gained - raw * inv**3 * mean).astype(BF)
+
+    loop(8, back_attn)
+    need("wo2")
+    scatter.tick(14, tall, turned, gate, 6)
+    d_heads = wu.at[2 * rows:3 * rows, 3 * local:4 * local]
+    d_heads[...] = dot_nt(d_attn[...], wg[0:local, :]).astype(BF)
+    scatter.tick(15, tall, turned, gate, 7)
+    dq, dk, dv = (wu.at[2 * rows:3 * rows, i * local:(i + 1) * local] for i in range(3))
+
+    def back_head(hd):
+        cols = span(hd * HD, HD)
+        dk_sum[...] = jnp.zeros(dk_sum.shape, F32)
+        dv_sum[...] = jnp.zeros(dv_sum.shape, F32)
+        for rb in range(4):
+            near, keys, allowed = allowed_at(rb)
+            lse = jnp.sum(jnp.where(lane_at == hd, stat[near, :], 0.0), axis=1, keepdims=True)
+            scores = jnp.where(allowed, dot_nt(qr[near, cols], kr[0:keys, cols]) * scale, -1e30)
+            probs = jnp.where(allowed, jnp.exp(scores - lse), 0.0)
+            grad = d_heads[near, cols]
+            d_prob = dot_nt(grad, v[0:keys, cols])
+            delta = jnp.sum(grad.astype(F32) * o[near, cols].astype(F32), axis=1, keepdims=True)
+            d_score = (probs * (d_prob - delta)).astype(BF)
+            back = dot(d_score, kr[0:keys, cols]) * scale
+            dq[near, cols] = turn_back(back, cos_tab[near, :], sin_tab[near, :]).astype(BF)
+            dk_sum[0:keys, :] += dot_tn(d_score, qr[near, cols])
+            dv_sum[0:keys, :] += dot_tn(probs.astype(BF), grad)
+        dk[:, cols] = turn_back(dk_sum[...] * scale, cos_tab[...], sin_tab[...]).astype(BF)
+        dv[:, cols] = dv_sum[...].astype(BF)
+
+    for hd in range(0, heads, 2):
+        loop(2, back_head, hd)
+        scatter.tick(16 + hd // 2, tall, turned, up, hd // 2)
+    row_sum_back = SmallSum(place, sums.at[1], small.at[1])
+    sums[1, 0] = jnp.zeros(sums.shape[2:], F32)
+    for at, (grad, raw, gain, lane_of) in enumerate(((dq, qp, q_gain, heads), (dk, kp, k_gain, heads + 1))):
+        both = grad[...].astype(F32) * raw[...].astype(F32)
+        gains[2 + at:3 + at, 0:local] = jnp.sum(both * stat[:, lane_of:lane_of + 1], axis=0, keepdims=True)
+        sums[1, 0, at:at + 1, :] = as_row(jnp.sum(gain[...] * both, axis=1, keepdims=True))
+    row_sum_back.begin()
+    scatter.tick(18, tall, turned, up, 2)
+    totals = row_sum_back.end()
+    for at, (grad, raw, gain, lane_of) in enumerate(((dq, qp, q_gain, heads), (dk, kp, k_gain, heads + 1))):
+        inv = stat[:, lane_of:lane_of + 1]
+        mean = as_col(totals[at:at + 1, :]) / width
+        gained = gain[...] * grad[...].astype(F32)
+        grad[...] = (inv * gained - raw[...].astype(F32) * inv**3 * mean).astype(BF)
+    need("wq2", "wk2", "wv2", "x2")
+    raw_x = d_ffn
+    sum_in = RowSum(place, part, took, raw_x, row_sems.at[3], halves_in_turn)
+
+    def back_in(r):
+        near = slice(r * half, (r + 1) * half)
+
+        def one(i):
+            spot = columns(i)
+            value = dot_nt(dq[near, :], wd[spot, 0:local]) + dot_nt(dk[near, :], wd[spot, local:2 * local])
+            part[near, spot] = (value + dot_nt(dv[near, :], wd[spot, 2 * local:3 * local])).astype(BF)
+            sum_in.begin(r * 8 + i)
+
+        loop(8, one)
+
+    back_in(0)
+    scatter.tick(19, tall, turned, up, 3)
+    back_in(1)
+
+    def with_up(i):
+        sum_in.tick(i)
+        scatter.tick(20 + i, tall, turned, up, 4 + i)
+
+    loop(4, with_up)
+    flip(d_attn)
+    for i in range(2):
+        sum_in.tick(4 + i)
+        scatter.tick(24 + i, tall, turned, o, i)
+    flip(wu.at[0:rows, :])
+    last = [(right, at) for right in (dq, dk, dv) for at in range(local // UNIT)]
+    partners = (place.sib, place.xn, place.yn)
+    n_units = scatter.count
+
+    def gain_copy(at):
+        return remote(
+            gains.at[pl.ds(8 * at, 8), :], gains_got.at[at], gain_sems.at[0, at], gain_sems.at[1, at],
+            {"dp": partners[at]},
+        )
+
+    def kind_of(u):
+        first_flat = 3 * n_ff
+        if u < n_ff:
+            return flat
+        if u < first_flat:
+            return tall
+        if u < first_flat + local // UNIT:
+            return (True, 2 * n_ff)
+        return (False, n_ff + local // UNIT)
+
+    gain_copy(0).start()
+    for i in range(n_units + 3 - 26):
+        u = 26 + i
+        if 6 + i < sum_in.ticks:
+            sum_in.tick(6 + i)
+        if last:
+            scatter.tick(u, kind_of(u - 3), turned, *last.pop(0))
+        else:
+            scatter.tick(u, kind_of(u - 3))
+        if i < 3:
+            gain_copy(i).wait_recv()
+            gains[8 * i + 8:8 * i + 16, :] = gains[8 * i:8 * i + 8, :] + gains_got[i]
+            if i < 2:
+                gain_copy(i + 1).start()
+    move("gains", gains.at[24:32, :], gains_out)
+    for tick in range(6 + n_units + 3 - 26, sum_in.ticks):
+        sum_in.tick(tick)
+
+    def end_tile(at):
+        near = span(at * tile, tile)
+        dh = side[near, 1:2] * cot[near, :].astype(F32) + raw_h[near, :].astype(F32)
+        raw_x[near, :] = (dh + raw_x[near, :].astype(F32)).astype(BF)
+
+    sum_in.drain()
+    loop(8, end_tile)
+    move("grad_in", raw_x, grad_in_out)
+    for at in range(3):
+        gain_copy(at).wait_send()
+    row_sum.drain()
+    row_sum_back.drain()
+    scatter.drain()
+    need("gains", "grad_in")
+
+
+def layer_call(n_mp, x, cot, weights, seg, live, freq, q_gain, k_gain, a_gain, f_gain):
+    rows, width = x.shape
+    local, ff = weights[0].shape[1], weights[4].shape[1]
+    high, half = width // 8, rows // 2
+    any_spec = pl.BlockSpec(memory_space=pl.ANY)
+    vmem = pl.BlockSpec(memory_space=pltpu.VMEM)
+    S, V, dma = jax.ShapeDtypeStruct, pltpu.VMEM, pltpu.SemaphoreType.DMA
+    fulls = [(width, local)] * 3 + [(local, width)] + [(width, ff)] * 2 + [(ff, width)]
+    outs = fulls[:4] + [
+        (rows, width), (rows, width), (ff + local, high), (high, 2 * ff + 3 * local),
+    ]
+    return pl.pallas_call(
+        functools.partial(layer_kernel, n_mp),
+        out_shape=[S(s, BF) for s in outs] + [S((8, width), F32)],
+        in_specs=[any_spec] * 9 + [vmem] * 7,
+        out_specs=[any_spec] * 9,
+        scratch_shapes=[V(s, BF) for s in fulls]
+        + [V((rows, width), BF)]
+        + [V((rows, local), BF)] * 6
+        + [V((rows, HD), F32)] * 4
+        + [V((rows, width), BF)] * 2
+        + [V((rows, ff), BF)] * 3
+        + [V((rows, width), BF)] * 3
+        + [V((2, 8, half, high), BF), V((width, rows), BF), V((rows, HD), F32), V((rows, HD), F32)]
+        + [V((2, n_mp, 8, rows), F32), V((32, width), F32), V((3, 8, width), F32)]
+        + [dma((7, 10)), dma((7, 10)), dma((7,)), dma((4, 4, 2, 8)), dma((2, 2, n_mp))]
+        + [dma((2, 5, 4)), dma((2,)), dma((2, 3)), dma((16,))],
+        compiler_params=pltpu.CompilerParams(
+            collective_id=0, has_side_effects=True, vmem_limit_bytes=67043328,
+        ),
+    )(x, cot, *weights, seg, live, freq, q_gain, k_gain, a_gain, f_gain)
+
+
+def with_kernel(n_mp, hidden_in, cotangent, segments, live_counts, *rest):
+    weights, (query_gain, key_gain, attn_gain, ffn_gain) = rest[:7], rest[7:]
+    local, ff = weights[0].shape[1], weights[4].shape[1]
+    inv_freq = THETA ** (-(jnp.arange(HD // 2, dtype=F32) * (2.0 / HD)))
+    freq = jnp.concatenate([inv_freq, inv_freq])[None]
+    _, _, _, _, hidden_out, grad_in, flat, tall, gains = layer_call(
+        n_mp, hidden_in, cotangent, weights, segments, live_counts[None], freq,
+        query_gain[None], key_gain[None], attn_gain[None], ffn_gain[None],
+    )
+
+    def piece(first, count):
+        return tall[:, first:first + count].astype(F32)
+
+    return (
+        hidden_out,
+        grad_in.astype(F32),
+        piece(2 * ff, local),
+        piece(2 * ff + local, local),
+        piece(2 * ff + 2 * local, local),
+        flat[ff:].astype(F32),
+        piece(0, ff),
+        piece(ff, ff),
+        flat[:ff].astype(F32),
+        gains[2, :local],
+        gains[3, :local],
+        gains[1],
+        gains[0],
+    )
 
 
 def doc_positions(seg_row):
@@ -270,41 +1248,56 @@
     )
 
 
+def kernel_fits(mesh, hidden_in, segments, w_query, w_gate):
+    n_dp, n_mp = mesh.shape["dp"], mesh.shape["mp"]
+    rows, width = hidden_in.shape[0] // n_dp, hidden_in.shape[1]
+    local, ff = w_query.shape[1] // n_mp, w_gate.shape[1] // n_mp
+    even = width % (8 * UNIT) == 0 and local % UNIT == 0 and ff % (2 * UNIT) == 0
+    fits = rows == UNIT * 2 and width == 8 * UNIT and local == rows and ff == width
+    return n_dp == 8 and n_mp >= 2 and even and fits
+
+
 def solution(mesh):
-    return jax.shard_map(
-        on_device,
-        mesh=mesh,
-        in_specs=(
-            P("dp", None),
-            P("dp", None),
-            P("dp", None),
-            P("dp"),
-            P("dp", "mp"),
-            P("dp", "mp"),
-            P("dp", "mp"),
-            P("mp", "dp"),
-            P("dp", "mp"),
-            P("dp", "mp"),
-            P("mp", "dp"),
-            P("mp"),
-            P("mp"),
-            P(),
-            P(),
-        ),
-        out_specs=(
-            P("dp", None),
-            P("dp", None),
-            P("dp", "mp"),
-            P("dp", "mp"),
-            P("dp", "mp"),
-            P("mp", "dp"),
-            P("dp", "mp"),
-            P("dp", "mp"),
-            P("mp", "dp"),
-            P("mp"),
-            P("mp"),
-            P(),
-            P(),
-        ),
-        check_vma=False,
-    )
+    in_specs = (
+        P("dp", None),
+        P("dp", None),
+        P("dp", None),
+        P("dp"),
+        P("dp", "mp"),
+        P("dp", "mp"),
+        P("dp", "mp"),
+        P("mp", "dp"),
+        P("dp", "mp"),
+        P("dp", "mp"),
+        P("mp", "dp"),
+        P("mp"),
+        P("mp"),
+        P(),
+        P(),
+    )
+    out_specs = (
+        P("dp", None),
+        P("dp", None),
+        P("dp", "mp"),
+        P("dp", "mp"),
+        P("dp", "mp"),
+        P("mp", "dp"),
+        P("dp", "mp"),
+        P("dp", "mp"),
+        P("mp", "dp"),
+        P("mp"),
+        P("mp"),
+        P(),
+        P(),
+    )
+
+    def step(*args):
+        if kernel_fits(mesh, args[0], args[2], args[4], args[8]):
+            body = functools.partial(with_kernel, mesh.shape["mp"])
+        else:
+            body = on_device
+        return jax.shard_map(
+            body, mesh=mesh, in_specs=in_specs, out_specs=out_specs, check_vma=False
+        )(*args)
+
+    return step

time: 1180 us -> 431 us (0.37)
  waiting for transfers between devices: 890 us -> 0 us
  Pallas kernels: 0 us -> 410 us
  matrix products: 135 us -> 0 us
  blocking collectives: 44.7 us -> 0 us
  other arithmetic: 53.6 us -> 11.4 us
  local copies, waits for them, and re-layouts: 25 us -> 4.33 us
  between operations: 16.1 us -> 1.54 us
    reduce_scatter x11 -> x0, waiting for transfers between devices: 491 us -> none  [the longest x7 361 us: scatter_grad(): lax.psum_scatter(grad.astype(jnp.bfloat16), axis_name, scatter_dimension=...]
    pallas_call x0 -> x1, Pallas kernels: none -> 410 us  [layer_call(): pl.pallas_call(functools.partial(layer_kernel, n_mp), out_shape=[S(s, BF)...]
    all_gather x11 -> x0, waiting for transfers between devices: 394 us -> none  [the longest x4 180 us: sum_parts(): lax.all_gather(own, axis_name, axis=0, tiled=True).astype(jnp.float32)]
    dot_general x27 -> x0, matrix products: 135 us -> none  [the longest x1 11.9 us: on_device(): d_act = jnp.dot(d_ffn, wd_back.T, preferred_element_type=jnp.float32)]
    psum x3 -> x0, blocking collectives: 44.7 us -> none  [the longest x1 23.1 us: on_device(): lax.psum((g_query_gain, g_key_gain, g_attn_gain, g_ffn_gain), 'dp')]
    unnamed x101 -> x7, local copies, waits for them, and re-layouts: 19.8 us -> 1.33 us
    reduce_sum x7 -> x0, other arithmetic: 14.9 us -> none  [the longest x1 4.43 us: on_device(): g_attn_gain = jnp.sum(dh * attn_raw * inv_a, axis=0)]
  transfers between devices with their start and end apart: 22 -> 0, of which waited for: 20 -> 0; matrix products, arithmetic and copies ran while one was open for 10% -> 0% of each run, Pallas kernels for 0% -> 0%
where the time goes in v3:
time: 431 us; the launch traced here: 427 us
  Pallas kernels  410 us (95%)
  other arithmetic  11.4 us (3%)
  local copies, waits for them, and re-layouts  4.33 us (1%)
    pallas_call x1, Pallas kernels, layer_call(): pl.pallas_call(functools.partial(layer_kernel, n_mp), out_shape=[S(s, BF)...  410 us

profile of v3, /device:TPU:0, one launch (start us, length us, event | category | flops | bytes accessed | tf_op | source)
XLA Modules:
  0.0 427.5 jit_solution(17748913449386881708)
XLA Ops:
  1.3 0.6 maximum_bitcast_fusion.freq
  1.9 410.2 %shard_map.246 = (bf16[2048,512]{1,0:T(8,128)(2,1)}, bf16[2048,512]{1,0:T(8,128)(2,1)}, bf16[2048,512]{1,0:T(8,128)(2,1)}, bf16[512,2048]{1,0:T(8,128)(2,1)}, bf...) custom-call(bf16[512,2048]{1,0:T(8,128)(2,1)} %x_in.1, ...), custom_call_target="tpu_custom_call" | custom-call | tf_op jit(solution)/shard_map/pallas_call | solution.py:941
  412.1 0.0 copy-start
  412.1 1.5 fusion.1
  413.6 1.5 fusion
  415.1 1.8 slice_convert_fusion.3
  416.9 2.7 slice_convert_fusion
  419.6 0.0 copy-done
  419.6 1.2 slice_convert_fusion.4
  420.8 0.0 copy-start.1
  420.8 2.6 slice_convert_fusion.1
  423.4 0.0 copy-done.1
  423.4 0.0 copy-start.2
  423.4 2.5 convert_element_type.24
  425.9 0.0 copy-done.2
  425.9 1.3 copy.30
  (1 shorter events, 0.0 us)
Async XLA Ops:
  412.1 7.5 %copy-start = (bf16[256,5632]{1,0:T(8,128)(2,1)S(1)}, bf16[256,5632]{1,0:T(8,128)(2,1)}, u32[]{:S(2)}) copy-start(bf16[256,5632]{1,0:T(8,128)(2,1)} %get-tuple-element.20) | copy-start | bytes 8650756
  420.8 2.6 copy-start.1
  423.4 2.5 copy-start.2

commit v4 on v3

--- a/solution.py
+++ b/solution.py
@@ -80,27 +80,33 @@
         self.half = self.rows // 2
 
     def spot(self, owner, part=None):
-        first, count = (0, self.rows) if part is None else (part * self.half, self.half)
-        if self.by_rows:
-            start = pl.multiple_of(owner * self.rows + first, self.half)
-            return self.full.at[pl.ds(start, count), :]
-        return self.full.at[pl.ds(first, count), span(owner * self.cols, self.cols)]
+        size = self.rows if self.by_rows else self.cols
+        first, count = (0, size) if part is None else (part * size // 2, size // 2)
+        near = pl.ds(pl.multiple_of(owner * size + first, size // 2), count)
+        return self.full.at[near, :] if self.by_rows else self.full.at[:, near]
+
+    def mine(self, part):
+        size = (self.rows if self.by_rows else self.cols) // 2
+        near = pl.ds(part * size, size)
+        return self.src.at[near, :] if self.by_rows else self.src.at[:, near]
 
     def copies(self):
         p = self.place
-        halves = [self.src.at[pl.ds(part * self.half, self.half), :] for part in range(2)]
-        return {
-            0: (halves[0], p.dp, 0, p.xn, p.xn),
-            1: (halves[1], p.dp, 1, p.xn, p.xn),
-            2: (halves[0], p.dp, 0, p.yn, p.yn),
-            3: (halves[1], p.dp, 1, p.yn, p.yn),
-            4: (self.spot(p.yn, 1), p.yn, 1, p.xn, p.dg),
-            5: (self.spot(p.xn, 0), p.xn, 0, p.yn, p.dg),
+        table = {
+            0: (self.mine(0), p.dp, 0, p.xn, p.xn),
+            1: (self.mine(1), p.dp, 1, p.xn, p.xn),
+            2: (self.mine(0), p.dp, 0, p.yn, p.yn),
+            3: (self.mine(1), p.dp, 1, p.yn, p.yn),
             6: (self.src, p.dp, None, p.sib, p.sib),
-            7: (self.spot(p.xn), p.xn, None, p.sib, p.block(3)),
-            8: (self.spot(p.yn), p.yn, None, p.sib, p.block(5)),
-            9: (self.spot(p.dg), p.dg, None, p.sib, p.block(7)),
         }
+        for kind, owner, part, target, arrives in (
+            (4, p.yn, 1, p.xn, p.dg), (5, p.xn, 0, p.yn, p.dg),
+            (7, p.xn, 0, p.sib, p.block(3)), (10, p.xn, 1, p.sib, p.block(3)),
+            (8, p.yn, 1, p.sib, p.block(5)), (11, p.yn, 0, p.sib, p.block(5)),
+            (9, p.dg, None, p.sib, p.block(7)),
+        ):
+            table[kind] = (self.spot(owner, part), owner, part, target, arrives)
+        return table
 
     def copy(self, kind):
         src, owner, part, target, _ = self.copies()[kind]
@@ -128,15 +134,15 @@
 
     def relay(self):
         self.arrived(0)
-        self.start(5)
+        self.start(5, 7)
         self.arrived(3)
-        self.start(4)
+        self.start(4, 8)
 
     def pass_on(self):
         self.arrived(1)
-        self.start(7)
+        self.start(10)
         self.arrived(2)
-        self.start(8)
+        self.start(11)
 
     def last(self):
         self.arrived(5, 4)
@@ -144,30 +150,28 @@
 
     def ready(self):
         self.own_copy().wait()
-        self.arrived(6, 7, 8, 9)
+        self.arrived(6, 7, 8, 9, 10, 11)
 
     def drain(self):
-        for kind in range(10):
+        for kind in range(12):
             self.copy(kind).wait_send()
 
 
 class RowSum:
-    def __init__(self, place, part, took, total, sems, chunk_at):
+    def __init__(self, place, part, took, total, sems, chunk_at, count):
         self.place, self.part, self.took, self.total, self.sems = place, part, took, total, sems
         self.chunk_at = chunk_at
-        self.count, self.high, self.wide = took.shape[1:]
-        self.ticks = self.count + 2 * place.end
+        self.count = count
 
     def spot(self, ref, flow, k):
-        half, bits = self.chunk_at(2 * k + flow)
-        return ref.at[span(half * self.high, self.high), span(self.place.block(bits) * self.wide, self.wide)]
+        return ref.at[self.chunk_at(flow, k)]
 
     def at(self, flow):
         return self.place.z + flow * (self.place.end - 2 * self.place.z)
 
     def forth(self, flow, k):
         return remote(
-            self.spot(self.part, flow, k), self.took.at[flow, k],
+            self.spot(self.part, flow, k), self.took(flow, k),
             self.sems.at[0, flow, k], self.sems.at[1, flow, k], {"mp": self.place.z + 1 - 2 * flow},
         )
 
@@ -175,56 +179,75 @@
         spot = self.spot(self.total, flow, k)
         return remote(spot, spot, self.sems.at[2, flow, k], self.sems.at[3, flow, k], {"mp": self.place.z - 1 + 2 * flow})
 
-    def begin(self, chunk):
-        flow, k = chunk % 2, chunk // 2
-
-        @pl.when(self.at(flow) == 0)
-        def _():
-            self.forth(flow, k).start()
+    def push(self, k):
+        if isinstance(k, int) and k >= self.count:
+            return
+
+        def one(flow):
+            @pl.when((self.at(flow) == 0) & (k < self.count))
+            def _():
+                self.forth(flow, k).start()
+
+        loop(2, one)
 
     def add(self, dst, flow, k):
-        mine, to = self.spot(self.part, flow, k), self.spot(dst, flow, k)
-        step = self.high // 4
+        mine, to, more = self.spot(self.part, flow, k), self.spot(dst, flow, k), self.took(flow, k)
+        step = mine.shape[0] // 4
 
         def one(at):
             near = span(at * step, step)
-            to[near, :] = (mine[near, :].astype(F32) + self.took[flow, k, near, :].astype(F32)).astype(BF)
+            to[near, :] = (mine[near, :].astype(F32) + more[near, :].astype(F32)).astype(BF)
 
         loop(4, one)
 
-    def tick(self, t):
-        end = self.place.end
-        for flow in range(2):
+    def tick(self, t, half):
+        end, count = self.place.end, self.count // 2
+        if isinstance(t, int) and t >= count + 2 * end:
+            return
+
+        def gather(flow):
             at = self.at(flow)
             k = t - at
 
-            @pl.when((at > 0) & (k >= 0) & (k < self.count))
+            @pl.when((at > 0) & (k >= 0) & (k < count))
             def _():
-                self.forth(flow, k).wait_recv()
+                chunk = half * count + k
+                self.forth(flow, chunk).wait_recv()
 
                 @pl.when(at < end)
                 def _():
-                    self.add(self.part, flow, k)
-                    self.forth(flow, k).start()
+                    self.add(self.part, flow, chunk)
+                    self.forth(flow, chunk).start()
 
                 @pl.when(at == end)
                 def _():
-                    self.add(self.total, flow, k)
-                    self.back(flow, k).start()
-
-        for flow in range(2):
+                    self.add(self.total, flow, chunk)
+                    self.back(flow, chunk).start()
+
+        def bring_back(flow):
             at = self.at(flow)
             k = t - 2 * end + at
 
-            @pl.when((at < end) & (k >= 0) & (k < self.count))
+            @pl.when((at < end) & (k >= 0) & (k < count))
             def _():
-                self.back(flow, k).wait_recv()
+                chunk = half * count + k
+                self.back(flow, chunk).wait_recv()
 
                 @pl.when(at > 0)
                 def _():
-                    self.back(flow, k).start()
-
-    def drain(self):
+                    self.back(flow, chunk).start()
+
+        if not isinstance(t, int) or t < count + end:
+            loop(2, gather)
+        if not isinstance(t, int) or t >= end + 1:
+            loop(2, bring_back)
+
+    def both(self, t, lag):
+        self.tick(t, 0)
+        self.tick(t - lag, 1)
+
+    def sent(self, half=None):
+        first, count = (0, self.count) if half is None else (half * self.count // 2, self.count // 2)
         for flow in range(2):
             at = self.at(flow)
 
@@ -237,7 +260,7 @@
                 def _():
                     self.back(flow, k).wait_send()
 
-            loop(self.count, one)
+            loop(count, one, first)
 
 
 class SmallSum:
@@ -269,8 +292,10 @@
 
 
 class Scatter:
-    def __init__(self, place, pool, outs, sems, out_sems, count):
-        self.place, self.pool, self.outs, self.count = place, pool, outs, count
+    def __init__(self, place, pool, outs, sems, out_sems, n_ff, n_local):
+        self.place, self.pool, self.outs = place, pool, outs
+        self.n_ff, self.n_local, self.early = n_ff, n_local, 3 * n_ff
+        self.count = 3 * n_ff + 4 * n_local
         self.sems, self.out_sems = sems, out_sems
         self.rows = pool[0].shape[0] // 8
         self.half = self.rows // 2
@@ -278,19 +303,15 @@
     def column(self, array, at, start, size):
         return self.pool[array].at[span(start, size), pl.ds(at, UNIT)]
 
-    def give(self, u, chip=None):
-        first = (u % 2) * 4 * self.rows
-        if chip is None:
-            return self.column(0, 0, first, 4 * self.rows)
-        return self.column(0, 0, first + chip * self.rows, self.rows)
+    def made(self, u, own):
+        return self.pool[0].at[span((u % 2) * 4 * self.rows, 4 * self.rows), span(own * UNIT, UNIT)]
 
     def got(self, u, chip=None):
         s = u % 4
         first, size = (s % 2) * 4 * self.rows, 4 * self.rows
         if chip is not None:
             first, size = first + chip * self.rows, self.rows
-        at = s // 2 * UNIT
-        return self.pool[1].at[span(first, size), pl.ds(at if isinstance(at, int) else pl.multiple_of(at, UNIT), UNIT)]
+        return self.pool[1].at[span(first, size), span(s // 2 * UNIT, UNIT)]
 
     def sums(self, which, u, to, then=None):
         first, size = (u % 4) * 2 * self.rows + to * self.rows, self.rows
@@ -299,7 +320,7 @@
         return self.column(2, which * UNIT, first, size)
 
     def met(self, which, u):
-        return self.column(0, UNIT, which * 4 * self.rows + (u % 4) * self.rows, self.rows)
+        return self.pool[3].at[span((u % 2) * self.rows, self.rows), span((3 + 2 * which + u % 4 // 2) * UNIT, UNIT)]
 
     def ended(self, which, u):
         return self.column(3, which * UNIT, (u % 4) * self.half, self.half)
@@ -310,7 +331,7 @@
     def send(self, kind, u):
         p, s = self.place, u % 4
         src, dst, target = {
-            0: lambda: (self.give(u), self.got(u), p.sib),
+            0: lambda: (self.made(u, 0), self.got(u), p.sib),
             1: lambda: (self.sums(0, u, 1 - p.x), self.met(0, u), p.xn),
             2: lambda: (self.sums(1, u, 1 - p.y), self.met(1, u), p.yn),
             3: lambda: (self.sums(0, u, p.x, 1 - p.y), self.ended(0, u), p.yn),
@@ -318,45 +339,31 @@
         }[kind]()
         return remote(src, dst, self.sems.at[0, kind, s], self.sems.at[1, kind, s], {"dp": target})
 
-    def write(self, u, flipped):
-        flat, first = flipped
-        at = (u - first) * UNIT
-        if flat:
-            target = self.outs[0].at[span(at, UNIT), :]
-        else:
-            target = self.outs[1].at[:, span(at, UNIT)]
-        return pltpu.make_async_copy(self.done(u), target, self.out_sems.at[u % 2])
-
     def product(self, u, turned, right, at):
-        p = self.place
         cols = span(at * UNIT, UNIT)
 
-        def other(chip):
-            near = span((2 * chip + 1 - p.c) * self.rows, self.rows)
-            self.give(u, chip)[...] = dot(turned[near, :], right[:, cols]).astype(BF)
-
-        loop(4, other)
-        self.send(0, u).start()
-
-        def own(chip):
-            near = span((2 * chip + p.c) * self.rows, self.rows)
-            value = dot(turned[near, :], right[:, cols]).astype(BF)
-            y_to, x_to = chip // 2, chip % 2
-            self.sums(0, u, x_to, y_to)[...] = value[:self.half]
-            self.sums(1, u, y_to, x_to)[...] = value[self.half:]
-
-        loop(4, own)
+        def one(own):
+            near = span(own * 4 * self.rows, 4 * self.rows)
+            self.made(u, own)[...] = dot(turned[near, :], right[:, cols]).astype(BF)
+
+            @pl.when(own == 0)
+            def _():
+                self.send(0, u).start()
+
+        loop(2, one)
 
     def across(self, u):
         self.send(0, u).wait_recv()
         self.send(0, u).wait_send()
+        mine = self.made(u, 1)
 
         def add(chip):
             y_to, x_to = chip // 2, chip % 2
             more = self.got(u, chip)
             for which, spot in ((0, self.sums(0, u, x_to, y_to)), (1, self.sums(1, u, y_to, x_to))):
                 near = slice(which * self.half, (which + 1) * self.half)
-                spot[...] = (spot[...].astype(F32) + more[near, :].astype(F32)).astype(BF)
+                own = mine[span(chip * self.rows + which * self.half, self.half), :]
+                spot[...] = (own.astype(F32) + more[near, :].astype(F32)).astype(BF)
 
         loop(4, add)
         self.send(1, u).start()
@@ -372,34 +379,56 @@
         for kind in (1, 2):
             self.send(kind, u).wait_send()
 
-    def finish(self, u, flipped):
+    def wait_write(self, u):
+        pltpu.make_async_copy(self.done(u), self.done(u), self.out_sems.at[u % 2]).wait()
+
+    def finish(self, u):
         p = self.place
-        if not isinstance(u, int) or u >= 2:
-            pltpu.make_async_copy(self.done(u), self.done(u), self.out_sems.at[u % 2]).wait()
+
+        @pl.when(u >= 2)
+        def _():
+            self.wait_write(u)
+
         parts = []
         for which, spot in ((0, self.sums(0, u, p.x, p.y)), (1, self.sums(1, u, p.y, p.x))):
             self.send(3 + which, u).wait_recv()
             parts.append(spot[...].astype(F32) + self.ended(which, u)[...].astype(F32))
         value = jnp.concatenate(parts, axis=0)
-        self.done(u)[...] = (value.T if flipped[0] else value).astype(BF)
-        self.write(u, flipped).start()
+        late = u // self.early
+        flat = (u < self.n_ff) | ((u >= self.early) & (u < self.early + self.n_local))
+
+        @pl.when(flat)
+        def _():
+            self.done(u)[...] = value.T.astype(BF)
+            target = self.outs[0].at[span((u - late * 2 * self.n_ff) * UNIT, UNIT), :]
+            pltpu.make_async_copy(self.done(u), target, self.out_sems.at[u % 2]).start()
+
+        @pl.when(jnp.logical_not(flat))
+        def _():
+            self.done(u)[...] = value.astype(BF)
+            target = self.outs[1].at[:, span((u - self.n_ff - late * self.n_local) * UNIT, UNIT)]
+            pltpu.make_async_copy(self.done(u), target, self.out_sems.at[u % 2]).start()
+
         for kind in (3, 4):
             self.send(kind, u).wait_send()
 
-    def tick(self, u, flipped, turned=None, right=None, at=None):
-        has = lambda lag: not isinstance(u, int) or 0 <= u - lag < self.count
-        if right is not None:
-            self.product(u, turned, right, at)
-        if has(1):
-            self.across(u - 1)
-        if has(2):
-            self.along(u - 2)
-        if has(3):
-            self.finish(u - 3, flipped)
+    def tick(self, u, turned, ffs, others):
+        @pl.when(u < self.early)
+        def _():
+            self.product(u, turned, ffs.at[u // self.n_ff], u % self.n_ff)
+
+        @pl.when((u >= self.early) & (u < self.count))
+        def _():
+            self.product(u, turned, others, u - self.early)
+
+        for lag, stage in ((1, self.across), (2, self.along), (3, self.finish)):
+            @pl.when((u >= lag) & (u < self.count + lag))
+            def _():
+                stage(u - lag)
 
     def drain(self):
         for u in (self.count - 2, self.count - 1):
-            pltpu.make_async_copy(self.done(u), self.done(u), self.out_sems.at[u % 2]).wait()
+            self.wait_write(u)
 
 
 def as_row(col):
@@ -422,14 +451,6 @@
 
 def turn_back(grads, cos_tab, sin_tab):
     return grads * cos_tab - pltpu.roll(grads, HD // 2, 1) * sin_tab
-
-
-def halves_in_turn(chunk):
-    return chunk // 8, chunk % 8
-
-
-def pairs_in_turn(chunk):
-    return (chunk // 2) % 2, 2 * (chunk // 4) + chunk % 2
 
 
 def layer_kernel(
@@ -438,27 +459,28 @@
     seg, live, freq, q_gain, k_gain, a_gain, f_gain,
     wq_out, wk_out, wv_out, wo_out, hidden_out, grad_in_out, flat_out, tall_out, gains_out,
     wq, wk, wv, wo, wg, wu, wd,
-    x, qp, kp, qr, kr, v, o, stat, cos_tab, sin_tab, side, raw_a, h, gate, up, act, d_ffn, cot, part, took,
+    x, qp, kp, qr, kr, v, o, stat, cos_tab, sin_tab, side, raw_a, h, ffs, d_ffn, cot, part, took,
     turned, dk_sum, dv_sum, sums, gains, gains_got,
     g_send, g_recv, g_local, row_sems, small, s_sems, s_out, gain_sems, io_sems,
 ):
     place = Place(n_mp)
     rows, width = x.shape
-    local, ff = qp.shape[1], gate.shape[1]
+    local, ff = qp.shape[1], ffs.shape[2]
+    act, gate, up = (ffs.at[i] for i in range(3))
     heads = local // HD
     scale = 1.0 / math.sqrt(HD)
     half = rows // 2
-    n_ff = ff // UNIT
+    n_ff, n_local = ff // UNIT, local // UNIT
     flying = {}
 
     def move(name, src, dst):
-        copy = pltpu.make_async_copy(src, dst, io_sems.at[len(flying)])
-        flying[name] = copy
-        copy.start()
+        at = len(flying)
+        flying[name] = lambda: pltpu.make_async_copy(src, dst, io_sems.at[at])
+        flying[name]().start()
 
     def need(*names):
         for name in names:
-            flying[name].wait()
+            flying[name]().wait()
 
     move("x", x_in, x)
     place.barrier()
@@ -490,7 +512,6 @@
     gk.relay()
     go.begin_a()
     gk.pass_on()
-    go.begin_b()
     gq.last()
     need("x")
     gq.ready()
@@ -511,21 +532,22 @@
     project(wq, qp, heads)
     sums[0, 0, 0:1, :] = as_row(stat[:, heads:heads + 1])
     gv.relay()
+    go.begin_b()
+    gv.pass_on()
     gk.last()
     gk.ready()
     move("wk", wk, wk_out)
     project(wk, kp, heads + 1)
     sums[0, 0, 1:2, :] = as_row(stat[:, heads + 1:heads + 2])
     row_sum.begin()
-    gv.pass_on()
     go.relay()
     gg.begin_a()
-    go.pass_on()
-    gg.begin_b()
     gv.last()
     gv.ready()
     move("wv", wv, wv_out)
     project(wv, v)
+    go.pass_on()
+    gg.begin_b()
     totals = row_sum.end()
     inv_q = lax.rsqrt(as_col(totals[0:1, :]) / width + EPS)
     inv_k = lax.rsqrt(as_col(totals[1:2, :]) / width + EPS)
@@ -538,6 +560,7 @@
         kr[:, cols] = turn(kp[:, cols].astype(F32) * inv_k * k_gain[:, cols], cos_tab[...], sin_tab[...]).astype(BF)
 
     loop(heads, rotate_head)
+    go.last()
     block = rows // 4
     lane_at = lax.broadcasted_iota(jnp.int32, (block, HD), 1)
 
@@ -566,44 +589,21 @@
     def columns(bits):
         return span(place.block(bits) * wide, wide)
 
-    sum_attn = RowSum(place, part, took, raw_a, row_sems.at[0], halves_in_turn)
+    def by_rows(flow, k):
+        return span(k // 4 * half, half), columns(2 * (k % 4) + flow)
+
+    def took_slot(flow, k):
+        return took.at[flow, k]
+
+    sum_attn = RowSum(place, part, took_slot, raw_a, row_sems.at[0], by_rows, 8)
 
     def project_out(r):
         near = slice(r * half, (r + 1) * half)
 
         def one(i):
             part[near, columns(i)] = dot(o[near, :], wo[:, columns(i)]).astype(BF)
-            sum_attn.begin(r * 8 + i)
 
         loop(8, one)
-
-    attend(0)
-    attend(1)
-    go.last()
-    go.ready()
-    move("wo", wo, wo_out)
-    project_out(0)
-    gu.begin_a()
-    attend(2)
-    sum_attn.tick(0)
-    attend(3)
-    project_out(1)
-    sum_attn.tick(1)
-    gg.relay()
-    gu.begin_b()
-    sum_attn.tick(2)
-    sum_attn.tick(3)
-    gg.pass_on()
-    sum_attn.tick(4)
-    sum_attn.tick(5)
-    gu.relay()
-    gd.begin_a()
-    sum_attn.tick(6)
-    sum_attn.tick(7)
-    gg.last()
-    gd.begin_b()
-    sum_attn.tick(8)
-    sum_attn.tick(9)
 
     def mid(r):
         tile = rows // 8
@@ -616,16 +616,16 @@
 
         loop(4, one, 4 * r)
 
-    def gate_half(r):
+    def gate_part(r, first, count):
         near = slice(r * half, (r + 1) * half)
 
         def one(at):
             cols = span(at * UNIT, UNIT)
             gate[near, cols] = dot(h[near, :], wg[:, cols]).astype(BF)
 
-        loop(n_ff, one)
-
-    def up_half(r):
+        loop(count, one, first)
+
+    def up_half(r, first, count):
         near = slice(r * half, (r + 1) * half)
 
         def one(at):
@@ -635,66 +635,103 @@
             pre = gate[near, cols].astype(F32)
             act[near, cols] = (pre * jax.nn.sigmoid(pre) * value).astype(BF)
 
-        loop(n_ff, one)
-
+        loop(count, one, first)
+
+    attend(0)
+    attend(1)
+    go.ready()
+    move("wo", wo, wo_out)
+    project_out(0)
+    sum_attn.push(0)
+    sum_attn.push(1)
+    gu.begin_a()
+    attend(2)
+    sum_attn.tick(1, 0)
+    sum_attn.push(2)
+    attend(3)
+    sum_attn.tick(2, 0)
+    sum_attn.push(3)
+    project_out(1)
+    gg.relay()
+    gu.begin_b()
+    sum_attn.push(4)
+    sum_attn.tick(3, 0)
+    gg.pass_on()
+
+    def attn_both(t):
+        sum_attn.push(t + 1)
+        sum_attn.both(t, 3)
+
+    attn_both(4)
+    attn_both(5)
+    gu.relay()
+    gd.begin_a()
+    loop(2, attn_both, 6)
+    gg.last()
+    gd.begin_b()
+    loop(2, attn_both, 8)
+    gg.ready()
     mid(0)
-    gg.ready()
-    sum_attn.tick(10)
-    gate_half(0)
+
+    def gate_and_tick(i):
+        gate_part(0, i * (n_ff // 2), n_ff // 2)
+        sum_attn.tick(7 + i, 1)
+
+    loop(2, gate_and_tick)
     gu.pass_on()
-    sum_attn.tick(11)
-    sum_attn.tick(12)
+    sum_attn.tick(9, 1)
+    mid(1)
+    gate_part(1, 0, n_ff)
     gu.last()
-    sum_attn.tick(13)
     gu.ready()
-    up_half(0)
-    need("wq", "wk", "wv", "wo", "cot")
-    for g in (gq, gk, gv, go):
-        g.drain()
-    gd.relay()
-    sum_attn.drain()
-    sum_ffn = RowSum(place, part, took, d_ffn, row_sems.at[1], pairs_in_turn)
-
-    def project_down(pair):
-        r, bits = pair % 2, 2 * (pair // 2)
-        near = slice(r * half, (r + 1) * half)
-
-        def one(i):
-            part[near, columns(bits + i)] = dot(act[near, :], wd[:, columns(bits + i)]).astype(BF)
-            sum_ffn.begin(2 * pair + i)
+    up_half(0, 0, n_ff)
+    sum_attn.sent()
+    sum_ffn = RowSum(place, part, took_slot, d_ffn, row_sems.at[1], by_rows, 8)
+
+    def project_down(k):
+        near = span(k // 4 * half, half)
+
+        def one(flow):
+            cols = columns(2 * (k % 4) + flow)
+            part[near, cols] = dot(act[near, :], wd[:, cols]).astype(BF)
 
         loop(2, one)
+        sum_ffn.push(k)
 
     gd.own_copy().wait()
     gd.arrived(6)
     project_down(0)
-    mid(1)
-    gate_half(1)
-    up_half(1)
-    sum_ffn.tick(0)
+    need("wq", "wk", "wv", "wo")
+    for g in (gq, gk, gv, go):
+        g.drain()
+    up_half(1, 0, n_ff // 2)
+    gd.relay()
+    sum_ffn.tick(1, 0)
+    up_half(1, n_ff // 2, n_ff // 2)
+    project_down(4)
+    gd.pass_on()
+    gd.arrived(7, 8, 10, 11)
     project_down(1)
-    sum_ffn.tick(1)
-    gd.pass_on()
-    gd.arrived(7)
+    sum_ffn.both(2, 1)
     project_down(2)
-    sum_ffn.tick(2)
+    project_down(5)
+    sum_ffn.both(3, 1)
+    project_down(6)
+    gd.last()
+    gd.arrived(9)
     project_down(3)
-    sum_ffn.tick(3)
-    gd.arrived(8)
-    project_down(4)
-    sum_ffn.tick(4)
-    gd.last()
-    project_down(5)
-    sum_ffn.tick(5)
-    gd.arrived(9)
-    project_down(6)
-    sum_ffn.tick(6)
+    sum_ffn.tick(4, 0)
     project_down(7)
-    for tick in range(7, sum_ffn.ticks):
-        sum_ffn.tick(tick)
-    sum_ffn.drain()
+    sum_ffn.tick(3, 1)
+
+    def ffn_both(t):
+        sum_ffn.both(t, 1)
+
+    loop(5, ffn_both, 5)
+    sum_ffn.sent(0)
     for g in (gg, gu, gd):
         g.drain()
+    need("cot")
 
     gains[...] = jnp.zeros(gains.shape, F32)
     tile = rows // 8
@@ -707,26 +744,24 @@
         inv = lax.rsqrt(jnp.mean(raw * raw, axis=1, keepdims=True) + EPS)
         normed = raw * inv
         gains[0:1, :] += jnp.sum(dy * normed, axis=0, keepdims=True)
-        part[near, :] = (alive * (h[near, :].astype(F32) + normed * f_gain[...])).astype(BF)
+        value = (alive * (h[near, :].astype(F32) + normed * f_gain[...])).astype(BF)
+        for q in range(width // local):
+            wv[span(q * rows + at * tile, tile), :] = value[:, q * local:(q + 1) * local]
         gained = f_gain[...] * dy
         mean = jnp.mean(gained * raw, axis=1, keepdims=True)
         d_ffn[near, :] = (inv * gained - raw * inv**3 * mean).astype(BF)
 
-    loop(8, back_ffn)
-    move("hidden_out", part, hidden_out)
-
     def flip(src):
         def one(at):
-            near = span(at * UNIT, UNIT)
-            turned[near, :] = src[:, near].T
-
-        loop(width // UNIT, one)
-
-    flip(d_ffn)
-    scatter = Scatter(place, (wq, wk, wv, wo), (flat_out, tall_out), s_sems, s_out, (3 * ff + 4 * local) // UNIT)
-    flat, tall = (True, 0), (False, n_ff)
-
-    def back_act(r):
+            parity = at % 2
+            own = 1 - (parity + place.c - 2 * parity * place.c)
+            turned[span((4 * own + at // 2) * wide, wide), :] = src[:, span(at * wide, wide)].T
+
+        loop(8, one)
+
+    scatter = Scatter(place, (wq, wk, wv, wo), (flat_out, tall_out), s_sems, s_out, n_ff, n_local)
+
+    def back_act(r, first, count):
         near = slice(r * half, (r + 1) * half)
 
         def one(at):
@@ -737,10 +772,10 @@
             up[near, cols] = (d_act * pre * sig).astype(BF)
             gate[near, cols] = (d_act * upper * sig * (1.0 + pre * (1.0 - sig))).astype(BF)
 
-        loop(n_ff, one)
+        loop(count, one, first)
 
     raw_h = x
-    sum_back = RowSum(place, part, took, raw_h, row_sems.at[2], halves_in_turn)
+    sum_back = RowSum(place, part, took_slot, raw_h, row_sems.at[2], by_rows, 8)
 
     def back_gate(r, first):
         near = slice(r * half, (r + 1) * half)
@@ -748,45 +783,23 @@
         def one(i):
             value = dot_nt(gate[near, :], wg[columns(i), :]) + dot_nt(up[near, :], wu[columns(i), :])
             part[near, columns(i)] = value.astype(BF)
-            sum_back.begin(r * 8 + i)
 
         loop(4, one, first)
 
-    scatter.tick(0, flat, turned, act, 0)
-    back_act(0)
-    scatter.tick(1, flat, turned, act, 1)
-    need("hidden_out")
+    dq, dk, dv = (wu.at[2 * rows:3 * rows, i * local:(i + 1) * local] for i in range(1, 4))
+    others = wu.at[2 * rows:3 * rows, :]
+    d_heads = wu.at[3 * rows:4 * rows, 0:local]
+    loop(4, back_ffn)
+    back_act(0, 0, n_ff // 2)
+    sum_ffn.tick(9, 1)
+    back_act(0, n_ff // 2, n_ff // 2)
     back_gate(0, 0)
-    back_gate(0, 4)
-    scatter.tick(2, flat, turned, act, 2)
-    sum_back.tick(0)
-    back_act(1)
-    sum_back.tick(1)
-    scatter.tick(3, flat, turned, act, 3)
-    sum_back.tick(2)
-    back_gate(1, 0)
-    sum_back.tick(3)
-    back_gate(1, 4)
-    move("wq2", wq_out, wd.at[:, 0:local])
-    move("wk2", wk_out, wd.at[:, local:2 * local])
-    move("wv2", wv_out, wd.at[:, 2 * local:3 * local])
-    move("wo2", wo_out, wg.at[0:local, :])
-    move("x2", x_in, wu.at[0:rows, :])
-
-    def with_act(i):
-        sum_back.tick(4 + i)
-        scatter.tick(4 + i, flat, turned, act, 4 + i)
-
-    with_act(0)
-    loop(3, with_act, 1)
-    flip(h)
-    for i in range(3):
-        sum_back.tick(8 + i)
-        scatter.tick(8 + i, flat, turned, gate, i)
-    for i in range(3, 6):
-        sum_back.tick(8 + i)
-        scatter.tick(8 + i, tall, turned, gate, i)
-    sum_back.drain()
+    loop(2, sum_back.push)
+    sum_ffn.sent(1)
+    loop(4, back_ffn, 4)
+    for q in range(width // local):
+        move(f"hidden{q}", wv.at[q * rows:(q + 1) * rows, :], hidden_out.at[:, q * local:(q + 1) * local])
+    flip(d_ffn)
     d_attn = wu.at[rows:2 * rows, :]
 
     def back_attn(at):
@@ -799,13 +812,10 @@
         mean = jnp.mean(gained * raw, axis=1, keepdims=True)
         d_attn[near, :] = (inv * gained - raw * inv**3 * mean).astype(BF)
 
-    loop(8, back_attn)
-    need("wo2")
-    scatter.tick(14, tall, turned, gate, 6)
-    d_heads = wu.at[2 * rows:3 * rows, 3 * local:4 * local]
-    d_heads[...] = dot_nt(d_attn[...], wg[0:local, :]).astype(BF)
-    scatter.tick(15, tall, turned, gate, 7)
-    dq, dk, dv = (wu.at[2 * rows:3 * rows, i * local:(i + 1) * local] for i in range(3))
+    def back_out(r):
+        near = slice(r * half, (r + 1) * half)
+        loop(4, back_attn, 4 * r)
+        d_heads[near, :] = dot_nt(d_attn[near, :], wg[0:local, :]).astype(BF)
 
     def back_head(hd):
         cols = span(hd * HD, HD)
@@ -827,26 +837,27 @@
         dk[:, cols] = turn_back(dk_sum[...] * scale, cos_tab[...], sin_tab[...]).astype(BF)
         dv[:, cols] = dv_sum[...].astype(BF)
 
-    for hd in range(0, heads, 2):
-        loop(2, back_head, hd)
-        scatter.tick(16 + hd // 2, tall, turned, up, hd // 2)
     row_sum_back = SmallSum(place, sums.at[1], small.at[1])
-    sums[1, 0] = jnp.zeros(sums.shape[2:], F32)
-    for at, (grad, raw, gain, lane_of) in enumerate(((dq, qp, q_gain, heads), (dk, kp, k_gain, heads + 1))):
-        both = grad[...].astype(F32) * raw[...].astype(F32)
-        gains[2 + at:3 + at, 0:local] = jnp.sum(both * stat[:, lane_of:lane_of + 1], axis=0, keepdims=True)
-        sums[1, 0, at:at + 1, :] = as_row(jnp.sum(gain[...] * both, axis=1, keepdims=True))
-    row_sum_back.begin()
-    scatter.tick(18, tall, turned, up, 2)
-    totals = row_sum_back.end()
-    for at, (grad, raw, gain, lane_of) in enumerate(((dq, qp, q_gain, heads), (dk, kp, k_gain, heads + 1))):
-        inv = stat[:, lane_of:lane_of + 1]
-        mean = as_col(totals[at:at + 1, :]) / width
-        gained = gain[...] * grad[...].astype(F32)
-        grad[...] = (inv * gained - raw[...].astype(F32) * inv**3 * mean).astype(BF)
-    need("wq2", "wk2", "wv2", "x2")
+    normed = ((dq, qp, q_gain, heads), (dk, kp, k_gain, heads + 1))
+
+    def begin_norms():
+        sums[1, 0] = jnp.zeros(sums.shape[2:], F32)
+        for at, (grad, raw, gain, lane_of) in enumerate(normed):
+            both = grad[...].astype(F32) * raw[...].astype(F32)
+            gains[2 + at:3 + at, 0:local] = jnp.sum(both * stat[:, lane_of:lane_of + 1], axis=0, keepdims=True)
+            sums[1, 0, at:at + 1, :] = as_row(jnp.sum(gain[...] * both, axis=1, keepdims=True))
+        row_sum_back.begin()
+
+    def end_norms():
+        totals = row_sum_back.end()
+        for at, (grad, raw, gain, lane_of) in enumerate(normed):
+            inv = stat[:, lane_of:lane_of + 1]
+            mean = as_col(totals[at:at + 1, :]) / width
+            gained = gain[...] * grad[...].astype(F32)
+            grad[...] = (inv * gained - raw[...].astype(F32) * inv**3 * mean).astype(BF)
+
     raw_x = d_ffn
-    sum_in = RowSum(place, part, took, raw_x, row_sems.at[3], halves_in_turn)
+    sum_in = RowSum(place, part, took_slot, raw_x, row_sems.at[3], by_rows, 8)
 
     def back_in(r):
         near = slice(r * half, (r + 1) * half)
@@ -855,27 +866,16 @@
             spot = columns(i)
             value = dot_nt(dq[near, :], wd[spot, 0:local]) + dot_nt(dk[near, :], wd[spot, local:2 * local])
             part[near, spot] = (value + dot_nt(dv[near, :], wd[spot, 2 * local:3 * local])).astype(BF)
-            sum_in.begin(r * 8 + i)
 
         loop(8, one)
-
-    back_in(0)
-    scatter.tick(19, tall, turned, up, 3)
-    back_in(1)
-
-    def with_up(i):
-        sum_in.tick(i)
-        scatter.tick(20 + i, tall, turned, up, 4 + i)
-
-    loop(4, with_up)
-    flip(d_attn)
-    for i in range(2):
-        sum_in.tick(4 + i)
-        scatter.tick(24 + i, tall, turned, o, i)
-    flip(wu.at[0:rows, :])
-    last = [(right, at) for right in (dq, dk, dv) for at in range(local // UNIT)]
+        loop(4, sum_in.push, 4 * r)
+
+    def end_tile(at):
+        near = span(at * tile, tile)
+        dh = side[near, 1:2] * cot[near, :].astype(F32) + raw_h[near, :].astype(F32)
+        raw_x[near, :] = (dh + raw_x[near, :].astype(F32)).astype(BF)
+
     partners = (place.sib, place.xn, place.yn)
-    n_units = scatter.count
 
     def gain_copy(at):
         return remote(
@@ -883,42 +883,94 @@
             {"dp": partners[at]},
         )
 
-    def kind_of(u):
-        first_flat = 3 * n_ff
-        if u < n_ff:
-            return flat
-        if u < first_flat:
-            return tall
-        if u < first_flat + local // UNIT:
-            return (True, 2 * n_ff)
-        return (False, n_ff + local // UNIT)
-
-    gain_copy(0).start()
-    for i in range(n_units + 3 - 26):
-        u = 26 + i
-        if 6 + i < sum_in.ticks:
-            sum_in.tick(6 + i)
-        if last:
-            scatter.tick(u, kind_of(u - 3), turned, *last.pop(0))
+    def add_gains(at):
+        gain_copy(at).wait_recv()
+        gains[8 * at + 8:8 * at + 16, :] = gains[8 * at:8 * at + 8, :] + gains_got[at]
+        if at < 2:
+            gain_copy(at + 1).start()
         else:
-            scatter.tick(u, kind_of(u - 3))
-        if i < 3:
-            gain_copy(i).wait_recv()
-            gains[8 * i + 8:8 * i + 16, :] = gains[8 * i:8 * i + 8, :] + gains_got[i]
-            if i < 2:
-                gain_copy(i + 1).start()
-    move("gains", gains.at[24:32, :], gains_out)
-    for tick in range(6 + n_units + 3 - 26, sum_in.ticks):
-        sum_in.tick(tick)
-
-    def end_tile(at):
-        near = span(at * tile, tile)
-        dh = side[near, 1:2] * cot[near, :].astype(F32) + raw_h[near, :].astype(F32)
-        raw_x[near, :] = (dh + raw_x[near, :].astype(F32)).astype(BF)
-
-    sum_in.drain()
-    loop(8, end_tile)
-    move("grad_in", raw_x, grad_in_out)
+            move("gains", gains.at[24:32, :], gains_out)
+
+    def fetch():
+        move("wq2", wq_out, wd.at[:, 0:local])
+        move("wk2", wk_out, wd.at[:, local:2 * local])
+        move("wv2", wv_out, wd.at[:, 2 * local:3 * local])
+        move("wo2", wo_out, wg.at[0:local, :])
+        move("x2", x_in, wu.at[0:rows, :])
+
+    def after_tick(u):
+        if u == 0:
+            back_gate(0, 4)
+            loop(2, sum_back.push, 2)
+        elif u in (1, 2):
+            back_act(1, (u - 1) * (n_ff // 2), n_ff // 2)
+        elif u == 3:
+            back_gate(1, 0)
+            loop(2, sum_back.push, 4)
+        elif u == 4:
+            back_gate(1, 4)
+            loop(2, sum_back.push, 6)
+            fetch()
+        elif u == 13:
+            need("wo2")
+            back_out(0)
+        elif u == 18:
+            sum_back.sent()
+            back_out(1)
+            others[:, 0:local] = o[...]
+        elif u == 19:
+            loop(heads // 2, back_head)
+        elif u == 20:
+            loop(heads - heads // 2, back_head, heads // 2)
+            begin_norms()
+        elif u == 21:
+            end_norms()
+            need("wq2", "wk2", "wv2", "x2")
+            back_in(0)
+        elif u == 22:
+            sum_in.tick(1, 0)
+            back_in(1)
+            gain_copy(0).start()
+        elif u in (24, 26, 28):
+            add_gains((u - 24) // 2)
+        elif u == 32:
+            sum_in.sent()
+            loop(8, end_tile)
+            move("grad_in", raw_x, grad_in_out)
+
+    def at_tick(u, act_on):
+        @pl.when(u == act_on[0])
+        def _():
+            act_on[1]()
+
+    def step(u):
+        for when, src in ((n_ff, h), (3 * n_ff, d_attn), (3 * n_ff + n_local, wu.at[0:rows, :])):
+            at_tick(u, (when, functools.partial(flip, src)))
+        at_tick(u, (1, functools.partial(need, *(f"hidden{q}" for q in range(width // local)))))
+        scatter.tick(u, turned, ffs, others)
+
+        @pl.when((u >= 1) & (u <= 5))
+        def _():
+            sum_back.tick(u, 0)
+
+        @pl.when((u >= 6) & (u <= 13))
+        def _():
+            odd = u % 2
+            sum_back.tick((u - 4 + 9 * odd) // 2, 1 - odd)
+
+        @pl.when((u >= 14) & (u <= 18))
+        def _():
+            sum_back.tick(u - 9, 1)
+
+        @pl.when((u >= 23) & (u <= 32))
+        def _():
+            sum_in.tick(u - 21, 0)
+            sum_in.tick(u - 23, 1)
+
+        for when in (0, 1, 2, 3, 4, 13, 18, 19, 20, 21, 22, 24, 26, 28, 32):
+            at_tick(u, (when, functools.partial(after_tick, when)))
+
+    loop(scatter.count + 3, step)
     for at in range(3):
         gain_copy(at).wait_send()
     row_sum.drain()
@@ -948,12 +1000,12 @@
         + [V((rows, local), BF)] * 6
         + [V((rows, HD), F32)] * 4
         + [V((rows, width), BF)] * 2
-        + [V((rows, ff), BF)] * 3
+        + [V((3, rows, ff), BF)]
         + [V((rows, width), BF)] * 3
         + [V((2, 8, half, high), BF), V((width, rows), BF), V((rows, HD), F32), V((rows, HD), F32)]
         + [V((2, n_mp, 8, rows), F32), V((32, width), F32), V((3, 8, width), F32)]
-        + [dma((7, 10)), dma((7, 10)), dma((7,)), dma((4, 4, 2, 8)), dma((2, 2, n_mp))]
-        + [dma((2, 5, 4)), dma((2,)), dma((2, 3)), dma((16,))],
+        + [dma((7, 12)), dma((7, 12)), dma((7,)), dma((4, 4, 2, 8)), dma((2, 2, n_mp))]
+        + [dma((2, 5, 4)), dma((2,)), dma((2, 3)), dma((20,))],
         compiler_params=pltpu.CompilerParams(
             collective_id=0, has_side_effects=True, vmem_limit_bytes=67043328,
         ),

time: 431 us -> 399 us (0.926)
  Pallas kernels: 410 us -> 381 us
    pallas_call x1, Pallas kernels: 410 us -> 381 us  [layer_call(): pl.pallas_call(functools.partial(layer_kernel, n_mp), out_shape=[S(s, BF)...]
where the time goes in v4:
time: 399 us; the launch traced here: 398 us
  Pallas kernels  381 us (95%)
  other arithmetic  11.4 us (3%)
  local copies, waits for them, and re-layouts  4.33 us (1%)
    pallas_call x1, Pallas kernels, layer_call(): pl.pallas_call(functools.partial(layer_kernel, n_mp), out_shape=[S(s, BF)...  381 us

profile of v4, /device:TPU:0, one launch (start us, length us, event | category | flops | bytes accessed | tf_op | source)
XLA Modules:
  0.0 398.2 jit_solution(12787230629857614258)
XLA Ops:
  1.3 0.6 maximum_bitcast_fusion.freq
  1.9 381.2 %shard_map.246 = (bf16[2048,512]{1,0:T(8,128)(2,1)}, bf16[2048,512]{1,0:T(8,128)(2,1)}, bf16[2048,512]{1,0:T(8,128)(2,1)}, bf16[512,2048]{1,0:T(8,128)(2,1)}, bf...) custom-call(bf16[512,2048]{1,0:T(8,128)(2,1)} %x_in.1, ...), custom_call_target="tpu_custom_call" | custom-call | tf_op jit(solution)/shard_map/pallas_call | solution.py:993
  383.1 0.0 copy-start
  383.1 1.5 fusion.1
  384.6 1.5 fusion
  386.1 1.8 slice_convert_fusion.3
  387.9 2.7 slice_convert_fusion
  390.6 0.0 copy-done
  390.6 1.2 slice_convert_fusion.4
  391.8 0.0 copy-start.1
  391.8 2.6 slice_convert_fusion.1
  394.4 0.0 copy-done.1
  394.4 0.0 copy-start.2
  394.4 2.5 convert_element_type.24
  396.9 0.0 copy-done.2
  396.9 1.3 copy.30
  (1 shorter events, 0.0 us)
Async XLA Ops:
  383.1 7.5 %copy-start = (bf16[256,5632]{1,0:T(8,128)(2,1)S(1)}, bf16[256,5632]{1,0:T(8,128)(2,1)}, u32[]{:S(2)}) copy-start(bf16[256,5632]{1,0:T(8,128)(2,1)} %get-tuple-element.20) | copy-start | bytes 8650756
  391.8 2.6 copy-start.1
  394.4 2.5 copy-start.2

commit v5 on v4

--- a/solution.py
+++ b/solution.py
@@ -292,44 +292,45 @@
 
 
 class Scatter:
-    def __init__(self, place, pool, outs, sems, out_sems, n_ff, n_local):
-        self.place, self.pool, self.outs = place, pool, outs
+    slots = 6
+
+    def __init__(self, place, tall, broad, outs, sems, out_sems, n_ff, n_local):
+        self.place, self.tall, self.broad, self.outs = place, tall, broad, outs
         self.n_ff, self.n_local, self.early = n_ff, n_local, 3 * n_ff
         self.count = 3 * n_ff + 4 * n_local
         self.sems, self.out_sems = sems, out_sems
-        self.rows = pool[0].shape[0] // 8
+        self.rows = broad.shape[1] // 8
         self.half = self.rows // 2
 
-    def column(self, array, at, start, size):
-        return self.pool[array].at[span(start, size), pl.ds(at, UNIT)]
-
     def made(self, u, own):
-        return self.pool[0].at[span((u % 2) * 4 * self.rows, 4 * self.rows), span(own * UNIT, UNIT)]
+        return self.tall.at[span((u % 2) * 4 * self.rows, 4 * self.rows), span(own * UNIT, UNIT)]
 
     def got(self, u, chip=None):
         s = u % 4
-        first, size = (s % 2) * 4 * self.rows, 4 * self.rows
+        first, size = (8 + s % 2 * 4) * self.rows, 4 * self.rows
         if chip is not None:
             first, size = first + chip * self.rows, self.rows
-        return self.pool[1].at[span(first, size), span(s // 2 * UNIT, UNIT)]
+        return self.tall.at[span(first, size), span(s // 2 * UNIT, UNIT)]
 
     def sums(self, which, u, to, then=None):
-        first, size = (u % 4) * 2 * self.rows + to * self.rows, self.rows
+        first, size = (16 + u % self.slots * 2 + to) * self.rows, self.rows
         if then is not None:
             first, size = first + then * self.half, self.half
-        return self.column(2, which * UNIT, first, size)
+        return self.tall.at[span(first, size), pl.ds(which * UNIT, UNIT)]
+
+    def ended(self, which, u):
+        first = (16 + 2 * self.slots) * self.rows + u % self.slots * self.half
+        return self.tall.at[span(first, self.half), pl.ds(which * UNIT, UNIT)]
 
     def met(self, which, u):
-        return self.pool[3].at[span((u % 2) * self.rows, self.rows), span((3 + 2 * which + u % 4 // 2) * UNIT, UNIT)]
-
-    def ended(self, which, u):
-        return self.column(3, which * UNIT, (u % 4) * self.half, self.half)
+        s = u % self.slots
+        return self.broad.at[span(s % 2 * self.rows, self.rows), span((s // 2 * 2 + which) * UNIT, UNIT)]
 
     def done(self, u):
-        return self.column(3, 2 * UNIT, (u % 2) * self.rows, self.rows)
+        return self.broad.at[span((u % 2) * self.rows, self.rows), span(self.slots * UNIT, UNIT)]
 
     def send(self, kind, u):
-        p, s = self.place, u % 4
+        p, s = self.place, u % self.slots
         src, dst, target = {
             0: lambda: (self.made(u, 0), self.got(u), p.sib),
             1: lambda: (self.sums(0, u, 1 - p.x), self.met(0, u), p.xn),
@@ -394,20 +395,18 @@
             self.send(3 + which, u).wait_recv()
             parts.append(spot[...].astype(F32) + self.ended(which, u)[...].astype(F32))
         value = jnp.concatenate(parts, axis=0)
-        late = u // self.early
-        flat = (u < self.n_ff) | ((u >= self.early) & (u < self.early + self.n_local))
-
-        @pl.when(flat)
-        def _():
-            self.done(u)[...] = value.T.astype(BF)
-            target = self.outs[0].at[span((u - late * 2 * self.n_ff) * UNIT, UNIT), :]
+
+        def put(first, out, flat):
+            self.done(u)[...] = (value.T if flat else value).astype(BF)
+            near = span((u - first) * UNIT, UNIT)
+            target = out.at[near, :] if flat else out.at[:, near]
             pltpu.make_async_copy(self.done(u), target, self.out_sems.at[u % 2]).start()
 
-        @pl.when(jnp.logical_not(flat))
-        def _():
-            self.done(u)[...] = value.astype(BF)
-            target = self.outs[1].at[:, span((u - self.n_ff - late * self.n_local) * UNIT, UNIT)]
-            pltpu.make_async_copy(self.done(u), target, self.out_sems.at[u % 2]).start()
+        first = 0
+        for at, out in enumerate(self.outs):
+            count = (self.n_ff, self.n_ff, self.n_ff, self.n_local, 3 * self.n_local)[at]
+            pl.when((u >= first) & (u < first + count))(functools.partial(put, first, out, at in (0, 3)))
+            first += count
 
         for kind in (3, 4):
             self.send(kind, u).wait_send()
@@ -421,7 +420,7 @@
         def _():
             self.product(u, turned, others, u - self.early)
 
-        for lag, stage in ((1, self.across), (2, self.along), (3, self.finish)):
+        for lag, stage in ((1, self.across), (3, self.along), (5, self.finish)):
             @pl.when((u >= lag) & (u < self.count + lag))
             def _():
                 stage(u - lag)
@@ -457,14 +456,18 @@
     n_mp,
     x_in, cot_in, wq_in, wk_in, wv_in, wo_in, wg_in, wu_in, wd_in,
     seg, live, freq, q_gain, k_gain, a_gain, f_gain,
-    wq_out, wk_out, wv_out, wo_out, hidden_out, grad_in_out, flat_out, tall_out, gains_out,
-    wq, wk, wv, wo, wg, wu, wd,
-    x, qp, kp, qr, kr, v, o, stat, cos_tab, sin_tab, side, raw_a, h, ffs, d_ffn, cot, part, took,
-    turned, dk_sum, dv_sum, sums, gains, gains_got,
-    g_send, g_recv, g_local, row_sems, small, s_sems, s_out, gain_sems, io_sems,
+    wq_out, wk_out, wv_out, wo_out, hidden_out, grad_in_out, gd_out, gg_out, gu_out, go_out, gqkv_out, *rest,
 ):
+    gain_outs = rest[:4]
+    (
+        tall, wo, wg, wu, wd,
+        x, qp, kp, qr, kr, v, o, stat, cos_tab, sin_tab, side, raw_a, h, ffs, d_ffn, cot, part, took,
+        turned, dk_sum, dv_sum, sums, gains, gains_got,
+        g_send, g_recv, g_local, row_sems, small, s_sems, s_out, gain_sems, io_sems,
+    ) = rest[4:]
     place = Place(n_mp)
     rows, width = x.shape
+    wq, wk, wv = (tall.at[i * width:(i + 1) * width, :] for i in range(3))
     local, ff = qp.shape[1], ffs.shape[2]
     act, gate, up = (ffs.at[i] for i in range(3))
     heads = local // HD
@@ -759,7 +762,8 @@
 
         loop(8, one)
 
-    scatter = Scatter(place, (wq, wk, wv, wo), (flat_out, tall_out), s_sems, s_out, n_ff, n_local)
+    grads_out = (gd_out, gg_out, gu_out, go_out, gqkv_out)
+    scatter = Scatter(place, tall, wo, grads_out, s_sems, s_out, n_ff, n_local)
 
     def back_act(r, first, count):
         near = slice(r * half, (r + 1) * half)
@@ -785,6 +789,7 @@
             part[near, columns(i)] = value.astype(BF)
 
         loop(4, one, first)
+        loop(2, sum_back.push, 4 * r + first // 2)
 
     dq, dk, dv = (wu.at[2 * rows:3 * rows, i * local:(i + 1) * local] for i in range(1, 4))
     others = wu.at[2 * rows:3 * rows, :]
@@ -794,7 +799,6 @@
     sum_ffn.tick(9, 1)
     back_act(0, n_ff // 2, n_ff // 2)
     back_gate(0, 0)
-    loop(2, sum_back.push)
     sum_ffn.sent(1)
     loop(4, back_ffn, 4)
     for q in range(width // local):
@@ -873,7 +877,12 @@
     def end_tile(at):
         near = span(at * tile, tile)
         dh = side[near, 1:2] * cot[near, :].astype(F32) + raw_h[near, :].astype(F32)
-        raw_x[near, :] = (dh + raw_x[near, :].astype(F32)).astype(BF)
+        cot[near, :] = (dh + raw_x[near, :].astype(F32)).astype(BF)
+
+    def end_half(r):
+        loop(4, end_tile, 4 * r)
+        near = slice(r * half, (r + 1) * half)
+        move(f"grad_in{r}", cot.at[near, :], grad_in_out.at[near, :])
 
     partners = (place.sib, place.xn, place.yn)
 
@@ -889,7 +898,8 @@
         if at < 2:
             gain_copy(at + 1).start()
         else:
-            move("gains", gains.at[24:32, :], gains_out)
+            for i, out in enumerate(gain_outs):
+                move(f"gain{i}", gains.at[24 + i:25 + i, 0:out.shape[1]], out)
 
     def fetch():
         move("wq2", wq_out, wd.at[:, 0:local])
@@ -898,85 +908,81 @@
         move("wo2", wo_out, wg.at[0:local, :])
         move("x2", x_in, wu.at[0:rows, :])
 
-    def after_tick(u):
-        if u == 0:
+    def at_step(s):
+        if s == 0:
             back_gate(0, 4)
-            loop(2, sum_back.push, 2)
-        elif u in (1, 2):
-            back_act(1, (u - 1) * (n_ff // 2), n_ff // 2)
-        elif u == 3:
-            back_gate(1, 0)
-            loop(2, sum_back.push, 4)
-        elif u == 4:
-            back_gate(1, 4)
-            loop(2, sum_back.push, 6)
-            fetch()
-        elif u == 13:
+        elif s in (1, 2):
+            back_act(1, (s - 1) * (n_ff // 2), n_ff // 2)
+        elif s in (3, 4):
+            back_gate(1, 4 * (s - 3))
+            if s == 4:
+                fetch()
+        elif s == 12:
             need("wo2")
             back_out(0)
-        elif u == 18:
+        elif s == 13:
             sum_back.sent()
             back_out(1)
             others[:, 0:local] = o[...]
-        elif u == 19:
+        elif s == 14:
             loop(heads // 2, back_head)
-        elif u == 20:
+        elif s == 15:
             loop(heads - heads // 2, back_head, heads // 2)
             begin_norms()
-        elif u == 21:
+        elif s == 17:
             end_norms()
             need("wq2", "wk2", "wv2", "x2")
-            back_in(0)
-        elif u == 22:
-            sum_in.tick(1, 0)
-            back_in(1)
+        elif s in (18, 19):
+            back_in(s - 18)
+        elif s == 20:
             gain_copy(0).start()
-        elif u in (24, 26, 28):
-            add_gains((u - 24) // 2)
-        elif u == 32:
-            sum_in.sent()
-            loop(8, end_tile)
-            move("grad_in", raw_x, grad_in_out)
+        elif s in (22, 24, 26):
+            add_gains((s - 22) // 2)
+        elif s in (28, 29):
+            end_half(s - 28)
 
     def at_tick(u, act_on):
         @pl.when(u == act_on[0])
         def _():
             act_on[1]()
 
-    def step(u):
+    doubles = (4, 7, 21, 22, 25, 26)
+
+    def one_tick(u):
         for when, src in ((n_ff, h), (3 * n_ff, d_attn), (3 * n_ff + n_local, wu.at[0:rows, :])):
             at_tick(u, (when, functools.partial(flip, src)))
         at_tick(u, (1, functools.partial(need, *(f"hidden{q}" for q in range(width // local)))))
         scatter.tick(u, turned, ffs, others)
 
-        @pl.when((u >= 1) & (u <= 5))
+    def step(s):
+        before = sum((s > at).astype(jnp.int32) for at in doubles)
+        here = sum((s == at).astype(jnp.int32) for at in doubles)
+        loop(1 + here, one_tick, s + before)
+
+        at_tick(s, (19, functools.partial(at_step, 19)))
+
+        for row_sum_, half_, t, first, last in (
+            (sum_back, 0, s, 1, 5), (sum_back, 1, s - 3, 4, 12), (sum_in, 0, s - 18, 19, 27), (sum_in, 1, s - 20, 21, 29),
+        ):
+            @pl.when((s >= first) & (s <= last))
+            def _():
+                row_sum_.tick(t, half_)
+
+        @pl.when((s >= 6) & (s <= 12) & (s % 2 == 0))
         def _():
-            sum_back.tick(u, 0)
-
-        @pl.when((u >= 6) & (u <= 13))
-        def _():
-            odd = u % 2
-            sum_back.tick((u - 4 + 9 * odd) // 2, 1 - odd)
-
-        @pl.when((u >= 14) & (u <= 18))
-        def _():
-            sum_back.tick(u - 9, 1)
-
-        @pl.when((u >= 23) & (u <= 32))
-        def _():
-            sum_in.tick(u - 21, 0)
-            sum_in.tick(u - 23, 1)
-
-        for when in (0, 1, 2, 3, 4, 13, 18, 19, 20, 21, 22, 24, 26, 28, 32):
-            at_tick(u, (when, functools.partial(after_tick, when)))
-
-    loop(scatter.count + 3, step)
+            sum_back.tick((s + 6) // 2, 0)
+
+        for when in (0, 1, 2, 3, 4, 12, 13, 14, 15, 17, 18, 20, 22, 24, 26, 28, 29):
+            at_tick(s, (when, functools.partial(at_step, when)))
+
+    loop(scatter.count + 5 - len(doubles), step)
     for at in range(3):
         gain_copy(at).wait_send()
+    sum_in.sent()
     row_sum.drain()
     row_sum_back.drain()
     scatter.drain()
-    need("gains", "grad_in")
+    need("gain0", "gain1", "gain2", "gain3", "grad_in0", "grad_in1")
 
 
 def layer_call(n_mp, x, cot, weights, seg, live, freq, q_gain, k_gain, a_gain, f_gain):
@@ -988,14 +994,15 @@
     S, V, dma = jax.ShapeDtypeStruct, pltpu.VMEM, pltpu.SemaphoreType.DMA
     fulls = [(width, local)] * 3 + [(local, width)] + [(width, ff)] * 2 + [(ff, width)]
     outs = fulls[:4] + [
-        (rows, width), (rows, width), (ff + local, high), (high, 2 * ff + 3 * local),
+        (rows, width), (rows, width), (ff, high), (high, ff), (high, ff), (local, high), (high, 3 * local),
     ]
     return pl.pallas_call(
         functools.partial(layer_kernel, n_mp),
-        out_shape=[S(s, BF) for s in outs] + [S((8, width), F32)],
+        out_shape=[S(s, BF) for s in outs] + [S((1, n), F32) for n in (width, width, local, local)],
         in_specs=[any_spec] * 9 + [vmem] * 7,
-        out_specs=[any_spec] * 9,
-        scratch_shapes=[V(s, BF) for s in fulls]
+        out_specs=[any_spec] * 15,
+        scratch_shapes=[V(((16 + 5 * Scatter.slots // 2) * high, local), BF)]
+        + [V(s, BF) for s in fulls[3:]]
         + [V((rows, width), BF)]
         + [V((rows, local), BF)] * 6
         + [V((rows, HD), F32)] * 4
@@ -1005,7 +1012,7 @@
         + [V((2, 8, half, high), BF), V((width, rows), BF), V((rows, HD), F32), V((rows, HD), F32)]
         + [V((2, n_mp, 8, rows), F32), V((32, width), F32), V((3, 8, width), F32)]
         + [dma((7, 12)), dma((7, 12)), dma((7,)), dma((4, 4, 2, 8)), dma((2, 2, n_mp))]
-        + [dma((2, 5, 4)), dma((2,)), dma((2, 3)), dma((20,))],
+        + [dma((2, 5, Scatter.slots)), dma((2,)), dma((2, 3)), dma((24,))],
         compiler_params=pltpu.CompilerParams(
             collective_id=0, has_side_effects=True, vmem_limit_bytes=67043328,
         ),
@@ -1014,31 +1021,28 @@
 
 def with_kernel(n_mp, hidden_in, cotangent, segments, live_counts, *rest):
     weights, (query_gain, key_gain, attn_gain, ffn_gain) = rest[:7], rest[7:]
-    local, ff = weights[0].shape[1], weights[4].shape[1]
+    local = weights[0].shape[1]
     inv_freq = THETA ** (-(jnp.arange(HD // 2, dtype=F32) * (2.0 / HD)))
     freq = jnp.concatenate([inv_freq, inv_freq])[None]
-    _, _, _, _, hidden_out, grad_in, flat, tall, gains = layer_call(
+    hidden_out, grad_in, g_down, g_gate, g_up, g_output, g_qkv, d_f, d_a, d_q, d_k = layer_call(
         n_mp, hidden_in, cotangent, weights, segments, live_counts[None], freq,
         query_gain[None], key_gain[None], attn_gain[None], ffn_gain[None],
-    )
-
-    def piece(first, count):
-        return tall[:, first:first + count].astype(F32)
+    )[4:]
 
     return (
         hidden_out,
         grad_in.astype(F32),
-        piece(2 * ff, local),
-        piece(2 * ff + local, local),
-        piece(2 * ff + 2 * local, local),
-        flat[ff:].astype(F32),
-        piece(0, ff),
-        piece(ff, ff),
-        flat[:ff].astype(F32),
-        gains[2, :local],
-        gains[3, :local],
-        gains[1],
-        gains[0],
+        g_qkv[:, :local].astype(F32),
+        g_qkv[:, local:2 * local].astype(F32),
+        g_qkv[:, 2 * local:].astype(F32),
+        g_output.astype(F32),
+        g_gate.astype(F32),
+        g_up.astype(F32),
+        g_down.astype(F32),
+        d_q[0],
+        d_k[0],
+        d_a[0],
+        d_f[0],
     )
 
 

time: 399 us -> 385 us (0.965)
  Pallas kernels: 381 us -> 367 us
    pallas_call x1, Pallas kernels: 381 us -> 367 us  [layer_call(): pl.pallas_call(functools.partial(layer_kernel, n_mp), out_shape=[S(s, BF)...]
    convert_element_type x4 -> x5, other arithmetic: 8.23 us -> 8.77 us  [the longest x1 2.31 us: with_kernel(): g_qkv[:, 2 * local:].astype(F32)]
where the time goes in v5:
time: 385 us
  Pallas kernels  367 us (95%)
  other arithmetic  11.9 us (3%)
  local copies, waits for them, and re-layouts  4.58 us (1%)
    pallas_call x1, Pallas kernels, layer_call(): pl.pallas_call(functools.partial(layer_kernel, n_mp), out_shape=[S(s, BF)...  367 us

profile of v5, /device:TPU:0, one launch (start us, length us, event | category | flops | bytes accessed | tf_op | source)
XLA Modules:
  0.0 384.7 jit_solution(3349165174149255426)
XLA Ops:
  1.3 0.6 maximum_bitcast_fusion.freq
  1.9 366.9 %shard_map.246 = (bf16[2048,512]{1,0:T(8,128)(2,1)}, bf16[2048,512]{1,0:T(8,128)(2,1)}, bf16[2048,512]{1,0:T(8,128)(2,1)}, bf16[512,2048]{1,0:T(8,128)(2,1)}, bf...) custom-call(bf16[512,2048]{1,0:T(8,128)(2,1)} %x_in.1, ...), custom_call_target="tpu_custom_call" | custom-call | tf_op jit(solution)/shard_map/pallas_call | solution.py:999
  368.8 0.0 copy-start.4
  368.8 1.9 convert_element_type.28
  370.7 2.3 slice_convert_fusion
  373.0 0.0 copy-start.3
  373.0 0.0 copy-done.4
  373.0 1.6 convert_element_type.29
  374.6 0.0 copy-done.3
  374.6 0.0 copy-start.2
  374.6 1.6 convert_element_type.30
  376.1 0.0 copy-done.2
  376.1 0.0 copy-start
  376.1 1.5 convert_element_type.31
  377.6 0.9 copy-done
  378.5 0.0 copy-start.1
  378.5 2.5 convert_element_type.24
  381.0 0.0 copy-done.1
  381.0 0.0 copy-start.8
  381.0 0.0 copy-start.7
  381.0 0.0 copy-start.6
  381.0 0.0 copy-start.5
  381.0 1.3 copy.34
  382.4 0.0 copy-done.8
  382.4 0.6 copy.35
  383.0 0.0 copy-done.7
  383.0 0.6 copy.36
  383.5 0.0 copy-done.6
  383.5 0.6 copy.37
  384.1 0.0 copy-done.5
  384.1 0.6 copy.38
  (1 shorter events, 0.0 us)
Async XLA Ops:
  368.8 4.2 %copy-start.4 = (bf16[256,2048]{1,0:T(8,128)(2,1)S(1)}, bf16[256,2048]{1,0:T(8,128)(2,1)}, u32[]{:S(2)}) copy-start(bf16[256,2048]{1,0:T(8,128)(2,1)} %get-tuple-element.28) | copy-start | bytes 3145732
  373.0 1.6 copy-start.3
  374.6 1.6 copy-start.2
  376.1 2.3 copy-start
  378.5 2.5 copy-start.1
  381.0 1.3 copy-start.8
  381.0 1.9 copy-start.7
  381.0 2.5 copy-start.6
  381.0 3.1 copy-start.5

commit v6 on v5

--- a/solution.py
+++ b/solution.py
@@ -946,7 +946,7 @@
         def _():
             act_on[1]()
 
-    doubles = (4, 7, 21, 22, 25, 26)
+    doubles = (4, 7, 20, 22, 23, 25)
 
     def one_tick(u):
         for when, src in ((n_ff, h), (3 * n_ff, d_attn), (3 * n_ff + n_local, wu.at[0:rows, :])):

time: 385 us -> 384 us (level)
  no operation moved by 1% of the time
where the time goes in v6:
time: 384 us
  Pallas kernels  366 us (95%)
  other arithmetic  11.9 us (3%)
  local copies, waits for them, and re-layouts  4.58 us (1%)
    pallas_call x1, Pallas kernels, layer_call(): pl.pallas_call(functools.partial(layer_kernel, n_mp), out_shape=[S(s, BF)...  366 us

profile of v6, /device:TPU:0, one launch (start us, length us, event | category | flops | bytes accessed | tf_op | source)
XLA Modules:
  0.0 384.1 jit_solution(4757780474471121284)
XLA Ops:
  1.3 0.6 maximum_bitcast_fusion.freq
  1.9 366.2 %shard_map.246 = (bf16[2048,512]{1,0:T(8,128)(2,1)}, bf16[2048,512]{1,0:T(8,128)(2,1)}, bf16[2048,512]{1,0:T(8,128)(2,1)}, bf16[512,2048]{1,0:T(8,128)(2,1)}, bf...) custom-call(bf16[512,2048]{1,0:T(8,128)(2,1)} %x_in.1, ...), custom_call_target="tpu_custom_call" | custom-call | tf_op jit(solution)/shard_map/pallas_call | solution.py:999
  368.1 0.0 copy-start.4
  368.1 1.9 convert_element_type.28
  370.0 2.3 slice_convert_fusion
  372.3 0.0 copy-start.3
  372.3 0.0 copy-done.4
  372.3 1.6 convert_element_type.29
  373.9 0.0 copy-done.3
  373.9 0.0 copy-start.2
  373.9 1.6 convert_element_type.30
  375.5 0.0 copy-done.2
  375.5 0.0 copy-start
  375.5 1.5 convert_element_type.31
  376.9 0.9 copy-done
  377.8 0.0 copy-start.1
  377.8 2.5 convert_element_type.24
  380.3 0.0 copy-done.1
  380.3 0.0 copy-start.8
  380.3 0.0 copy-start.7
  380.4 0.0 copy-start.6
  380.4 0.0 copy-start.5
  380.4 1.3 copy.34
  381.7 0.0 copy-done.8
  381.7 0.6 copy.35
  382.3 0.0 copy-done.7
  382.3 0.6 copy.36
  382.9 0.0 copy-done.6
  382.9 0.6 copy.37
  383.5 0.0 copy-done.5
  383.5 0.6 copy.38
  (1 shorter events, 0.0 us)
Async XLA Ops:
  368.1 4.2 %copy-start.4 = (bf16[256,2048]{1,0:T(8,128)(2,1)S(1)}, bf16[256,2048]{1,0:T(8,128)(2,1)}, u32[]{:S(2)}) copy-start(bf16[256,2048]{1,0:T(8,128)(2,1)} %get-tuple-element.28) | copy-start | bytes 3145732
  372.3 1.6 copy-start.3
  373.9 1.6 copy-start.2
  375.5 2.3 copy-start
  377.8 2.5 copy-start.1
  380.3 1.3 copy-start.8
  380.3 1.9 copy-start.7
  380.4 2.5 copy-start.6
  380.4 3.1 copy-start.5
